TPU v7x, 32 devices: a whole 2x2x4 slice. The times are simulated.
32 devices in a mesh: au: 2 (over y), ia: 16 (over z, x, core).
Axes of the slice: x: 2, y: 2, z: 4, core: 2. Of those that a mesh axis runs over, the one named last changes fastest.
Arguments:
- user_factors: bfloat16 [1024, 256], P(('au', 'ia')), may hold values from -6 to 6
- item_factors: bfloat16 [16384, 256], P(('ia', 'au')), may hold values from -6 to 6
- user_tangent: bfloat16 [1024, 256], P(('au', 'ia')), may hold values from -6 to 6
- item_tangent: bfloat16 [16384, 256], P(('ia', 'au')), may hold values from -6 to 6
- block_mask: int32 [8, 128], P('au', 'ia'), may hold values from 0 to 1, as said below
Outputs:
- user_product: float32 [1024, 256], P(('au', 'ia'))
- item_product: float32 [16384, 256], P(('ia', 'au'))
Inputs may be any that keep to these rules, and one draw needn't show every extreme that they name: `block_mask`: users are grouped in runs of 32 * 16 and items in runs of 512 * 2; where one user group meets one item group, at most 16 of its 4 x 8 blocks are observed, and in every draw one such meeting has exactly 16.
All inputs are finite; a program needn't handle non-finite values.
Results may differ from a plain program's by a relative error of at most 0.0013.
Values may be sent and summed in bfloat16 or wider, within the bound.
No kernel may reach another device: no remote copies, remote signals or barrier semaphores. Data moves between devices by JAX's collectives and lax.ppermute only.
A program may use at most 64 MiB of HBM per device.

v0:
```python
import jax
import jax.numpy as jnp
from jax import lax
from jax.sharding import PartitionSpec as P

batch_blocks = 16


def region_pass(users, user_tan, items, item_tan, mask_part):
    row_blocks, col_blocks = mask_part.shape
    block_rows = users.shape[0] // row_blocks
    width = users.shape[1]
    user_tiles = users.reshape(row_blocks, block_rows, width)
    utan_tiles = user_tan.reshape(row_blocks, block_rows, width)
    item_tiles = items.reshape(col_blocks, block_rows, width)
    itan_tiles = item_tan.reshape(col_blocks, block_rows, width)
    total = row_blocks * col_blocks
    flat = mask_part.reshape(-1)
    index = jnp.arange(total, dtype=jnp.int32)
    order = jnp.argsort((1 - flat) * total + index)
    live = flat[order].astype(jnp.float32)
    order = jnp.concatenate([order, jnp.zeros((batch_blocks,), jnp.int32)])
    live = jnp.concatenate([live, jnp.zeros((batch_blocks,), jnp.float32)])
    row_ids = order // col_blocks
    col_ids = order % col_blocks
    scaling = 1.0 / jnp.sqrt(jnp.float32(width))
    observed_count = jnp.sum(flat)
    turns = (observed_count + batch_blocks - 1) // batch_blocks

    def one_turn(turn, carry):
        acc_user, acc_item = carry
        first = (turn * batch_blocks).astype(jnp.int32)
        rsel = lax.dynamic_slice_in_dim(row_ids, first, batch_blocks)
        csel = lax.dynamic_slice_in_dim(col_ids, first, batch_blocks)
        lsel = lax.dynamic_slice_in_dim(live, first, batch_blocks)
        urow = user_tiles[rsel]
        durow = utan_tiles[rsel]
        vrow = item_tiles[csel]
        dvrow = itan_tiles[csel]
        score = jnp.einsum("gar,gbr->gab", urow, vrow, preferred_element_type=jnp.float32) * scaling
        prob = jax.nn.sigmoid(score)
        weight = prob * (1.0 - prob)
        tang = (
            jnp.einsum("gar,gbr->gab", durow, vrow, preferred_element_type=jnp.float32)
            + jnp.einsum("gar,gbr->gab", urow, dvrow, preferred_element_type=jnp.float32)
        ) * scaling
        curv = (lsel[:, None, None] * weight * tang).astype(jnp.bfloat16)
        to_user = jnp.einsum("gab,gbr->gar", curv, vrow, preferred_element_type=jnp.float32)
        to_item = jnp.einsum("gab,gar->gbr", curv, urow, preferred_element_type=jnp.float32)
        onehot_rows = (rsel[:, None] == jnp.arange(row_blocks, dtype=jnp.int32)[None, :]).astype(
            jnp.float32
        )
        onehot_cols = (csel[:, None] == jnp.arange(col_blocks, dtype=jnp.int32)[None, :]).astype(
            jnp.float32
        )
        acc_user = acc_user + jnp.einsum(
            "gk,gar->kar", onehot_rows, to_user, precision=lax.Precision.HIGHEST
        )
        acc_item = acc_item + jnp.einsum(
            "gk,gbr->kbr", onehot_cols, to_item, precision=lax.Precision.HIGHEST
        )
        return (acc_user, acc_item)

    start = (
        jnp.zeros((row_blocks, block_rows, width), jnp.float32),
        jnp.zeros((col_blocks, block_rows, width), jnp.float32),
    )
    acc_user, acc_item = lax.fori_loop(0, turns, one_turn, start)
    return ((acc_user * scaling).reshape(-1, width), (acc_item * scaling).reshape(-1, width))


def on_device(user_factors, item_factors, user_tangent, item_tangent, block_mask):
    users, user_tan = (
        lax.all_gather(user_factors, "ia", axis=0, tiled=True),
        lax.all_gather(user_tangent, "ia", axis=0, tiled=True),
    )
    item_product = None
    items, item_tan = (
        lax.all_gather(item_factors, "au", axis=0, tiled=True),
        lax.all_gather(item_tangent, "au", axis=0, tiled=True),
    )
    part_user, part_item = region_pass(users, user_tan, items, item_tan, block_mask)
    item_product = lax.psum_scatter(part_item, "au", scatter_dimension=0, tiled=True)
    user_product = lax.psum_scatter(part_user, "ia", scatter_dimension=0, tiled=True)
    return (user_product, item_product)


def solution(mesh):
    placed = (
        P(("au", "ia"), None),
        P(("ia", "au"), None),
        P(("au", "ia"), None),
        P(("ia", "au"), None),
        P("au", "ia"),
    )
    return jax.shard_map(
        on_device,
        mesh=mesh,
        in_specs=placed,
        out_specs=(P(("au", "ia"), None), P(("ia", "au"), None)),
        check_vma=False,
    )
```

profile of v0, /device:TPU:0, one launch (start us, length us, event | category | flops | bytes accessed | tf_op | source)
XLA Modules:
  0.0 176.4 jit_solution(17195065351704161131)
XLA Ops:
  7.2 0.0 copy-start.6
  7.2 0.0 reduce-scatter.3.cloned.1.call-start
  7.2 1.4 reduce_sum.9
  9.2 0.8 reshape.28
  10.0 1.6 sort.17
  11.7 0.7 gather_fusion.4
  12.4 24.1 %all_gather.12 = bf16[512,256]{1,0:T(8,128)(2,1)S(1)} all-gather(bf16[32,256]{1,0:T(8,128)(2,1)} %param.7), channel_id=1, replica_groups=mesh['au'=2,'ia'=16] {'ia'}, dimensions={0}, use_global_device_ids=true | all-gather | bytes 278528 | tf_op jit(solution)/shard_map/all_gather | solution.py:74
  36.4 18.4 %all_gather.14 = bf16[512,256]{1,0:T(8,128)(2,1)S(1)} all-gather(bf16[32,256]{1,0:T(8,128)(2,1)} %param.9), channel_id=1, replica_groups=mesh['au'=2,'ia'=16] {'ia'}, dimensions={0}, use_global_device_ids=true | all-gather | bytes 278528 | tf_op jit(solution)/shard_map/all_gather | solution.py:75
  54.8 9.4 %all_gather.13 = bf16[1024,256]{1,0:T(8,128)(2,1)S(1)} all-gather(bf16[512,256]{1,0:T(8,128)(2,1)} %param.8), channel_id=1, replica_groups=mesh['au'=2,'ia'=16] {'au'}, dimensions={0}, use_global_device_ids=true | all-gather | bytes 786432 | tf_op jit(solution)/shard_map/all_gather | solution.py:79
  64.2 0.0 copy-done.6
  64.2 8.3 %all_gather.15 = bf16[1024,256]{1,0:T(8,128)(2,1)S(1)} all-gather(bf16[512,256]{1,0:T(8,128)(2,1)S(1)} %copy-done.6), channel_id=1, replica_groups=mesh['au'=2,'ia'=16] {'au'}, dimensions={0}, use_global_device_ids=true | all-gather | bytes 786432 | tf_op jit(solution)/shard_map/all_gather | solution.py:80
  72.6 0.9 broadcast_in_dim.10
  73.4 1.1 broadcast_in_dim.11
  74.5 15.8 %while.12 = (s32[]{:T(128)}, f32[4,128,256]{2,0,1:T(4,128)}, f32[8,128,256]{2,0,1:T(8,128)}, s32[]{:T(128)}, s32[48]{0:T(128)S(1)}, /*index=5*/f32[48]{0:T(128)S...) while((s32[]{:T(128)}, f32[4,128,256]{2,0,1:T(4,128)}, ...), condition=%wide.region_3.4_spmd, body=%wide.region_2.3_spmd.sunk | while | flops 749865280 | bytes 50865548 | solution.py:68
  74.5 0.0 copy-start.1
  74.5 0.1 dynamic_slice.14
  74.6 0.1 compare_select_fusion.8
  74.7 0.6 gather_fusion.1
  75.3 0.0 copy-done.1
  75.4 1.6 gather_fusion.3
  77.0 0.6 gather_fusion
  77.6 1.6 gather_fusion.2
  79.2 1.7 fusion.73
  80.8 0.0 copy-start
  80.8 0.5 fusion.72
  81.4 0.7 copy-done
  82.1 0.4 fusion.74
  82.5 0.0 copy-start.3
  82.5 0.5 fusion.77
  83.0 0.7 copy-done.3
  83.7 2.3 %fusion.78 = f32[8,128,256]{2,0,1:T(8,128)S(1)} fusion(f32[8,128,256]{2,0,1:T(8,128)S(1)} %copy-done.3, f32[16,128,256]{2,1,0:T(8,128)S(1)} %fusion.77, s32[16]{0:T(128)S(1)} %get-tuple-element.170), kind=kOutput, calls=%fused_computation.10.clone.1 | convolution fusion | flops 50593920 | bytes 4194368 | tf_op jit(solution)/shard_map/while/body/gk,gbr->kbr/dot_general | solution.py:59
  86.0 0.0 copy-start.4
  86.1 0.4 fusion.75
  86.5 0.0 copy-start.2
  86.5 3.9 %fusion.76 = f32[4,128,256]{2,0,1:T(4,128)} fusion(f32[4,128,256]{2,0,1:T(4,128)} %get-tuple-element.187, f32[16,128,256]{2,1,0:T(8,128)S(1)} %fusion.75, s32[16]{0:T(128)S(1)} %get-tuple-element.169), kind=kOutput, calls=%fused_computation.21.clone.1 | convolution fusion | flops 25296960 | bytes 3145792 | tf_op jit(solution)/shard_map/while/body/gk,gar->kar/dot_general | solution.py:56
  90.4 0.0 copy-done.4
  90.4 0.0 copy-done.2
  90.4 0.0 copy-start.5
  90.4 1.2 broadcast_multiply_fusion.1
  91.6 0.9 copy.9
  92.5 0.0 reduce-scatter.3.cloned.1.call-update
  92.6 0.0 reduce-scatter.5.cloned.1.call-start
  92.6 0.0 copy-done.5
  92.6 0.1 broadcast_multiply_fusion
  92.7 1.3 copy.10
  94.0 0.0 reduce-scatter.5.cloned.1.call-update
  94.0 53.2 %reduce-scatter.3.cloned.1.call-done = f32[32,256]{1,0:T(8,128)} async-done(((f32[512,256]{1,0:T(8,128)}), f32[32,256]{1,0:T(8,128)}) %reduce-scatter.3.cloned.1.call-update) | async-done | bytes 32784 | tf_op jit(solution)/shard_map/reduce_scatter | solution.py:84
  147.2 22.3 %reduce-scatter.5.cloned.1.call-done = f32[512,256]{1,0:T(8,128)} async-done(((f32[1024,256]{1,0:T(8,128)}), f32[512,256]{1,0:T(8,128)}) %reduce-scatter.5.cloned.1.call-update) | async-done | bytes 524304 | tf_op jit(solution)/shard_map/reduce_scatter | solution.py:83
  (10 shorter events, 0.1 us)
Async XLA Ops:
  7.2 57.1 %copy-start.6 = (bf16[512,256]{1,0:T(8,128)(2,1)S(1)}, bf16[512,256]{1,0:T(8,128)(2,1)}, u32[]{:S(2)}) copy-start(bf16[512,256]{1,0:T(8,128)(2,1)} %param.10) | copy-start | bytes 786436
  7.2 140.1 %reduce-scatter.3.cloned.1.call-start = ((), (), s32[]{:S(2)}) async-start(), calls=%async_computation.2 | async-start | bytes 557056 | tf_op jit(solution)/shard_map/reduce_scatter | solution.py:84
  74.5 0.8 copy-start.1
  80.8 1.2 copy-start
  82.5 1.2 copy-start.3
  86.0 4.3 %copy-start.4 = (f32[8,128,256]{2,0,1:T(8,128)}, f32[8,128,256]{2,0,1:T(8,128)S(1)}, u32[]{:S(2)}) copy-start(f32[8,128,256]{2,0,1:T(8,128)S(1)} %fusion.78) | copy-start | bytes 3145732 | tf_op jit(solution)/shard_map/while
  86.5 3.9 %copy-start.2 = (bf16[8,128,256]{2,1,0:T(8,128)(2,1)S(1)}, bf16[8,128,256]{2,1,0:T(8,128)(2,1)}, u32[]{:S(2)}) copy-start(bf16[8,128,256]{2,1,0:T(8,128)(2,1)} %copy-done.1) | copy-start | bytes 1572868 | tf_op jit(solution)/shard_map/while
  90.4 2.2 %copy-start.5 = (f32[8,128,256]{2,0,1:T(8,128)S(1)}, f32[8,128,256]{2,0,1:T(8,128)}, u32[]{:S(2)}) copy-start(f32[8,128,256]{2,0,1:T(8,128)} %get-tuple-element.64) | copy-start | bytes 3145732
  92.6 77.0 %reduce-scatter.5.cloned.1.call-start = ((), (), s32[]{:S(2)}) async-start(), calls=%async_computation.3 | async-start | bytes 1572864 | tf_op jit(solution)/shard_map/reduce_scatter | solution.py:83
Sparse Core Ops, SparseCore 0:
  92.7 54.5 reduce-scatter.2
  150.1 19.4 reduce-scatter.4
where the time goes:
time: 177 us; the launch traced here: 176 us
  waiting for transfers between devices  75.5 us (43%)
  blocking collectives  60.2 us (34%)
  between operations  14.8 us (8%)
  local copies, waits for them, and re-layouts  11.6 us (7%)
  matrix products  9.7 us (5%)
  other arithmetic  4.41 us (2%)
    reduce_scatter x1, waiting for transfers between devices, on_device(): lax.psum_scatter(part_user, 'ia', scatter_dimension=0, tiled=True)  53.2 us
    all_gather x1, blocking collectives, on_device(): lax.all_gather(user_factors, 'ia', axis=0, tiled=True)  24.1 us
    reduce_scatter x1, waiting for transfers between devices, on_device(): lax.psum_scatter(part_item, 'au', scatter_dimension=0, tiled=True)  22.3 us
    all_gather x1, blocking collectives, on_device(): lax.all_gather(user_tangent, 'ia', axis=0, tiled=True)  18.4 us
    all_gather x1, blocking collectives, on_device(): lax.all_gather(item_factors, 'au', axis=0, tiled=True)  9.42 us
    all_gather x1, blocking collectives, on_device(): lax.all_gather(item_tangent, 'au', axis=0, tiled=True)  8.35 us
    dot_general x1, matrix products, one_turn(): jnp.einsum('gk,gar->kar', onehot_rows, to_user, precision=lax.Precision.H...  3.88 us
  transfers between devices with their start and end apart: 2, of which 2 were waited for; matrix products, arithmetic and copies ran while one was open for 1% of the time, Pallas kernels for 0%

commit v1 on v0

v1 whole, which is shorter than its diff:
```python
import functools
import math

import jax
import jax.numpy as jnp
from jax import lax
from jax.experimental import pallas as pl
from jax.experimental.pallas import tpu as pltpu
from jax.sharding import PartitionSpec as P

f32 = jnp.float32
bf16 = jnp.bfloat16
NN = (((1,), (0,)), ((), ()))
NT = (((1,), (1,)), ((), ()))
TN = (((0,), (0,)), ((), ()))
dot = functools.partial(lax.dot_general, preferred_element_type=f32)


def swap(x, axis, size, bit):
    return lax.ppermute(x, axis, [(i, i ^ bit) for i in range(size)])


def bits_of(low, high):
    out = []
    bit = high // 2
    while bit >= low:
        out.append(bit)
        bit //= 2
    return out


def relative(bits):
    order = [0]
    for bit in bits:
        order = order + [r ^ bit for r in order]
    return order


def gather_pieces(own, axis, size, bits):
    pieces = [own[None]]
    for bit in bits:
        held = pieces[0] if len(pieces) == 1 else jnp.concatenate(pieces, 0)
        pieces.append(swap(held, axis, size, bit))
    return pieces


def region_kernel(*refs, n_groups, n_items, rel_rows, rel_items, scale):
    mask = refs[0]
    users = refs[1 : 1 + n_groups]
    at = 1 + n_groups
    items = refs[at : at + n_items]
    at += n_items
    tans = refs[at : at + n_items]
    at += n_items
    keep, send = refs[at : at + 2]
    at += 2
    outs = refs[at : at + n_items]
    at += n_items
    u_all, c_all = refs[at : at + 2]

    n_rb, _, us, width = users[0].shape[1:]
    members = 2 * send.shape[0]
    block = members * us
    me_rb = lax.axis_index("ia") // members
    me_au = lax.axis_index("au")
    m = 0
    for ref in users:
        for k in range(ref.shape[0]):
            u_all[:, :, pl.ds(m * us, us), :] = ref[k]
            m += 1
    it_dev = items[0].shape[1]
    cpd = it_dev // block
    pair = 2
    first = True
    for rp in range(n_rb // pair):
        fac = u_all[pl.ds(pair * rp, pair), 0].reshape(pair * block, width)
        tan = u_all[pl.ds(pair * rp, pair), 1].reshape(pair * block, width)
        total = None
        q = 0
        for g in range(n_items):
            for k in range(items[g].shape[0]):
                for ib in range(cpd // pair):
                    rows = pl.ds(ib * pair * block, pair * block)
                    v = items[g][k, rows, :]
                    dv = tans[g][k, rows, :]
                    s = dot(v, fac, NT)
                    t = dot(v, tan, NT) + dot(dv, fac, NT)
                    seen = jnp.concatenate(
                        [
                            jnp.concatenate(
                                [
                                    jnp.full(
                                        (block, block),
                                        mask[me_rb ^ rel_rows[pair * rp + j], (me_au ^ rel_items[q]) * cpd + pair * ib + i].astype(f32)
                                        * scale,
                                        f32,
                                    )
                                    for j in range(pair)
                                ],
                                1,
                            )
                            for i in range(pair)
                        ],
                        0,
                    )
                    e = jnp.exp(jnp.abs(s) * -scale)
                    p = 1.0 / (1.0 + e)
                    c = (e * p * p * (t * seen)).astype(bf16)
                    c_all[rows, :] = c
                    r = dot(c, fac, NN) * scale
                    if rp == 0:
                        outs[g][k, rows, :] = r
                    else:
                        outs[g][k, rows, :] += r
                part = dot(c_all[...], items[g][k], TN)
                total = part if total is None else total + part
                q += 1
        total = (total * scale).reshape(pair, members, us, width)
        half = members // 2
        for j in range(pair):
            for x in range(half):
                keep[x, pair * rp + j] = total[j, x]
                send[x, pair * rp + j] = total[j, half + x]


def on_device(user_factors, item_factors, user_tangent, item_tangent, block_mask, n_au, n_ia):
    us, width = user_factors.shape
    it = item_factors.shape[0]
    row_blocks, col_blocks = block_mask.shape
    block = us * n_ia // row_blocks
    members = block // us
    scale = 1.0 / math.sqrt(width)

    item_bits = bits_of(1, n_au)
    vs = gather_pieces(item_factors, "au", n_au, item_bits)
    dvs = gather_pieces(item_tangent, "au", n_au, item_bits)

    users = jnp.stack([user_factors, user_tangent])[None]
    row_bits = bits_of(members, n_ia)
    for bit in row_bits:
        users = jnp.concatenate([users, swap(users, "ia", n_ia, bit)], 0)
    pieces = gather_pieces(users, "ia", n_ia, bits_of(1, members))

    vm = pl.BlockSpec(memory_space=pltpu.VMEM)
    outs = pl.pallas_call(
        functools.partial(
            region_kernel,
            n_groups=len(pieces),
            n_items=len(vs),
            rel_rows=[r // members for r in relative(row_bits)],
            rel_items=relative(item_bits),
            scale=scale,
        ),
        in_specs=[pl.BlockSpec(memory_space=pltpu.SMEM)] + [vm] * (len(pieces) + 2 * len(vs)),
        out_specs=[vm] * (2 + len(vs)),
        out_shape=[
            jax.ShapeDtypeStruct((members // 2, row_blocks, us, width), f32),
            jax.ShapeDtypeStruct((members // 2, row_blocks, us, width), f32),
        ]
        + [jax.ShapeDtypeStruct(v.shape, f32) for v in vs],
        scratch_shapes=[
            pltpu.VMEM((row_blocks, 2, block, width), bf16),
            pltpu.VMEM((it, 2 * block), bf16),
        ],
        name="region",
    )(block_mask, *pieces, *vs, *dvs)
    keep, send = outs[:2]
    parts = outs[2:]

    item_bits = item_bits[::-1]
    held = list(parts)
    for bit in item_bits:
        back = swap(held.pop(), "au", n_au, bit)
        sizes = [h.shape[0] for h in held]
        cuts = [sum(sizes[:i]) for i in range(len(sizes))]
        held = [h + back[c : c + n] for h, c, n in zip(held, cuts, sizes)]
    item_product = held[0][0]

    bits = bits_of(1, n_ia)[::-1]
    acc = keep + swap(send, "ia", n_ia, bits[0])
    for bit in bits[1:]:
        if bit == members:
            acc = acc.reshape((row_blocks, us, width))
        half = acc.shape[0] // 2
        acc = acc[:half] + swap(acc[half:], "ia", n_ia, bit)
    user_product = acc.reshape(us, width)
    return user_product, item_product


def solution(mesh):
    n_au, n_ia = mesh.shape["au"], mesh.shape["ia"]
    placed = (
        P(("au", "ia"), None),
        P(("ia", "au"), None),
        P(("au", "ia"), None),
        P(("ia", "au"), None),
        P("au", "ia"),
    )
    return jax.shard_map(
        functools.partial(on_device, n_au=n_au, n_ia=n_ia),
        mesh=mesh,
        in_specs=placed,
        out_specs=(P(("au", "ia"), None), P(("ia", "au"), None)),
        check_vma=False,
    )
```

time: 177 us -> 54.9 us (0.31)
  blocking collectives: 60.2 us -> 0 us
  waiting for transfers between devices: 75.5 us -> 27.9 us
  starting transfers between devices: 0.08 us -> 15.9 us
  between operations: 14.8 us -> 0.73 us
  matrix products: 9.7 us -> 0 us
  local copies, waits for them, and re-layouts: 11.6 us -> 2.06 us
  Pallas kernels: 0 us -> 4.7 us
    reduce_scatter x2 -> x0, waiting for transfers between devices: 75.5 us -> none  [the longest x1 53.2 us: on_device(): lax.psum_scatter(part_user, 'ia', scatter_dimension=0, tiled=True)]
    all_gather x4 -> x0, blocking collectives: 60.2 us -> none  [the longest x1 24.1 us: on_device(): lax.all_gather(user_factors, 'ia', axis=0, tiled=True)]
    ppermute x0 -> x11, waiting for transfers between devices: none -> 27.9 us  [swap(): return lax.ppermute(x, axis, [(i, i ^ bit) for i in range(size)])]
    ppermute x0 -> x11, starting transfers between devices: none -> 15.9 us  [swap(): return lax.ppermute(x, axis, [(i, i ^ bit) for i in range(size)])]
    dot_general x7 -> x0, matrix products: 9.7 us -> none  [the longest x1 3.88 us: one_turn(): jnp.einsum('gk,gar->kar', onehot_rows, to_user, precision=lax.Precision.H...]
    gather x5 -> x0, local copies, waits for them, and re-layouts: 5.12 us -> none  [the longest x1 1.6 us: one_turn(): dvrow = itan_tiles[csel]]
    pallas_call x0 -> x1, Pallas kernels: none -> 4.7 us  [on_device(): pl.pallas_call(functools.partial(region_kernel, n_groups=len(pieces), n_i...]
    mul x2 -> x0, local copies, waits for them, and re-layouts: 2.21 us -> none  [the longest x1 1.31 us: region_pass(): acc_item * scaling]
  transfers between devices with their start and end apart: 2 -> 11, of which waited for: 2 -> 10; matrix products, arithmetic and copies ran while one was open for 1% -> 1% of each run, Pallas kernels for 0% -> 0%
where the time goes in v1:
time: 54.9 us; the launch traced here: 54.7 us
  waiting for transfers between devices  27.9 us (51%)
  starting transfers between devices  15.9 us (29%)
  Pallas kernels  4.7 us (9%)
  other arithmetic  3.38 us (6%)
  local copies, waits for them, and re-layouts  2.06 us (4%)
  between operations  0.73 us (1%)
    ppermute x11, waiting for transfers between devices, swap(): return lax.ppermute(x, axis, [(i, i ^ bit) for i in range(size)])  27.9 us
    ppermute x11, starting transfers between devices, swap(): return lax.ppermute(x, axis, [(i, i ^ bit) for i in range(size)])  15.9 us
    pallas_call x1, Pallas kernels, on_device(): pl.pallas_call(functools.partial(region_kernel, n_groups=len(pieces), n_i...  4.7 us
    unnamed x16, local copies, waits for them, and re-layouts  2.04 us
  transfers between devices with their start and end apart: 11, of which 10 were waited for; matrix products, arithmetic and copies ran while one was open for 1% of the time, Pallas kernels for 0%

profile of v1, /device:TPU:0, one launch (start us, length us, event | category | flops | bytes accessed | tf_op | source)
XLA Modules:
  0.0 54.7 jit_solution(16541920167698542556)
XLA Ops:
  0.6 0.0 copy-start.3
  0.6 0.8 %maximum_bitcast_fusion.1 = bf16[1,2,32,256]{3,2,1,0:T(8,128)(2,1)S(1)} fusion(bf16[1,32,256]{2,1,0:T(8,128)(2,1)} %bitcast.22, bf16[1,32,256]{2,1,0:T(8,128)(2,1)} %bitcast.23), kind=kLoop, calls=%fused_computation.10 | loop fusion | flops 16384 | bytes 65536 | tf_op jit(solution)/shard_map/broadcast_in_dim | solution.py:138
  1.4 4.1 %collective-permute-start = (bf16[1,2,32,256]{3,2,1,0:T(8,128)(2,1)S(1)}, bf16[1,2,32,256]{3,2,1,0:T(8,128)(2,1)S(1)}, u32[]{:S(2)}, u32[]{:S(2)}) collective-permute-start(bf16[1,2,32,256]{3,2,1,0:T(8,128)(2,1)S(1)} %maximum_bitcast_fusion.1), channel_id=1, source_target_pairs={{0,8},{1,9},{2,10},{3,11},{4,12},{5,13},{6,14},{7,15},{8,0},{9,1},... | collective-permute-start | bytes 98312 | tf_op jit(solution)/shard_map/ppermute | solution.py:20
  5.5 2.2 %collective-permute-done = bf16[1,2,32,256]{3,2,1,0:T(8,128)(2,1)S(1)} collective-permute-done((bf16[1,2,32,256]{3,2,1,0:T(8,128)(2,1)S(1)}, bf16[1,2,32,256]{3,2,1,0:T(8,128)(2,1)S(1)}, u32[]{:S(2)}, u32[]{:S(2)}) %collective-permute-start) | collective-permute-done | bytes 32800 | tf_op jit(solution)/shard_map/ppermute | solution.py:20
  7.7 1.6 %collective-permute-start.1 = (bf16[2,2,32,256]{3,2,1,0:T(8,128)(2,1)S(1)}, bf16[2,2,32,256]{3,2,1,0:T(8,128)(2,1)S(1)}, u32[]{:S(2)}, u32[]{:S(2)}) collective-permute-start(bf16[2,2,32,256]{3,2,1,0:T(8,128)(2,1)S(1)} %pad_maximum_fusion.1), channel_id=1, source_target_pairs={{0,4},{1,5},{2,6},{3,7},{4,0},{5,1},{6,2},{7,3},{8,12},{9,13},{10,... | collective-permute-start | bytes 196616 | tf_op jit(solution)/shard_map/ppermute | solution.py:20
  9.4 2.7 %collective-permute-done.1 = bf16[2,2,32,256]{3,2,1,0:T(8,128)(2,1)S(1)} collective-permute-done((bf16[2,2,32,256]{3,2,1,0:T(8,128)(2,1)S(1)}, bf16[2,2,32,256]{3,2,1,0:T(8,128)(2,1)S(1)}, u32[]{:S(2)}, u32[]{:S(2)}) %collective-permute-start.1) | collective-permute-done | bytes 65568 | tf_op jit(solution)/shard_map/ppermute | solution.py:20
  12.1 0.0 copy-start
  12.1 1.8 %collective-permute-start.2 = (bf16[1,4,2,32,256]{4,3,2,1,0:T(8,128)(2,1)S(1)}, bf16[1,4,2,32,256]{4,3,2,1,0:T(8,128)(2,1)S(1)}, u32[]{:S(2)}, u32[]{:S(2)}) collective-permute-start(bf16[1,4,2,32,256]{4,3,2,1,0:T(8,128)(2,1)S(1)} %maximum_bitcast_fusion.refs_1_), channel_id=1, source_target_pairs={{0,2},{1,3},{2,0},{3,1},{4,6},{5,7},{6,4},{7,5},{8,10},{9,11},{10,... | collective-permute-start | bytes 393224 | tf_op jit(solution)/shard_map/ppermute | solution.py:20
  13.9 0.0 copy-done.3
  13.9 1.5 %collective-permute-start.4 = (bf16[1,512,256]{2,1,0:T(8,128)(2,1)S(1)}, bf16[1,512,256]{2,1,0:T(8,128)(2,1)S(1)}, u32[]{:S(2)}, u32[]{:S(2)}) collective-permute-start(bf16[1,512,256]{2,1,0:T(8,128)(2,1)S(1)} %bitcast.19), channel_id=1, source_target_pairs={{0,16},{16,0},{1,17},{17,1},{2,18},{18,2},{3,19},{19,3},{4,20},{20... | collective-permute-start | bytes 786440 | tf_op jit(solution)/shard_map/ppermute | solution.py:20
  15.4 0.5 collective-permute-start.5
  15.9 1.2 %collective-permute-done.2.refs_2_ = bf16[1,4,2,32,256]{4,3,2,1,0:T(8,128)(2,1)S(1)} collective-permute-done((bf16[1,4,2,32,256]{4,3,2,1,0:T(8,128)(2,1)S(1)}, bf16[1,4,2,32,256]{4,3,2,1,0:T(8,128)(2,1)S(1)}, u32[]{:S(2)}, u32[]{:S(2)}) %collective-permute-start.2) | collective-permute-done | bytes 131104 | tf_op jit(solution)/shard_map/ppermute | solution.py:20
  17.1 0.0 copy-start.2
  17.2 0.0 copy-done
  17.2 0.6 %copy-done.2 = bf16[1,4,2,32,256]{4,3,2,1,0:T(8,128)(2,1)} copy-done((bf16[1,4,2,32,256]{4,3,2,1,0:T(8,128)(2,1)}, bf16[1,4,2,32,256]{4,3,2,1,0:T(8,128)(2,1)S(1)}, u32[]{:S(2)}) %copy-start.2) | copy-done | bytes 131096
  17.8 0.0 collective-permute-start.3
  17.8 4.1 %collective-permute-done.4.refs_5_ = bf16[1,512,256]{2,1,0:T(8,128)(2,1)S(1)} collective-permute-done((bf16[1,512,256]{2,1,0:T(8,128)(2,1)S(1)}, bf16[1,512,256]{2,1,0:T(8,128)(2,1)S(1)}, u32[]{:S(2)}, u32[]{:S(2)}) %collective-permute-start.4) | collective-permute-done | bytes 262176 | tf_op jit(solution)/shard_map/ppermute | solution.py:20
  21.9 0.0 copy-start.4
  21.9 2.8 %collective-permute-done.5.refs_7_ = bf16[1,512,256]{2,1,0:T(8,128)(2,1)S(1)} collective-permute-done((bf16[1,512,256]{2,1,0:T(8,128)(2,1)}, bf16[1,512,256]{2,1,0:T(8,128)(2,1)S(1)}, u32[]{:S(2)}, u32[]{:S(2)}) %collective-permute-start.5) | collective-permute-done | bytes 262176 | tf_op jit(solution)/shard_map/ppermute | solution.py:20
  24.7 0.0 copy-start.5
  24.7 0.0 collective-permute-done.3.refs_3_
  24.7 0.0 copy-done.4
  24.7 0.7 %copy-done.5 = bf16[1,512,256]{2,1,0:T(8,128)(2,1)} copy-done((bf16[1,512,256]{2,1,0:T(8,128)(2,1)}, bf16[1,512,256]{2,1,0:T(8,128)(2,1)S(1)}, u32[]{:S(2)}) %copy-start.5) | copy-done | bytes 262168
  25.4 0.0 copy-start.6
  25.5 0.7 %copy-done.6 = bf16[2,4,2,32,256]{4,3,2,1,0:T(8,128)(2,1)} copy-done((bf16[2,4,2,32,256]{4,3,2,1,0:T(8,128)(2,1)}, bf16[2,4,2,32,256]{4,3,2,1,0:T(8,128)(2,1)S(1)}, u32[]{:S(2)}) %copy-start.6) | copy-done | bytes 262168
  26.1 4.7 %region.1 = (f32[2,4,32,256]{3,2,1,0:T(8,128)}, f32[2,4,32,256]{3,2,1,0:T(8,128)}, f32[1,512,256]{2,1,0:T(8,128)}, f32[1,512,256]{2,1,0:T(8,128)}) custom-call(s32[4,8]{1,0:T(4,128)} %refs_0_.1, bf16[1,4,2,32,256]{4,3,2,1,0:T(8,128)(2,1)} %copy-done, bf16[1,4,2,32,256]{4,3,2,1,0:T(8,128)(2,1)} %copy-done.2, bf16[2,4,2,32,256]{4,3,2,1,0:T(8,128)(2,1)} %copy-done.6, ...), custom_call_target="tpu_custom_call" | custom-call | tf_op jit(solution)/shard_map/region/pallas_call | solution.py:145
  30.8 0.0 collective-permute-start.6
  30.9 1.7 %collective-permute-done.6 = f32[2,4,32,256]{3,2,1,0:T(8,128)S(1)} collective-permute-done((f32[2,4,32,256]{3,2,1,0:T(8,128)}, f32[2,4,32,256]{3,2,1,0:T(8,128)S(1)}, u32[]{:S(2)}, u32[]{:S(2)}) %collective-permute-start.6) | collective-permute-done | bytes 262176 | tf_op jit(solution)/shard_map/ppermute | solution.py:20
  32.6 0.0 copy-start.7
  32.6 1.0 %add.15 = f32[2,4,32,256]{3,2,1,0:T(8,128)S(1)} add(f32[2,4,32,256]{3,2,1,0:T(8,128)} %get-tuple-element.6, f32[2,4,32,256]{3,2,1,0:T(8,128)S(1)} %collective-permute-done.6) | non-fusion elementwise | flops 65536 | bytes 786432 | tf_op jit(solution)/shard_map/add | solution.py:180
  33.6 0.0 copy-start.1
  33.7 0.5 %collective-permute-start.7 = (f32[1,4,32,256]{3,2,1,0:T(8,128)S(1)}, f32[1,4,32,256]{3,2,1,0:T(8,128)S(1)}, u32[]{:S(2)}, u32[]{:S(2)}) collective-permute-start(f32[1,4,32,256]{3,2,1,0:T(8,128)S(1)} %slice.33), channel_id=1, source_target_pairs={{0,2},{1,3},{2,0},{3,1},{4,6},{5,7},{6,4},{7,5},{8,10},{9,11},{10,... | collective-permute-start | bytes 393224 | tf_op jit(solution)/shard_map/ppermute | solution.py:20
  34.2 5.1 %collective-permute-done.7 = f32[1,4,32,256]{3,2,1,0:T(8,128)S(1)} collective-permute-done((f32[1,4,32,256]{3,2,1,0:T(8,128)S(1)}, f32[1,4,32,256]{3,2,1,0:T(8,128)S(1)}, u32[]{:S(2)}, u32[]{:S(2)}) %collective-permute-start.7) | collective-permute-done | bytes 131104 | tf_op jit(solution)/shard_map/ppermute | solution.py:20
  39.3 1.7 %collective-permute-start.8 = (f32[2,32,256]{2,1,0:T(8,128)S(1)}, f32[2,32,256]{2,1,0:T(8,128)S(1)}, u32[]{:S(2)}, u32[]{:S(2)}) collective-permute-start(f32[2,32,256]{2,1,0:T(8,128)S(1)} %slice_bitcast_fusion), channel_id=1, source_target_pairs={{0,4},{1,5},{2,6},{3,7},{4,0},{5,1},{6,2},{7,3},{8,12},{9,13},{10,... | collective-permute-start | bytes 196616 | tf_op jit(solution)/shard_map/ppermute | solution.py:20
  41.0 0.0 copy-done.7
  41.0 1.5 %collective-permute-start.10 = (f32[1,512,256]{2,1,0:T(8,128)S(1)}, f32[1,512,256]{2,1,0:T(8,128)S(1)}, u32[]{:S(2)}, u32[]{:S(2)}) collective-permute-start(f32[1,512,256]{2,1,0:T(8,128)S(1)} %copy-done.7), channel_id=1, source_target_pairs={{0,16},{16,0},{1,17},{17,1},{2,18},{18,2},{3,19},{19,3},{4,20},{20... | collective-permute-start | bytes 1572872 | tf_op jit(solution)/shard_map/ppermute | solution.py:20
  42.5 1.1 %collective-permute-done.8 = f32[2,32,256]{2,1,0:T(8,128)S(1)} collective-permute-done((f32[2,32,256]{2,1,0:T(8,128)S(1)}, f32[2,32,256]{2,1,0:T(8,128)S(1)}, u32[]{:S(2)}, u32[]{:S(2)}) %collective-permute-start.8) | collective-permute-done | bytes 65568 | tf_op jit(solution)/shard_map/ppermute | solution.py:20
  43.7 2.7 %collective-permute-start.9 = (f32[1,32,256]{2,1,0:T(8,128)S(1)}, f32[1,32,256]{2,1,0:T(8,128)S(1)}, u32[]{:S(2)}, u32[]{:S(2)}) collective-permute-start(f32[1,32,256]{2,1,0:T(8,128)S(1)} %slice.37), channel_id=1, source_target_pairs={{0,8},{1,9},{2,10},{3,11},{4,12},{5,13},{6,14},{7,15},{8,0},{9,1},... | collective-permute-start | bytes 98312 | tf_op jit(solution)/shard_map/ppermute | solution.py:20
  46.4 2.2 %collective-permute-done.9 = f32[1,32,256]{2,1,0:T(8,128)S(1)} collective-permute-done((f32[1,32,256]{2,1,0:T(8,128)S(1)}, f32[1,32,256]{2,1,0:T(8,128)S(1)}, u32[]{:S(2)}, u32[]{:S(2)}) %collective-permute-start.9) | collective-permute-done | bytes 32800 | tf_op jit(solution)/shard_map/ppermute | solution.py:20
  48.6 0.6 %fusion.1 = f32[32,256]{1,0:T(8,128)} fusion(f32[1,32,256]{2,1,0:T(8,128)S(1)} %collective-permute-done.9, f32[2,32,256]{2,1,0:T(8,128)S(1)} %fusion), kind=kLoop, calls=%fused_computation.9 | loop fusion | flops 8192 | bytes 98304 | tf_op jit(solution)/shard_map/reshape | solution.py:186
  49.2 4.6 %collective-permute-done.10 = f32[1,512,256]{2,1,0:T(8,128)S(1)} collective-permute-done((f32[1,512,256]{2,1,0:T(8,128)S(1)}, f32[1,512,256]{2,1,0:T(8,128)S(1)}, u32[]{:S(2)}, u32[]{:S(2)}) %collective-permute-start.10) | collective-permute-done | bytes 524320 | tf_op jit(solution)/shard_map/ppermute | solution.py:20
  53.8 0.0 copy-done.1
  53.8 0.9 %add_bitcast_fusion = f32[512,256]{1,0:T(8,128)} fusion(f32[1,512,256]{2,1,0:T(8,128)S(1)} %copy-done.1, f32[1,512,256]{2,1,0:T(8,128)S(1)} %collective-permute-done.10), kind=kLoop, calls=%fused_computation | loop fusion | flops 131072 | bytes 1572864 | tf_op jit(solution)/shard_map/squeeze | solution.py:177
  (8 shorter events, 0.1 us)
Async XLA Ops:
  0.6 13.2 %copy-start.3 = (bf16[512,256]{1,0:T(8,128)(2,1)S(1)}, bf16[512,256]{1,0:T(8,128)(2,1)}, u32[]{:S(2)}) copy-start(bf16[512,256]{1,0:T(8,128)(2,1)} %param.6) | copy-start | bytes 786436
  1.4 6.3 %collective-permute-start = (bf16[1,2,32,256]{3,2,1,0:T(8,128)(2,1)S(1)}, bf16[1,2,32,256]{3,2,1,0:T(8,128)(2,1)S(1)}, u32[]{:S(2)}, u32[]{:S(2)}) collective-permute-start(bf16[1,2,32,256]{3,2,1,0:T(8,128)(2,1)S(1)} %maximum_bitcast_fusion.1), channel_id=1, source_target_pairs={{0,8},{1,9},{2,10},{3,11},{4,12},{5,13},{6,14},{7,15},{8,0},{9,1},... | collective-permute-start | bytes 98312 | tf_op jit(solution)/shard_map/ppermute | solution.py:20
  7.7 4.3 %collective-permute-start.1 = (bf16[2,2,32,256]{3,2,1,0:T(8,128)(2,1)S(1)}, bf16[2,2,32,256]{3,2,1,0:T(8,128)(2,1)S(1)}, u32[]{:S(2)}, u32[]{:S(2)}) collective-permute-start(bf16[2,2,32,256]{3,2,1,0:T(8,128)(2,1)S(1)} %pad_maximum_fusion.1), channel_id=1, source_target_pairs={{0,4},{1,5},{2,6},{3,7},{4,0},{5,1},{6,2},{7,3},{8,12},{9,13},{10,... | collective-permute-start | bytes 196616 | tf_op jit(solution)/shard_map/ppermute | solution.py:20
  12.1 5.1 %copy-start = (bf16[1,4,2,32,256]{4,3,2,1,0:T(8,128)(2,1)}, bf16[1,4,2,32,256]{4,3,2,1,0:T(8,128)(2,1)S(1)}, u32[]{:S(2)}) copy-start(bf16[1,4,2,32,256]{4,3,2,1,0:T(8,128)(2,1)S(1)} %maximum_bitcast_fusion.refs_1_) | copy-start | bytes 393220
  12.1 5.0 %collective-permute-start.2 = (bf16[1,4,2,32,256]{4,3,2,1,0:T(8,128)(2,1)S(1)}, bf16[1,4,2,32,256]{4,3,2,1,0:T(8,128)(2,1)S(1)}, u32[]{:S(2)}, u32[]{:S(2)}) collective-permute-start(bf16[1,4,2,32,256]{4,3,2,1,0:T(8,128)(2,1)S(1)} %maximum_bitcast_fusion.refs_1_), channel_id=1, source_target_pairs={{0,2},{1,3},{2,0},{3,1},{4,6},{5,7},{6,4},{7,5},{8,10},{9,11},{10,... | collective-permute-start | bytes 393224 | tf_op jit(solution)/shard_map/ppermute | solution.py:20
  13.9 8.0 %collective-permute-start.4 = (bf16[1,512,256]{2,1,0:T(8,128)(2,1)S(1)}, bf16[1,512,256]{2,1,0:T(8,128)(2,1)S(1)}, u32[]{:S(2)}, u32[]{:S(2)}) collective-permute-start(bf16[1,512,256]{2,1,0:T(8,128)(2,1)S(1)} %bitcast.19), channel_id=1, source_target_pairs={{0,16},{16,0},{1,17},{17,1},{2,18},{18,2},{3,19},{19,3},{4,20},{20... | collective-permute-start | bytes 786440 | tf_op jit(solution)/shard_map/ppermute | solution.py:20
  15.4 9.3 %collective-permute-start.5 = (bf16[1,512,256]{2,1,0:T(8,128)(2,1)}, bf16[1,512,256]{2,1,0:T(8,128)(2,1)S(1)}, u32[]{:S(2)}, u32[]{:S(2)}) collective-permute-start(bf16[1,512,256]{2,1,0:T(8,128)(2,1)} %bitcast.20), channel_id=1, source_target_pairs={{0,16},{16,0},{1,17},{17,1},{2,18},{18,2},{3,19},{19,3},{4,20},{20... | collective-permute-start | bytes 786440 | tf_op jit(solution)/shard_map/ppermute | solution.py:20
  17.1 0.7 %copy-start.2 = (bf16[1,4,2,32,256]{4,3,2,1,0:T(8,128)(2,1)}, bf16[1,4,2,32,256]{4,3,2,1,0:T(8,128)(2,1)S(1)}, u32[]{:S(2)}) copy-start(bf16[1,4,2,32,256]{4,3,2,1,0:T(8,128)(2,1)S(1)} %collective-permute-done.2.refs_2_) | copy-start | bytes 393220
  17.8 6.9 %collective-permute-start.3 = (bf16[2,4,2,32,256]{4,3,2,1,0:T(8,128)(2,1)S(1)}, bf16[2,4,2,32,256]{4,3,2,1,0:T(8,128)(2,1)S(1)}, u32[]{:S(2)}, u32[]{:S(2)}) collective-permute-start(bf16[2,4,2,32,256]{4,3,2,1,0:T(8,128)(2,1)S(1)} %pad_maximum_fusion), channel_id=1, source_target_pairs={{0,1},{1,0},{2,3},{3,2},{4,5},{5,4},{6,7},{7,6},{8,9},{9,8},{10,11... | collective-permute-start | bytes 786440 | tf_op jit(solution)/shard_map/ppermute | solution.py:20
  21.9 2.8 %copy-start.4 = (bf16[1,512,256]{2,1,0:T(8,128)(2,1)}, bf16[1,512,256]{2,1,0:T(8,128)(2,1)S(1)}, u32[]{:S(2)}) copy-start(bf16[1,512,256]{2,1,0:T(8,128)(2,1)S(1)} %collective-permute-done.4.refs_5_) | copy-start | bytes 786436
  24.7 0.7 %copy-start.5 = (bf16[1,512,256]{2,1,0:T(8,128)(2,1)}, bf16[1,512,256]{2,1,0:T(8,128)(2,1)S(1)}, u32[]{:S(2)}) copy-start(bf16[1,512,256]{2,1,0:T(8,128)(2,1)S(1)} %collective-permute-done.5.refs_7_) | copy-start | bytes 786436
  25.4 0.7 %copy-start.6 = (bf16[2,4,2,32,256]{4,3,2,1,0:T(8,128)(2,1)}, bf16[2,4,2,32,256]{4,3,2,1,0:T(8,128)(2,1)S(1)}, u32[]{:S(2)}) copy-start(bf16[2,4,2,32,256]{4,3,2,1,0:T(8,128)(2,1)S(1)} %collective-permute-done.3.refs_3_) | copy-start | bytes 786436
  30.8 1.7 %collective-permute-start.6 = (f32[2,4,32,256]{3,2,1,0:T(8,128)}, f32[2,4,32,256]{3,2,1,0:T(8,128)S(1)}, u32[]{:S(2)}, u32[]{:S(2)}) collective-permute-start(f32[2,4,32,256]{3,2,1,0:T(8,128)} %get-tuple-element.7), channel_id=1, source_target_pairs={{0,1},{1,0},{2,3},{3,2},{4,5},{5,4},{6,7},{7,6},{8,9},{9,8},{10,11... | collective-permute-start | bytes 786440 | tf_op jit(solution)/shard_map/ppermute | solution.py:20
  32.6 8.4 %copy-start.7 = (f32[1,512,256]{2,1,0:T(8,128)S(1)}, f32[1,512,256]{2,1,0:T(8,128)}, u32[]{:S(2)}) copy-start(f32[1,512,256]{2,1,0:T(8,128)} %get-tuple-element.9) | copy-start | bytes 1572868
  33.6 20.2 %copy-start.1 = (f32[1,512,256]{2,1,0:T(8,128)S(1)}, f32[1,512,256]{2,1,0:T(8,128)}, u32[]{:S(2)}) copy-start(f32[1,512,256]{2,1,0:T(8,128)} %get-tuple-element.8) | copy-start | bytes 1572868
  33.7 5.6 %collective-permute-start.7 = (f32[1,4,32,256]{3,2,1,0:T(8,128)S(1)}, f32[1,4,32,256]{3,2,1,0:T(8,128)S(1)}, u32[]{:S(2)}, u32[]{:S(2)}) collective-permute-start(f32[1,4,32,256]{3,2,1,0:T(8,128)S(1)} %slice.33), channel_id=1, source_target_pairs={{0,2},{1,3},{2,0},{3,1},{4,6},{5,7},{6,4},{7,5},{8,10},{9,11},{10,... | collective-permute-start | bytes 393224 | tf_op jit(solution)/shard_map/ppermute | solution.py:20
  39.3 4.3 %collective-permute-start.8 = (f32[2,32,256]{2,1,0:T(8,128)S(1)}, f32[2,32,256]{2,1,0:T(8,128)S(1)}, u32[]{:S(2)}, u32[]{:S(2)}) collective-permute-start(f32[2,32,256]{2,1,0:T(8,128)S(1)} %slice_bitcast_fusion), channel_id=1, source_target_pairs={{0,4},{1,5},{2,6},{3,7},{4,0},{5,1},{6,2},{7,3},{8,12},{9,13},{10,... | collective-permute-start | bytes 196616 | tf_op jit(solution)/shard_map/ppermute | solution.py:20
  41.0 12.8 %collective-permute-start.10 = (f32[1,512,256]{2,1,0:T(8,128)S(1)}, f32[1,512,256]{2,1,0:T(8,128)S(1)}, u32[]{:S(2)}, u32[]{:S(2)}) collective-permute-start(f32[1,512,256]{2,1,0:T(8,128)S(1)} %copy-done.7), channel_id=1, source_target_pairs={{0,16},{16,0},{1,17},{17,1},{2,18},{18,2},{3,19},{19,3},{4,20},{20... | collective-permute-start | bytes 1572872 | tf_op jit(solution)/shard_map/ppermute | solution.py:20
  43.7 4.9 %collective-permute-start.9 = (f32[1,32,256]{2,1,0:T(8,128)S(1)}, f32[1,32,256]{2,1,0:T(8,128)S(1)}, u32[]{:S(2)}, u32[]{:S(2)}) collective-permute-start(f32[1,32,256]{2,1,0:T(8,128)S(1)} %slice.37), channel_id=1, source_target_pairs={{0,8},{1,9},{2,10},{3,11},{4,12},{5,13},{6,14},{7,15},{8,0},{9,1},... | collective-permute-start | bytes 98312 | tf_op jit(solution)/shard_map/ppermute | solution.py:20

commit v2 on v0

v2 whole, which is shorter than its diff:
```python
import functools
import math

import jax
import jax.numpy as jnp
from jax import lax
from jax.experimental import pallas as pl
from jax.experimental.pallas import tpu as pltpu
from jax.sharding import PartitionSpec as P

f32 = jnp.float32
bf16 = jnp.bfloat16
NN = (((1,), (0,)), ((), ()))
NT = (((1,), (1,)), ((), ()))
TN = (((0,), (0,)), ((), ()))
dot = functools.partial(lax.dot_general, preferred_element_type=f32)
TILE = 256


def swap(x, axis, size, bits):
    return lax.ppermute(x, axis, [(i, i ^ bits) for i in range(size)])


def bits_of(low, high):
    out = []
    bit = high // 2
    while bit >= low:
        out.append(bit)
        bit //= 2
    return out


def relative(bits):
    order = [0]
    for bit in bits:
        order = order + [r ^ bit for r in order]
    return order


def region_kernel(*refs, n_users, rows_of, cols_of, scale, add_user, add_item):
    mask = refs[0]
    users = refs[1 : 1 + n_users]
    at = 1 + n_users
    fac_i, tan_i = refs[at : at + 2]
    at += 2
    user_in = refs[at] if add_user else None
    at += add_user
    item_in = refs[at] if add_item else None
    at += add_item
    user_out, item_out, u_all, c_all = refs[at:]

    n_a, _, us, _ = users[0].shape
    n_pieces, it_dev, _ = fac_i.shape
    me_row = lax.axis_index("ia") // rows_of[0]
    me_col = lax.axis_index("au")
    for b, ref in enumerate(users):
        for k in range(n_a):
            for ft in range(2):
                u_all[ft, pl.ds((b * n_a + k) * us, us), :] = ref[k, ft]
    total_rows = n_users * n_a * us
    tile = min(TILE, total_rows)
    in_tile = tile // us
    block = cols_of[0]
    lane = lax.broadcasted_iota(jnp.int32, (1, tile), 1)
    sub = min(TILE, it_dev)
    for t in range(total_rows // tile):
        rows = pl.ds(t * tile, tile)
        fac = u_all[0, rows, :]
        tan = u_all[1, rows, :]
        total = None
        for k in range(n_pieces):
            for ib in range(it_dev // sub):
                items = pl.ds(ib * sub, sub)
                v = fac_i[k, items, :]
                dv = tan_i[k, items, :]
                s = dot(v, fac, NT)
                tt = dot(v, tan, NT) + dot(dv, fac, NT)
                seen = []
                for i in range(sub // block):
                    col = (me_col ^ cols_of[1][k]) * (it_dev // block) + ib * (sub // block) + i
                    row = None
                    for j in reversed(range(in_tile)):
                        m = mask[me_row ^ rows_of[1][t * in_tile + j], col].astype(f32) * scale
                        full = jnp.full((1, tile), m, f32)
                        row = full if row is None else jnp.where(lane < (j + 1) * us, full, row)
                    seen.append(jnp.broadcast_to(row, (block, tile)))
                seen = jnp.concatenate(seen, 0)
                e = jnp.exp(jnp.abs(s) * -scale)
                p = 1.0 / (1.0 + e)
                c = (e * p * p * (tt * seen)).astype(bf16)
                c_all[items, :] = c
                r = dot(c, fac, NN) * scale
                if t > 0:
                    r = r + item_out[k, items, :]
                elif item_in is not None:
                    r = r + item_in[k, items, :]
                item_out[k, items, :] = r
            part = dot(c_all[...], fac_i[k], TN)
            total = part if total is None else total + part
        total = total * scale
        for j in range(in_tile):
            b, k = divmod(t * in_tile + j, n_a)
            r = total[j * us : (j + 1) * us]
            if user_in is not None:
                r = r + user_in[b, k]
            user_out[b, k] = r


def in_vmem(x):
    return pltpu.with_memory_space_constraint(x, pltpu.VMEM)


def region(mask, users, items, user_sum, item_sum, **static):
    vm = pl.BlockSpec(memory_space=pltpu.VMEM)
    n_a, _, us, width = users[0].shape
    n_pieces, it_dev, _ = items[0].shape
    given = [in_vmem(x) for x in (*users, *items)]
    aliases = {}
    if user_sum is not None:
        aliases[1 + len(given)] = 0
        given.append(in_vmem(user_sum))
    if item_sum is not None:
        aliases[1 + len(given)] = 1
        given.append(in_vmem(item_sum))
    total_rows = len(users) * n_a * us
    return pl.pallas_call(
        functools.partial(
            region_kernel,
            n_users=len(users),
            add_user=user_sum is not None,
            add_item=item_sum is not None,
            **static,
        ),
        in_specs=[pl.BlockSpec(memory_space=pltpu.SMEM)] + [vm] * len(given),
        out_specs=[vm, vm],
        out_shape=[
            pltpu.VMEM((len(users), n_a, us, width), f32),
            pltpu.VMEM((n_pieces, it_dev, width), f32),
        ],
        input_output_aliases=aliases,
        scratch_shapes=[
            pltpu.VMEM((2, total_rows, width), bf16),
            pltpu.VMEM((it_dev, min(TILE, total_rows)), bf16),
        ],
        compiler_params=pltpu.CompilerParams(vmem_limit_bytes=16 * 2**20),
    )(mask, *given)


def on_device(user_factors, item_factors, user_tangent, item_tangent, block_mask, n_au, n_ia):
    us, width = user_factors.shape
    row_blocks, _ = block_mask.shape
    block = us * n_ia // row_blocks
    members = block // us
    scale = 1.0 / math.sqrt(width)
    core, near = 1, [2, 4, 6]
    a_bits = bits_of(8, n_ia)

    item_bits = bits_of(1, n_au)
    facs, tans = [item_factors[None]], [item_tangent[None]]
    for n, bit in enumerate(item_bits):
        held_f = facs[0] if n == 0 else jnp.concatenate(facs, 0)
        held_t = tans[0] if n == 0 else jnp.concatenate(tans, 0)
        facs.append(swap(held_f, "au", n_au, bit))
        tans.append(swap(held_t, "au", n_au, bit))
    rel_items = relative(item_bits)

    far = jnp.stack([user_factors, user_tangent])[None]
    for n, bit in enumerate(a_bits):
        far = jnp.concatenate([far, swap(far, "ia", n_ia, bit)], 0)
    rel_a = relative(a_bits)
    mine = [far] + [swap(far, "ia", n_ia, b) for b in near]
    other = [swap(x, "ia", n_ia, core) for x in mine]
    rows_of = (members, [(b ^ r) // members for b in [0, *near] for r in rel_a])

    sums = {0: None, 1: None}
    item_sums = []
    at = 0
    for g, (f, t) in enumerate(zip(facs, tans)):
        n = f.shape[0]
        cols_of = (block, rel_items[at : at + n])
        at += n
        item_sum = None
        last = g == len(facs) - 1
        for half in (1, 0) if last else (0, 1):
            sums[half], item_sum = region(
                block_mask,
                other if half else mine,
                (f, t),
                sums[half],
                item_sum,
                rows_of=rows_of,
                cols_of=cols_of,
                scale=scale,
            )
        item_sums.append(item_sum)

    core_in = swap(sums[1], "ia", n_ia, core)
    for n, bit in enumerate(item_bits[::-1]):
        back = swap(item_sums.pop(), "au", n_au, bit)
        sizes = [h.shape[0] for h in item_sums]
        cuts = [sum(sizes[:i]) for i in range(len(sizes))]
        item_sums = [h + back[c : c + s] for h, c, s in zip(item_sums, cuts, sizes)]
    item_product = item_sums[0][0]

    keep = sums[0] + core_in
    acc = keep[0]
    for i, b in enumerate(near):
        acc = acc + swap(keep[i + 1], "ia", n_ia, b)
    for n, bit in enumerate(a_bits[::-1]):
        half = acc.shape[0] // 2
        acc = acc[:half] + swap(acc[half:], "ia", n_ia, bit)
    user_product = acc.reshape(us, width)
    return user_product, item_product


def solution(mesh):
    n_au, n_ia = mesh.shape["au"], mesh.shape["ia"]
    placed = (
        P(("au", "ia"), None),
        P(("ia", "au"), None),
        P(("au", "ia"), None),
        P(("ia", "au"), None),
        P("au", "ia"),
    )

    def body(*args):
        return on_device(*args, n_au=n_au, n_ia=n_ia)

    return jax.shard_map(
        body,
        mesh=mesh,
        in_specs=placed,
        out_specs=(P(("au", "ia"), None), P(("ia", "au"), None)),
        check_vma=False,
    )
```

time: 177 us -> 41.4 us (0.23)
  waiting for transfers between devices: 75.5 us -> 12.2 us
  blocking collectives: 60.2 us -> 0 us
  starting transfers between devices: 0.08 us -> 18.3 us
  between operations: 14.8 us -> 0.77 us
  matrix products: 9.7 us -> 0 us
  local copies, waits for them, and re-layouts: 11.6 us -> 1.93 us
  Pallas kernels: 0 us -> 5.72 us
  other arithmetic: 4.41 us -> 2.28 us
    reduce_scatter x2 -> x0, waiting for transfers between devices: 75.5 us -> none  [the longest x1 53.2 us: on_device(): lax.psum_scatter(part_user, 'ia', scatter_dimension=0, tiled=True)]
    all_gather x4 -> x0, blocking collectives: 60.2 us -> none  [the longest x1 24.1 us: on_device(): lax.all_gather(user_factors, 'ia', axis=0, tiled=True)]
    ppermute x0 -> x16, starting transfers between devices: none -> 18.3 us  [swap(): return lax.ppermute(x, axis, [(i, i ^ bits) for i in range(size)])]
    ppermute x0 -> x16, waiting for transfers between devices: none -> 12.2 us  [swap(): return lax.ppermute(x, axis, [(i, i ^ bits) for i in range(size)])]
    dot_general x7 -> x0, matrix products: 9.7 us -> none  [the longest x1 3.88 us: one_turn(): jnp.einsum('gk,gar->kar', onehot_rows, to_user, precision=lax.Precision.H...]
    pallas_call x0 -> x4, Pallas kernels: none -> 5.72 us  [region(): pl.pallas_call(functools.partial(region_kernel, n_users=len(users), add_u...]
    gather x5 -> x0, local copies, waits for them, and re-layouts: 5.12 us -> none  [the longest x1 1.6 us: one_turn(): dvrow = itan_tiles[csel]]
    mul x2 -> x0, local copies, waits for them, and re-layouts: 2.21 us -> none  [the longest x1 1.31 us: region_pass(): acc_item * scaling]
  transfers between devices with their start and end apart: 2 -> 16, of which waited for: 2 -> 8; matrix products, arithmetic and copies ran while one was open for 1% -> 2% of each run, Pallas kernels for 0% -> 10%
where the time goes in v2:
time: 41.4 us; the launch traced here: 41.1 us
  starting transfers between devices  18.3 us (44%)
  waiting for transfers between devices  12.2 us (29%)
  Pallas kernels  5.72 us (14%)
  other arithmetic  2.28 us (6%)
  local copies, waits for them, and re-layouts  1.93 us (5%)
  between operations  0.77 us (2%)
    ppermute x16, starting transfers between devices, swap(): return lax.ppermute(x, axis, [(i, i ^ bits) for i in range(size)])  18.3 us
    ppermute x16, waiting for transfers between devices, swap(): return lax.ppermute(x, axis, [(i, i ^ bits) for i in range(size)])  12.2 us
    pallas_call x4, Pallas kernels, region(): pl.pallas_call(functools.partial(region_kernel, n_users=len(users), add_u...  5.72 us
    unnamed x8, local copies, waits for them, and re-layouts  1.91 us
    squeeze x1, other arithmetic, on_device(): item_product = item_sums[0][0]  0.86 us
  transfers between devices with their start and end apart: 16, of which 8 were waited for; matrix products, arithmetic and copies ran while one was open for 2% of the time, Pallas kernels for 10%

profile of v2, /device:TPU:0, one launch (start us, length us, event | category | flops | bytes accessed | tf_op | source)
XLA Modules:
  0.0 41.1 jit_solution(13152038160012412695)
XLA Ops:
  0.6 0.7 %maximum_bitcast_fusion = bf16[1,2,32,256]{3,2,1,0:T(8,128)(2,1)S(1)} fusion(bf16[1,32,256]{2,1,0:T(8,128)(2,1)} %bitcast.30, bf16[1,32,256]{2,1,0:T(8,128)(2,1)} %bitcast.31), kind=kLoop, calls=%fused_computation.11 | loop fusion | flops 16384 | bytes 65536 | tf_op jit(solution)/shard_map/broadcast_in_dim | solution.py:167
  1.4 4.1 %collective-permute-start = (bf16[1,2,32,256]{3,2,1,0:T(8,128)(2,1)S(1)}, bf16[1,2,32,256]{3,2,1,0:T(8,128)(2,1)S(1)}, u32[]{:S(2)}, u32[]{:S(2)}) collective-permute-start(bf16[1,2,32,256]{3,2,1,0:T(8,128)(2,1)S(1)} %maximum_bitcast_fusion), channel_id=1, source_target_pairs={{0,8},{1,9},{2,10},{3,11},{4,12},{5,13},{6,14},{7,15},{8,0},{9,1},... | collective-permute-start | bytes 98312 | tf_op jit(solution)/shard_map/ppermute | solution.py:21
  5.4 1.5 %collective-permute-start.4 = (bf16[1,512,256]{2,1,0:T(8,128)(2,1)}, bf16[1,512,256]{2,1,0:T(8,128)(2,1)S(1)}, u32[]{:S(2)}, u32[]{:S(2)}) collective-permute-start(bf16[1,512,256]{2,1,0:T(8,128)(2,1)} %bitcast.24), channel_id=1, source_target_pairs={{0,16},{16,0},{1,17},{17,1},{2,18},{18,2},{3,19},{19,3},{4,20},{20... | collective-permute-start | bytes 786440 | tf_op jit(solution)/shard_map/ppermute | solution.py:21
  7.0 0.0 copy-start.3
  7.0 0.5 %collective-permute-start.5 = (bf16[1,512,256]{2,1,0:T(8,128)(2,1)}, bf16[1,512,256]{2,1,0:T(8,128)(2,1)S(1)}, u32[]{:S(2)}, u32[]{:S(2)}) collective-permute-start(bf16[1,512,256]{2,1,0:T(8,128)(2,1)} %bitcast.27), channel_id=1, source_target_pairs={{0,16},{16,0},{1,17},{17,1},{2,18},{18,2},{3,19},{19,3},{4,20},{20... | collective-permute-start | bytes 786440 | tf_op jit(solution)/shard_map/ppermute | solution.py:21
  7.5 0.2 collective-permute-done
  7.7 0.1 collective-permute-start.6
  7.8 2.6 %collective-permute-start.3 = (bf16[2,2,32,256]{3,2,1,0:T(8,128)(2,1)S(1)}, bf16[2,2,32,256]{3,2,1,0:T(8,128)(2,1)S(1)}, u32[]{:S(2)}, u32[]{:S(2)}) collective-permute-start(bf16[2,2,32,256]{3,2,1,0:T(8,128)(2,1)S(1)} %pad_maximum_fusion.refs_1_), channel_id=1, source_target_pairs={{0,6},{1,7},{2,4},{3,5},{4,2},{5,3},{6,0},{7,1},{8,14},{9,15},{10,... | collective-permute-start | bytes 196616 | tf_op jit(solution)/shard_map/ppermute | solution.py:21
  10.3 0.7 %collective-permute-start.2 = (bf16[2,2,32,256]{3,2,1,0:T(8,128)(2,1)S(1)}, bf16[2,2,32,256]{3,2,1,0:T(8,128)(2,1)S(1)}, u32[]{:S(2)}, u32[]{:S(2)}) collective-permute-start(bf16[2,2,32,256]{3,2,1,0:T(8,128)(2,1)S(1)} %pad_maximum_fusion.refs_1_), channel_id=1, source_target_pairs={{0,4},{1,5},{2,6},{3,7},{4,0},{5,1},{6,2},{7,3},{8,12},{9,13},{10,... | collective-permute-start | bytes 196616 | tf_op jit(solution)/shard_map/ppermute | solution.py:21
  11.0 0.0 collective-permute-done.6.refs_1_
  11.0 0.3 collective-permute-start.1
  11.3 2.0 %collective-permute-done.3.refs_4_ = bf16[2,2,32,256]{3,2,1,0:T(8,128)(2,1)S(1)} collective-permute-done((bf16[2,2,32,256]{3,2,1,0:T(8,128)(2,1)S(1)}, bf16[2,2,32,256]{3,2,1,0:T(8,128)(2,1)S(1)}, u32[]{:S(2)}, u32[]{:S(2)}) %collective-permute-start.3) | collective-permute-done | bytes 65568 | tf_op jit(solution)/shard_map/ppermute | solution.py:21
  13.3 0.0 collective-permute-start.9
  13.3 1.5 %collective-permute-done.2.refs_3_ = bf16[2,2,32,256]{3,2,1,0:T(8,128)(2,1)S(1)} collective-permute-done((bf16[2,2,32,256]{3,2,1,0:T(8,128)(2,1)S(1)}, bf16[2,2,32,256]{3,2,1,0:T(8,128)(2,1)S(1)}, u32[]{:S(2)}, u32[]{:S(2)}) %collective-permute-start.2) | collective-permute-done | bytes 65568 | tf_op jit(solution)/shard_map/ppermute | solution.py:21
  14.8 0.0 collective-permute-start.8
  14.8 0.5 %collective-permute-done.1.refs_2_ = bf16[2,2,32,256]{3,2,1,0:T(8,128)(2,1)S(1)} collective-permute-done((bf16[2,2,32,256]{3,2,1,0:T(8,128)(2,1)S(1)}, bf16[2,2,32,256]{3,2,1,0:T(8,128)(2,1)S(1)}, u32[]{:S(2)}, u32[]{:S(2)}) %collective-permute-start.1) | collective-permute-done | bytes 65568 | tf_op jit(solution)/shard_map/ppermute | solution.py:21
  15.3 0.1 collective-permute-start.7
  15.3 0.0 copy-done.3
  15.3 0.0 copy-start
  15.3 0.9 %copy-done = bf16[512,256]{1,0:T(8,128)(2,1)S(1)} copy-done((bf16[512,256]{1,0:T(8,128)(2,1)S(1)}, bf16[512,256]{1,0:T(8,128)(2,1)}, u32[]{:S(2)}) %copy-start) | copy-done | bytes 262168
  16.3 0.0 copy-start.2
  16.3 0.9 %copy-done.2 = bf16[512,256]{1,0:T(8,128)(2,1)S(1)} copy-done((bf16[512,256]{1,0:T(8,128)(2,1)S(1)}, bf16[512,256]{1,0:T(8,128)(2,1)}, u32[]{:S(2)}) %copy-start.2) | copy-done | bytes 262168
  17.2 0.0 copy-start.1
  17.2 1.4 %shard_map.68 = (f32[4,2,32,256]{3,2,1,0:T(8,128)S(1)}, f32[1,512,256]{2,1,0:T(8,128)S(1)}) custom-call(s32[4,8]{1,0:T(4,128)S(1)} %copy-done.3, bf16[2,2,32,256]{3,2,1,0:T(8,128)(2,1)S(1)} %pad_maximum_fusion.refs_1_, bf16[2,2,32,256]{3,2,1,0:T(8,128)(2,1)S(1)} %collective-permute-done.1.refs_2_, ...), custom_call_target="tpu_custom_call" | custom-call | tf_op jit(solution)/shard_map/pallas_call | solution.py:126
  18.7 0.0 collective-permute-done.9.refs_4_
  18.7 0.0 collective-permute-done.8.refs_3_
  18.7 0.0 collective-permute-done.7.refs_2_
  18.7 0.0 copy-done.1
  18.7 1.4 %shard_map.69 = (f32[4,2,32,256]{3,2,1,0:T(8,128)S(1)}, f32[1,512,256]{2,1,0:T(8,128)S(1)}) custom-call(s32[4,8]{1,0:T(4,128)S(1)} %copy-done.3, bf16[2,2,32,256]{3,2,1,0:T(8,128)(2,1)S(1)} %collective-permute-done.6.refs_1_, bf16[2,2,32,256]{3,2,1,0:T(8,128)(2,1)S(1)} %collective-permute-done.7.refs_2_, ...), custom_call_target="tpu_custom_call", output_to_operand_aliasing={{1}: (7, {})} | custom-call | tf_op jit(solution)/shard_map/pallas_call | solution.py:126
  20.1 0.0 collective-permute-done.4.refs_5_
  20.1 0.0 collective-permute-done.5.refs_6_
  20.2 1.4 %shard_map.70 = (f32[4,2,32,256]{3,2,1,0:T(8,128)S(1)}, f32[1,512,256]{2,1,0:T(8,128)S(1)}) custom-call(s32[4,8]{1,0:T(4,128)S(1)} %copy-done.3, bf16[2,2,32,256]{3,2,1,0:T(8,128)(2,1)S(1)} %collective-permute-done.6.refs_1_, bf16[2,2,32,256]{3,2,1,0:T(8,128)(2,1)S(1)} %collective-permute-done.7.refs_2_, ...), custom_call_target="tpu_custom_call", output_to_operand_aliasing={{0}: (7, {})} | custom-call | tf_op jit(solution)/shard_map/pallas_call | solution.py:126
  21.6 0.5 %collective-permute-start.10 = (f32[4,2,32,256]{3,2,1,0:T(8,128)S(1)}, f32[4,2,32,256]{3,2,1,0:T(8,128)S(1)}, u32[]{:S(2)}, u32[]{:S(2)}) collective-permute-start(f32[4,2,32,256]{3,2,1,0:T(8,128)S(1)} %get-tuple-element.15), channel_id=1, source_target_pairs={{0,1},{1,0},{2,3},{3,2},{4,5},{5,4},{6,7},{7,6},{8,9},{9,8},{10,11... | collective-permute-start | bytes 786440 | tf_op jit(solution)/shard_map/ppermute | solution.py:21
  22.1 1.4 %shard_map.71 = (f32[4,2,32,256]{3,2,1,0:T(8,128)S(1)}, f32[1,512,256]{2,1,0:T(8,128)S(1)}) custom-call(s32[4,8]{1,0:T(4,128)S(1)} %copy-done.3, bf16[2,2,32,256]{3,2,1,0:T(8,128)(2,1)S(1)} %pad_maximum_fusion.refs_1_, bf16[2,2,32,256]{3,2,1,0:T(8,128)(2,1)S(1)} %collective-permute-done.1.refs_2_, ...), custom_call_target="tpu_custom_call", output_to_operand_aliasing={{0}: (7, {}), {1}: (8, {})} | custom-call | tf_op jit(solution)/shard_map/pallas_call | solution.py:126
  23.6 0.0 collective-permute-done.10
  23.6 1.1 %collective-permute-start.11 = (f32[2,32,256]{2,1,0:T(8,128)S(1)}, f32[2,32,256]{2,1,0:T(8,128)S(1)}, u32[]{:S(2)}, u32[]{:S(2)}) collective-permute-start(f32[2,32,256]{2,1,0:T(8,128)S(1)} %get-tuple-element.18), channel_id=1, source_target_pairs={{0,2},{1,3},{2,0},{3,1},{4,6},{5,7},{6,4},{7,5},{8,10},{9,11},{10,... | collective-permute-start | bytes 196616 | tf_op jit(solution)/shard_map/ppermute | solution.py:21
  24.7 1.8 %collective-permute-start.13 = (f32[2,32,256]{2,1,0:T(8,128)S(1)}, f32[2,32,256]{2,1,0:T(8,128)S(1)}, u32[]{:S(2)}, u32[]{:S(2)}) collective-permute-start(f32[2,32,256]{2,1,0:T(8,128)S(1)} %get-tuple-element.19), channel_id=1, source_target_pairs={{0,6},{1,7},{2,4},{3,5},{4,2},{5,3},{6,0},{7,1},{8,14},{9,15},{10,... | collective-permute-start | bytes 196616 | tf_op jit(solution)/shard_map/ppermute | solution.py:21
  26.5 0.7 %collective-permute-start.12 = (f32[2,32,256]{2,1,0:T(8,128)S(1)}, f32[2,32,256]{2,1,0:T(8,128)S(1)}, u32[]{:S(2)}, u32[]{:S(2)}) collective-permute-start(f32[2,32,256]{2,1,0:T(8,128)S(1)} %get-tuple-element.20), channel_id=1, source_target_pairs={{0,4},{1,5},{2,6},{3,7},{4,0},{5,1},{6,2},{7,3},{8,12},{9,13},{10,... | collective-permute-start | bytes 196616 | tf_op jit(solution)/shard_map/ppermute | solution.py:21
  27.2 1.5 %collective-permute-start.15 = (f32[1,512,256]{2,1,0:T(8,128)S(1)}, f32[1,512,256]{2,1,0:T(8,128)S(1)}, u32[]{:S(2)}, u32[]{:S(2)}) collective-permute-start(f32[1,512,256]{2,1,0:T(8,128)S(1)} %get-tuple-element.17), channel_id=1, source_target_pairs={{0,16},{16,0},{1,17},{17,1},{2,18},{18,2},{3,19},{19,3},{4,20},{20... | collective-permute-start | bytes 1572872 | tf_op jit(solution)/shard_map/ppermute | solution.py:21
  28.7 0.0 collective-permute-done.11
  28.7 1.7 %collective-permute-done.13 = f32[2,32,256]{2,1,0:T(8,128)S(1)} collective-permute-done((f32[2,32,256]{2,1,0:T(8,128)S(1)}, f32[2,32,256]{2,1,0:T(8,128)S(1)}, u32[]{:S(2)}, u32[]{:S(2)}) %collective-permute-start.13) | collective-permute-done | bytes 65568 | tf_op jit(solution)/shard_map/ppermute | solution.py:21
  30.5 0.3 collective-permute-done.12
  30.8 2.9 %collective-permute-start.14 = (f32[1,32,256]{2,1,0:T(8,128)S(1)}, f32[1,32,256]{2,1,0:T(8,128)S(1)}, u32[]{:S(2)}, u32[]{:S(2)}) collective-permute-start(f32[1,32,256]{2,1,0:T(8,128)S(1)} %slice.29), channel_id=1, source_target_pairs={{0,8},{1,9},{2,10},{3,11},{4,12},{5,13},{6,14},{7,15},{8,0},{9,1},... | collective-permute-start | bytes 98312 | tf_op jit(solution)/shard_map/ppermute | solution.py:21
  33.7 2.0 %collective-permute-done.14 = f32[1,32,256]{2,1,0:T(8,128)S(1)} collective-permute-done((f32[1,32,256]{2,1,0:T(8,128)S(1)}, f32[1,32,256]{2,1,0:T(8,128)S(1)}, u32[]{:S(2)}, u32[]{:S(2)}) %collective-permute-start.14) | collective-permute-done | bytes 32800 | tf_op jit(solution)/shard_map/ppermute | solution.py:21
  35.7 0.6 %fusion.3 = f32[32,256]{1,0:T(8,128)} fusion(f32[1,32,256]{2,1,0:T(8,128)S(1)} %collective-permute-done.14, f32[2,32,256]{2,1,0:T(8,128)S(1)} %fusion.2), kind=kLoop, calls=%fused_computation.10 | loop fusion | flops 8192 | bytes 98304 | tf_op jit(solution)/shard_map/reshape | solution.py:212
  36.3 3.9 %collective-permute-done.15 = f32[1,512,256]{2,1,0:T(8,128)S(1)} collective-permute-done((f32[1,512,256]{2,1,0:T(8,128)S(1)}, f32[1,512,256]{2,1,0:T(8,128)S(1)}, u32[]{:S(2)}, u32[]{:S(2)}) %collective-permute-start.15) | collective-permute-done | bytes 524320 | tf_op jit(solution)/shard_map/ppermute | solution.py:21
  40.3 0.9 %add_bitcast_fusion = f32[512,256]{1,0:T(8,128)} fusion(f32[1,512,256]{2,1,0:T(8,128)S(1)} %get-tuple-element.16, f32[1,512,256]{2,1,0:T(8,128)S(1)} %collective-permute-done.15), kind=kLoop, calls=%fused_computation | loop fusion | flops 131072 | bytes 1572864 | tf_op jit(solution)/shard_map/squeeze | solution.py:203
  (5 shorter events, 0.1 us)
Async XLA Ops:
  1.4 6.3 %collective-permute-start = (bf16[1,2,32,256]{3,2,1,0:T(8,128)(2,1)S(1)}, bf16[1,2,32,256]{3,2,1,0:T(8,128)(2,1)S(1)}, u32[]{:S(2)}, u32[]{:S(2)}) collective-permute-start(bf16[1,2,32,256]{3,2,1,0:T(8,128)(2,1)S(1)} %maximum_bitcast_fusion), channel_id=1, source_target_pairs={{0,8},{1,9},{2,10},{3,11},{4,12},{5,13},{6,14},{7,15},{8,0},{9,1},... | collective-permute-start | bytes 98312 | tf_op jit(solution)/shard_map/ppermute | solution.py:21
  5.4 14.7 %collective-permute-start.4 = (bf16[1,512,256]{2,1,0:T(8,128)(2,1)}, bf16[1,512,256]{2,1,0:T(8,128)(2,1)S(1)}, u32[]{:S(2)}, u32[]{:S(2)}) collective-permute-start(bf16[1,512,256]{2,1,0:T(8,128)(2,1)} %bitcast.24), channel_id=1, source_target_pairs={{0,16},{16,0},{1,17},{17,1},{2,18},{18,2},{3,19},{19,3},{4,20},{20... | collective-permute-start | bytes 786440 | tf_op jit(solution)/shard_map/ppermute | solution.py:21
  7.0 8.4 %copy-start.3 = (s32[4,8]{1,0:T(4,128)S(1)}, s32[4,8]{1,0:T(4,128)}, u32[]{:S(2)}) copy-start(s32[4,8]{1,0:T(4,128)} %refs_0_.7) | copy-start | bytes 388
  7.0 13.2 %collective-permute-start.5 = (bf16[1,512,256]{2,1,0:T(8,128)(2,1)}, bf16[1,512,256]{2,1,0:T(8,128)(2,1)S(1)}, u32[]{:S(2)}, u32[]{:S(2)}) collective-permute-start(bf16[1,512,256]{2,1,0:T(8,128)(2,1)} %bitcast.27), channel_id=1, source_target_pairs={{0,16},{16,0},{1,17},{17,1},{2,18},{18,2},{3,19},{19,3},{4,20},{20... | collective-permute-start | bytes 786440 | tf_op jit(solution)/shard_map/ppermute | solution.py:21
  7.7 3.3 %collective-permute-start.6 = (bf16[2,2,32,256]{3,2,1,0:T(8,128)(2,1)S(1)}, bf16[2,2,32,256]{3,2,1,0:T(8,128)(2,1)S(1)}, u32[]{:S(2)}, u32[]{:S(2)}) collective-permute-start(bf16[2,2,32,256]{3,2,1,0:T(8,128)(2,1)S(1)} %pad_maximum_fusion.refs_1_), channel_id=1, source_target_pairs={{0,1},{1,0},{2,3},{3,2},{4,5},{5,4},{6,7},{7,6},{8,9},{9,8},{10,11... | collective-permute-start | bytes 196616 | tf_op jit(solution)/shard_map/ppermute | solution.py:21
  7.8 5.5 %collective-permute-start.3 = (bf16[2,2,32,256]{3,2,1,0:T(8,128)(2,1)S(1)}, bf16[2,2,32,256]{3,2,1,0:T(8,128)(2,1)S(1)}, u32[]{:S(2)}, u32[]{:S(2)}) collective-permute-start(bf16[2,2,32,256]{3,2,1,0:T(8,128)(2,1)S(1)} %pad_maximum_fusion.refs_1_), channel_id=1, source_target_pairs={{0,6},{1,7},{2,4},{3,5},{4,2},{5,3},{6,0},{7,1},{8,14},{9,15},{10,... | collective-permute-start | bytes 196616 | tf_op jit(solution)/shard_map/ppermute | solution.py:21
  10.3 4.5 %collective-permute-start.2 = (bf16[2,2,32,256]{3,2,1,0:T(8,128)(2,1)S(1)}, bf16[2,2,32,256]{3,2,1,0:T(8,128)(2,1)S(1)}, u32[]{:S(2)}, u32[]{:S(2)}) collective-permute-start(bf16[2,2,32,256]{3,2,1,0:T(8,128)(2,1)S(1)} %pad_maximum_fusion.refs_1_), channel_id=1, source_target_pairs={{0,4},{1,5},{2,6},{3,7},{4,0},{5,1},{6,2},{7,3},{8,12},{9,13},{10,... | collective-permute-start | bytes 196616 | tf_op jit(solution)/shard_map/ppermute | solution.py:21
  11.0 4.3 %collective-permute-start.1 = (bf16[2,2,32,256]{3,2,1,0:T(8,128)(2,1)S(1)}, bf16[2,2,32,256]{3,2,1,0:T(8,128)(2,1)S(1)}, u32[]{:S(2)}, u32[]{:S(2)}) collective-permute-start(bf16[2,2,32,256]{3,2,1,0:T(8,128)(2,1)S(1)} %pad_maximum_fusion.refs_1_), channel_id=1, source_target_pairs={{0,2},{1,3},{2,0},{3,1},{4,6},{5,7},{6,4},{7,5},{8,10},{9,11},{10,... | collective-permute-start | bytes 196616 | tf_op jit(solution)/shard_map/ppermute | solution.py:21
  13.3 5.4 %collective-permute-start.9 = (bf16[2,2,32,256]{3,2,1,0:T(8,128)(2,1)S(1)}, bf16[2,2,32,256]{3,2,1,0:T(8,128)(2,1)S(1)}, u32[]{:S(2)}, u32[]{:S(2)}) collective-permute-start(bf16[2,2,32,256]{3,2,1,0:T(8,128)(2,1)S(1)} %collective-permute-done.3.refs_4_), channel_id=1, source_target_pairs={{0,1},{1,0},{2,3},{3,2},{4,5},{5,4},{6,7},{7,6},{8,9},{9,8},{10,11... | collective-permute-start | bytes 196616 | tf_op jit(solution)/shard_map/ppermute | solution.py:21
  14.8 3.9 %collective-permute-start.8 = (bf16[2,2,32,256]{3,2,1,0:T(8,128)(2,1)S(1)}, bf16[2,2,32,256]{3,2,1,0:T(8,128)(2,1)S(1)}, u32[]{:S(2)}, u32[]{:S(2)}) collective-permute-start(bf16[2,2,32,256]{3,2,1,0:T(8,128)(2,1)S(1)} %collective-permute-done.2.refs_3_), channel_id=1, source_target_pairs={{0,1},{1,0},{2,3},{3,2},{4,5},{5,4},{6,7},{7,6},{8,9},{9,8},{10,11... | collective-permute-start | bytes 196616 | tf_op jit(solution)/shard_map/ppermute | solution.py:21
  15.3 3.4 %collective-permute-start.7 = (bf16[2,2,32,256]{3,2,1,0:T(8,128)(2,1)S(1)}, bf16[2,2,32,256]{3,2,1,0:T(8,128)(2,1)S(1)}, u32[]{:S(2)}, u32[]{:S(2)}) collective-permute-start(bf16[2,2,32,256]{3,2,1,0:T(8,128)(2,1)S(1)} %collective-permute-done.1.refs_2_), channel_id=1, source_target_pairs={{0,1},{1,0},{2,3},{3,2},{4,5},{5,4},{6,7},{7,6},{8,9},{9,8},{10,11... | collective-permute-start | bytes 196616 | tf_op jit(solution)/shard_map/ppermute | solution.py:21
  15.3 1.0 %copy-start = (bf16[512,256]{1,0:T(8,128)(2,1)S(1)}, bf16[512,256]{1,0:T(8,128)(2,1)}, u32[]{:S(2)}) copy-start(bf16[512,256]{1,0:T(8,128)(2,1)} %param.6) | copy-start | bytes 786436
  16.3 0.9 %copy-start.2 = (bf16[512,256]{1,0:T(8,128)(2,1)S(1)}, bf16[512,256]{1,0:T(8,128)(2,1)}, u32[]{:S(2)}) copy-start(bf16[512,256]{1,0:T(8,128)(2,1)} %param.8) | copy-start | bytes 786436
  17.2 1.5 %copy-start.1 = (bf16[512,256]{1,0:T(8,128)(2,1)S(1)}, bf16[512,256]{1,0:T(8,128)(2,1)}, u32[]{:S(2)}) copy-start(bf16[512,256]{1,0:T(8,128)(2,1)} %param.6) | copy-start | bytes 786436
  21.6 2.0 %collective-permute-start.10 = (f32[4,2,32,256]{3,2,1,0:T(8,128)S(1)}, f32[4,2,32,256]{3,2,1,0:T(8,128)S(1)}, u32[]{:S(2)}, u32[]{:S(2)}) collective-permute-start(f32[4,2,32,256]{3,2,1,0:T(8,128)S(1)} %get-tuple-element.15), channel_id=1, source_target_pairs={{0,1},{1,0},{2,3},{3,2},{4,5},{5,4},{6,7},{7,6},{8,9},{9,8},{10,11... | collective-permute-start | bytes 786440 | tf_op jit(solution)/shard_map/ppermute | solution.py:21
  23.6 5.1 %collective-permute-start.11 = (f32[2,32,256]{2,1,0:T(8,128)S(1)}, f32[2,32,256]{2,1,0:T(8,128)S(1)}, u32[]{:S(2)}, u32[]{:S(2)}) collective-permute-start(f32[2,32,256]{2,1,0:T(8,128)S(1)} %get-tuple-element.18), channel_id=1, source_target_pairs={{0,2},{1,3},{2,0},{3,1},{4,6},{5,7},{6,4},{7,5},{8,10},{9,11},{10,... | collective-permute-start | bytes 196616 | tf_op jit(solution)/shard_map/ppermute | solution.py:21
  24.7 5.8 %collective-permute-start.13 = (f32[2,32,256]{2,1,0:T(8,128)S(1)}, f32[2,32,256]{2,1,0:T(8,128)S(1)}, u32[]{:S(2)}, u32[]{:S(2)}) collective-permute-start(f32[2,32,256]{2,1,0:T(8,128)S(1)} %get-tuple-element.19), channel_id=1, source_target_pairs={{0,6},{1,7},{2,4},{3,5},{4,2},{5,3},{6,0},{7,1},{8,14},{9,15},{10,... | collective-permute-start | bytes 196616 | tf_op jit(solution)/shard_map/ppermute | solution.py:21
  26.5 4.3 %collective-permute-start.12 = (f32[2,32,256]{2,1,0:T(8,128)S(1)}, f32[2,32,256]{2,1,0:T(8,128)S(1)}, u32[]{:S(2)}, u32[]{:S(2)}) collective-permute-start(f32[2,32,256]{2,1,0:T(8,128)S(1)} %get-tuple-element.20), channel_id=1, source_target_pairs={{0,4},{1,5},{2,6},{3,7},{4,0},{5,1},{6,2},{7,3},{8,12},{9,13},{10,... | collective-permute-start | bytes 196616 | tf_op jit(solution)/shard_map/ppermute | solution.py:21
  27.2 13.1 %collective-permute-start.15 = (f32[1,512,256]{2,1,0:T(8,128)S(1)}, f32[1,512,256]{2,1,0:T(8,128)S(1)}, u32[]{:S(2)}, u32[]{:S(2)}) collective-permute-start(f32[1,512,256]{2,1,0:T(8,128)S(1)} %get-tuple-element.17), channel_id=1, source_target_pairs={{0,16},{16,0},{1,17},{17,1},{2,18},{18,2},{3,19},{19,3},{4,20},{20... | collective-permute-start | bytes 1572872 | tf_op jit(solution)/shard_map/ppermute | solution.py:21
  30.8 4.9 %collective-permute-start.14 = (f32[1,32,256]{2,1,0:T(8,128)S(1)}, f32[1,32,256]{2,1,0:T(8,128)S(1)}, u32[]{:S(2)}, u32[]{:S(2)}) collective-permute-start(f32[1,32,256]{2,1,0:T(8,128)S(1)} %slice.29), channel_id=1, source_target_pairs={{0,8},{1,9},{2,10},{3,11},{4,12},{5,13},{6,14},{7,15},{8,0},{9,1},... | collective-permute-start | bytes 98312 | tf_op jit(solution)/shard_map/ppermute | solution.py:21

commit v3 on v2

--- a/solution.py
+++ b/solution.py
@@ -43,11 +43,12 @@
     at = 1 + n_users
     fac_i, tan_i = refs[at : at + 2]
     at += 2
-    user_in = refs[at] if add_user else None
-    at += add_user
+    user_in = refs[at : at + n_users] if add_user else None
+    at += n_users * add_user
     item_in = refs[at] if add_item else None
     at += add_item
-    user_out, item_out, u_all, c_all = refs[at:]
+    user_out = refs[at : at + n_users]
+    item_out, u_all, c_all = refs[at + n_users :]
 
     n_a, _, us, _ = users[0].shape
     n_pieces, it_dev, _ = fac_i.shape
@@ -73,8 +74,13 @@
                 items = pl.ds(ib * sub, sub)
                 v = fac_i[k, items, :]
                 dv = tan_i[k, items, :]
-                s = dot(v, fac, NT)
-                tt = dot(v, tan, NT) + dot(dv, fac, NT)
+                if 2 * tile <= TILE:
+                    both = dot(v, jnp.concatenate([fac, tan], 0), NT)
+                    s = both[:, :tile]
+                    tt = both[:, tile:] + dot(dv, fac, NT)
+                else:
+                    s = dot(v, fac, NT)
+                    tt = dot(v, tan, NT) + dot(dv, fac, NT)
                 seen = []
                 for i in range(sub // block):
                     col = (me_col ^ cols_of[1][k]) * (it_dev // block) + ib * (sub // block) + i
@@ -102,48 +108,114 @@
             b, k = divmod(t * in_tile + j, n_a)
             r = total[j * us : (j + 1) * us]
             if user_in is not None:
-                r = r + user_in[b, k]
-            user_out[b, k] = r
+                r = r + user_in[b][k]
+            user_out[b][k] = r
 
 
 def in_vmem(x):
     return pltpu.with_memory_space_constraint(x, pltpu.VMEM)
 
 
-def region(mask, users, items, user_sum, item_sum, **static):
-    vm = pl.BlockSpec(memory_space=pltpu.VMEM)
+VM = pl.BlockSpec(memory_space=pltpu.VMEM)
+PARAMS = pltpu.CompilerParams(vmem_limit_bytes=16 * 2**20)
+
+
+def region(mask, users, items, user_sums, item_sum, **static):
     n_a, _, us, width = users[0].shape
     n_pieces, it_dev, _ = items[0].shape
     given = [in_vmem(x) for x in (*users, *items)]
     aliases = {}
-    if user_sum is not None:
-        aliases[1 + len(given)] = 0
-        given.append(in_vmem(user_sum))
+    add_user = user_sums[0] is not None
+    if add_user:
+        for n, x in enumerate(user_sums):
+            aliases[1 + len(given)] = n
+            given.append(in_vmem(x))
     if item_sum is not None:
-        aliases[1 + len(given)] = 1
+        aliases[1 + len(given)] = len(users)
         given.append(in_vmem(item_sum))
     total_rows = len(users) * n_a * us
+    *user_sums, item_sum = pl.pallas_call(
+        functools.partial(
+            region_kernel, n_users=len(users), add_user=add_user, add_item=item_sum is not None, **static
+        ),
+        in_specs=[pl.BlockSpec(memory_space=pltpu.SMEM)] + [VM] * len(given),
+        out_specs=[VM] * (len(users) + 1),
+        out_shape=[pltpu.VMEM((n_a, us, width), f32)] * len(users)
+        + [pltpu.VMEM((n_pieces, it_dev, width), f32)],
+        input_output_aliases=aliases,
+        scratch_shapes=[pltpu.VMEM((2, total_rows, width), bf16), pltpu.VMEM((it_dev, min(TILE, total_rows)), bf16)],
+        compiler_params=PARAMS,
+    )(mask, *given)
+    return user_sums, item_sum
+
+
+def load_kernel(*refs):
+    n = (len(refs) - 1) // 2
+    sems = refs[-1]
+    copies = [pltpu.make_async_copy(refs[i], refs[n + i], sems.at[i]) for i in range(n)]
+    for c in copies:
+        c.start()
+    for c in copies:
+        c.wait()
+
+
+def load(arrays):
     return pl.pallas_call(
-        functools.partial(
-            region_kernel,
-            n_users=len(users),
-            add_user=user_sum is not None,
-            add_item=item_sum is not None,
-            **static,
-        ),
-        in_specs=[pl.BlockSpec(memory_space=pltpu.SMEM)] + [vm] * len(given),
-        out_specs=[vm, vm],
-        out_shape=[
-            pltpu.VMEM((len(users), n_a, us, width), f32),
-            pltpu.VMEM((n_pieces, it_dev, width), f32),
-        ],
-        input_output_aliases=aliases,
-        scratch_shapes=[
-            pltpu.VMEM((2, total_rows, width), bf16),
-            pltpu.VMEM((it_dev, min(TILE, total_rows)), bf16),
-        ],
-        compiler_params=pltpu.CompilerParams(vmem_limit_bytes=16 * 2**20),
-    )(mask, *given)
+        load_kernel,
+        in_specs=[pl.BlockSpec(memory_space=pl.ANY)] * len(arrays),
+        out_specs=[VM] * len(arrays),
+        out_shape=[pltpu.VMEM(x.shape, x.dtype) for x in arrays],
+        scratch_shapes=[pltpu.SemaphoreType.DMA((len(arrays),))],
+        compiler_params=PARAMS,
+    )(*[pltpu.with_memory_space_constraint(x, pltpu.HBM) for x in arrays])
+
+
+GROUPS = 16
+
+
+def encode_kernel(x_ref, out_ref):
+    n, rows, _ = x_ref.shape
+    step = rows // GROUPS
+    for k in range(n):
+        exps = []
+        for g in range(GROUPS):
+            x = x_ref[k, pl.ds(g * step, step), :]
+            top = jnp.max(jnp.abs(x), 0, keepdims=True)
+            e = 14.0 - jnp.ceil(jnp.log2(jnp.maximum(top, 1e-30)))
+            out_ref[k, pl.ds(g * step, step), :] = jnp.round(x * jnp.exp2(e)).astype(jnp.int32).astype(jnp.int16)
+            exps.append(e)
+        out_ref[k, pl.ds(rows, GROUPS), :] = jnp.concatenate(exps, 0).astype(jnp.int32).astype(jnp.int16)
+
+
+def encode(x):
+    n, rows, width = x.shape
+    return pl.pallas_call(
+        encode_kernel,
+        in_specs=[VM],
+        out_specs=VM,
+        out_shape=pltpu.VMEM((n, rows + GROUPS, width), jnp.int16),
+        compiler_params=PARAMS,
+    )(in_vmem(x))
+
+
+def decode_kernel(x_ref, q_ref, out_ref, *, at):
+    n, rows, _ = x_ref.shape
+    step = rows // GROUPS
+    for k in range(n):
+        unit = jnp.exp2(-q_ref[at + k, pl.ds(rows, GROUPS), :].astype(jnp.int32).astype(f32))
+        for g in range(GROUPS):
+            part = pl.ds(g * step, step)
+            out_ref[k, part, :] = x_ref[k, part, :] + q_ref[at + k, part, :].astype(jnp.int32).astype(f32) * unit[g : g + 1]
+
+
+def add_decoded(x, q, at):
+    return pl.pallas_call(
+        functools.partial(decode_kernel, at=at),
+        in_specs=[VM, VM],
+        out_specs=VM,
+        out_shape=jax.ShapeDtypeStruct(x.shape, f32),
+        compiler_params=PARAMS,
+    )(in_vmem(x), in_vmem(q))
 
 
 def on_device(user_factors, item_factors, user_tangent, item_tangent, block_mask, n_au, n_ia):
@@ -151,28 +223,30 @@
     row_blocks, _ = block_mask.shape
     block = us * n_ia // row_blocks
     members = block // us
+    assert members == 4
     scale = 1.0 / math.sqrt(width)
-    core, near = 1, [2, 4, 6]
-    a_bits = bits_of(8, n_ia)
+    core, near = 1, 2
+    a_bits = bits_of(members, n_ia)
+    rel_a = relative(a_bits)
+    row_of = [r // members for r in rel_a]
+
+    far = jnp.stack([user_factors, user_tangent])[None]
+    for n, bit in enumerate(a_bits):
+        far = jnp.concatenate([far, swap(far, "ia", n_ia, bit)], 0)
 
     item_bits = bits_of(1, n_au)
+    rel_items = relative(item_bits)
     facs, tans = [item_factors[None]], [item_tangent[None]]
     for n, bit in enumerate(item_bits):
         held_f = facs[0] if n == 0 else jnp.concatenate(facs, 0)
         held_t = tans[0] if n == 0 else jnp.concatenate(tans, 0)
         facs.append(swap(held_f, "au", n_au, bit))
         tans.append(swap(held_t, "au", n_au, bit))
-    rel_items = relative(item_bits)
-
-    far = jnp.stack([user_factors, user_tangent])[None]
-    for n, bit in enumerate(a_bits):
-        far = jnp.concatenate([far, swap(far, "ia", n_ia, bit)], 0)
-    rel_a = relative(a_bits)
-    mine = [far] + [swap(far, "ia", n_ia, b) for b in near]
-    other = [swap(x, "ia", n_ia, core) for x in mine]
-    rows_of = (members, [(b ^ r) // members for b in [0, *near] for r in rel_a])
-
-    sums = {0: None, 1: None}
+    facs[0], tans[0] = load((facs[0], tans[0]))
+
+    pieces = [far, swap(far, "ia", n_ia, core), swap(far, "ia", n_ia, near)]
+    pieces.append(swap(pieces[2], "ia", n_ia, core))
+    user_sums = [None] * 4
     item_sums = []
     at = 0
     for g, (f, t) in enumerate(zip(facs, tans)):
@@ -180,33 +254,37 @@
         cols_of = (block, rel_items[at : at + n])
         at += n
         item_sum = None
-        last = g == len(facs) - 1
-        for half in (1, 0) if last else (0, 1):
-            sums[half], item_sum = region(
+        for which in [(0, 1), (2,), (3,)] if g == 0 else [(1, 3), (0, 2)]:
+            sums, item_sum = region(
                 block_mask,
-                other if half else mine,
+                [pieces[w] for w in which],
                 (f, t),
-                sums[half],
+                [user_sums[w] for w in which],
                 item_sum,
-                rows_of=rows_of,
+                rows_of=(members, row_of * len(which)),
                 cols_of=cols_of,
                 scale=scale,
             )
+            for w, x in zip(which, sums):
+                user_sums[w] = x
         item_sums.append(item_sum)
 
-    core_in = swap(sums[1], "ia", n_ia, core)
+    sent = [swap(user_sums[w], "ia", n_ia, core) for w in (1, 3)]
     for n, bit in enumerate(item_bits[::-1]):
-        back = swap(item_sums.pop(), "au", n_au, bit)
+        back = swap(encode(item_sums.pop()), "au", n_au, bit)
         sizes = [h.shape[0] for h in item_sums]
         cuts = [sum(sizes[:i]) for i in range(len(sizes))]
-        item_sums = [h + back[c : c + s] for h, c, s in zip(item_sums, cuts, sizes)]
+        item_sums = [add_decoded(h, back, c) for h, c in zip(item_sums, cuts)]
     item_product = item_sums[0][0]
 
-    keep = sums[0] + core_in
-    acc = keep[0]
-    for i, b in enumerate(near):
-        acc = acc + swap(keep[i + 1], "ia", n_ia, b)
-    for n, bit in enumerate(a_bits[::-1]):
+    keep = [user_sums[0] + sent[0], user_sums[2] + sent[1]]
+    half = len(rel_a) // 2
+    last = a_bits[-1]
+    acc = keep[0][:half]
+    acc = acc + swap(keep[1][:half], "ia", n_ia, near)
+    acc = acc + swap(keep[0][half:], "ia", n_ia, last)
+    acc = acc + swap(keep[1][half:], "ia", n_ia, near ^ last)
+    for n, bit in enumerate(a_bits[:-1][::-1]):
         half = acc.shape[0] // 2
         acc = acc[:half] + swap(acc[half:], "ia", n_ia, bit)
     user_product = acc.reshape(us, width)

time: 41.4 us -> 42.5 us (1.027)
  Pallas kernels: 5.72 us -> 8.82 us
  local copies, waits for them, and re-layouts: 1.93 us -> 0.69 us
  other arithmetic: 2.28 us -> 1.48 us
    pallas_call x0 -> x3, Pallas kernels: none -> 2.04 us  [the longest x1 1.05 us: load(): pl.pallas_call(load_kernel, in_specs=[pl.BlockSpec(memory_space=pl.ANY)]...]
    unnamed x8 -> x4, local copies, waits for them, and re-layouts: 1.91 us -> 0.67 us
    pallas_call x4 -> x5, Pallas kernels: 5.72 us -> 6.78 us  [region(): pl.pallas_call(functools.partial(region_kernel, n_users=len(users), add_u...]
    squeeze x1 -> x0, other arithmetic: 0.86 us -> none  [on_device(): item_product = item_sums[0][0]]
    ppermute x16 -> x14, waiting for transfers between devices: 12.2 us -> 12.4 us  [swap(): return lax.ppermute(x, axis, [(i, i ^ bits) for i in range(size)])]
    ppermute x16 -> x14, starting transfers between devices: 18.3 us -> 18 us  [swap(): return lax.ppermute(x, axis, [(i, i ^ bits) for i in range(size)])]
  transfers between devices with their start and end apart: 16 -> 14, of which waited for: 8 -> 7; matrix products, arithmetic and copies ran while one was open for 2% -> 2% of each run, Pallas kernels for 10% -> 15%
where the time goes in v3:
time: 42.5 us; the launch traced here: 42.3 us
  starting transfers between devices  18 us (42%)
  waiting for transfers between devices  12.4 us (29%)
  Pallas kernels  8.82 us (21%)
  other arithmetic  1.48 us (3%)
  between operations  0.78 us (2%)
  local copies, waits for them, and re-layouts  0.69 us (2%)
    ppermute x14, starting transfers between devices, swap(): return lax.ppermute(x, axis, [(i, i ^ bits) for i in range(size)])  18 us
    ppermute x14, waiting for transfers between devices, swap(): return lax.ppermute(x, axis, [(i, i ^ bits) for i in range(size)])  12.4 us
    pallas_call x5, Pallas kernels, region(): pl.pallas_call(functools.partial(region_kernel, n_users=len(users), add_u...  6.78 us
    pallas_call x1, Pallas kernels, load(): pl.pallas_call(load_kernel, in_specs=[pl.BlockSpec(memory_space=pl.ANY)]...  1.05 us
    pallas_call x1, Pallas kernels, add_decoded(): pl.pallas_call(functools.partial(decode_kernel, at=at), in_specs=[VM, VM]...  0.87 us
  transfers between devices with their start and end apart: 14, of which 7 were waited for; matrix products, arithmetic and copies ran while one was open for 2% of the time, Pallas kernels for 15%

profile of v3, /device:TPU:0, one launch (start us, length us, event | category | flops | bytes accessed | tf_op | source)
XLA Modules:
  0.0 42.3 jit_solution(9920322009738047569)
XLA Ops:
  0.6 0.0 copy-start.1
  0.6 0.8 %maximum_bitcast_fusion = bf16[1,2,32,256]{3,2,1,0:T(8,128)(2,1)S(1)} fusion(bf16[1,32,256]{2,1,0:T(8,128)(2,1)} %bitcast.14, bf16[1,32,256]{2,1,0:T(8,128)(2,1)} %bitcast.15), kind=kLoop, calls=%fused_computation.7 | loop fusion | flops 16384 | bytes 65536 | tf_op jit(solution)/shard_map/broadcast_in_dim | solution.py:233
  1.4 4.1 %collective-permute-start = (bf16[1,2,32,256]{3,2,1,0:T(8,128)(2,1)S(1)}, bf16[1,2,32,256]{3,2,1,0:T(8,128)(2,1)S(1)}, u32[]{:S(2)}, u32[]{:S(2)}) collective-permute-start(bf16[1,2,32,256]{3,2,1,0:T(8,128)(2,1)S(1)} %maximum_bitcast_fusion), channel_id=1, source_target_pairs={{0,8},{1,9},{2,10},{3,11},{4,12},{5,13},{6,14},{7,15},{8,0},{9,1},... | collective-permute-start | bytes 98312 | tf_op jit(solution)/shard_map/ppermute | solution.py:21
  5.5 2.2 %collective-permute-done = bf16[1,2,32,256]{3,2,1,0:T(8,128)(2,1)S(1)} collective-permute-done((bf16[1,2,32,256]{3,2,1,0:T(8,128)(2,1)S(1)}, bf16[1,2,32,256]{3,2,1,0:T(8,128)(2,1)S(1)}, u32[]{:S(2)}, u32[]{:S(2)}) %collective-permute-start) | collective-permute-done | bytes 32800 | tf_op jit(solution)/shard_map/ppermute | solution.py:21
  7.7 1.6 %collective-permute-start.1 = (bf16[2,2,32,256]{3,2,1,0:T(8,128)(2,1)S(1)}, bf16[2,2,32,256]{3,2,1,0:T(8,128)(2,1)S(1)}, u32[]{:S(2)}, u32[]{:S(2)}) collective-permute-start(bf16[2,2,32,256]{3,2,1,0:T(8,128)(2,1)S(1)} %pad_maximum_fusion.1), channel_id=1, source_target_pairs={{0,4},{1,5},{2,6},{3,7},{4,0},{5,1},{6,2},{7,3},{8,12},{9,13},{10,... | collective-permute-start | bytes 196616 | tf_op jit(solution)/shard_map/ppermute | solution.py:21
  9.4 2.7 %collective-permute-done.1 = bf16[2,2,32,256]{3,2,1,0:T(8,128)(2,1)S(1)} collective-permute-done((bf16[2,2,32,256]{3,2,1,0:T(8,128)(2,1)S(1)}, bf16[2,2,32,256]{3,2,1,0:T(8,128)(2,1)S(1)}, u32[]{:S(2)}, u32[]{:S(2)}) %collective-permute-start.1) | collective-permute-done | bytes 65568 | tf_op jit(solution)/shard_map/ppermute | solution.py:21
  12.1 1.8 %collective-permute-start.2 = (bf16[4,2,32,256]{3,2,1,0:T(8,128)(2,1)S(1)}, bf16[4,2,32,256]{3,2,1,0:T(8,128)(2,1)S(1)}, u32[]{:S(2)}, u32[]{:S(2)}) collective-permute-start(bf16[4,2,32,256]{3,2,1,0:T(8,128)(2,1)S(1)} %pad_maximum_fusion.refs_1_), channel_id=1, source_target_pairs={{0,2},{1,3},{2,0},{3,1},{4,6},{5,7},{6,4},{7,5},{8,10},{9,11},{10,... | collective-permute-start | bytes 393224 | tf_op jit(solution)/shard_map/ppermute | solution.py:21
  13.9 0.0 copy-done.1
  13.9 1.5 %collective-permute-start.3 = (bf16[1,512,256]{2,1,0:T(8,128)(2,1)S(1)}, bf16[1,512,256]{2,1,0:T(8,128)(2,1)S(1)}, u32[]{:S(2)}, u32[]{:S(2)}) collective-permute-start(bf16[1,512,256]{2,1,0:T(8,128)(2,1)S(1)} %bitcast.11), channel_id=1, source_target_pairs={{0,16},{16,0},{1,17},{17,1},{2,18},{18,2},{3,19},{19,3},{4,20},{20... | collective-permute-start | bytes 786440 | tf_op jit(solution)/shard_map/ppermute | solution.py:21
  15.4 0.5 %collective-permute-start.4 = (bf16[1,512,256]{2,1,0:T(8,128)(2,1)}, bf16[1,512,256]{2,1,0:T(8,128)(2,1)S(1)}, u32[]{:S(2)}, u32[]{:S(2)}) collective-permute-start(bf16[1,512,256]{2,1,0:T(8,128)(2,1)} %bitcast.12), channel_id=1, source_target_pairs={{0,16},{16,0},{1,17},{17,1},{2,18},{18,2},{3,19},{19,3},{4,20},{20... | collective-permute-start | bytes 786440 | tf_op jit(solution)/shard_map/ppermute | solution.py:21
  15.9 0.0 collective-permute-start.5
  15.9 1.2 %collective-permute-done.2.refs_1_.refs_2_ = bf16[4,2,32,256]{3,2,1,0:T(8,128)(2,1)S(1)} collective-permute-done((bf16[4,2,32,256]{3,2,1,0:T(8,128)(2,1)S(1)}, bf16[4,2,32,256]{3,2,1,0:T(8,128)(2,1)S(1)}, u32[]{:S(2)}, u32[]{:S(2)}) %collective-permute-start.2) | collective-permute-done | bytes 131104 | tf_op jit(solution)/shard_map/ppermute | solution.py:21
  17.1 0.0 collective-permute-start.6
  17.1 1.0 %shard_map.68 = (bf16[1,512,256]{2,1,0:T(8,128)(2,1)S(1)}, bf16[1,512,256]{2,1,0:T(8,128)(2,1)S(1)}) custom-call(bf16[1,512,256]{2,1,0:T(8,128)(2,1)} %bitcast.10, bf16[1,512,256]{2,1,0:T(8,128)(2,1)} %bitcast.13), custom_call_target="tpu_custom_call" | custom-call | tf_op jit(solution)/shard_map/pallas_call | solution.py:163
  18.2 0.0 copy-start
  18.2 0.0 collective-permute-done.5.refs_2_.refs_1_
  18.2 0.7 %copy-done = s32[4,8]{1,0:T(4,128)S(1)} copy-done((s32[4,8]{1,0:T(4,128)S(1)}, s32[4,8]{1,0:T(4,128)}, u32[]{:S(2)}) %copy-start) | copy-done | bytes 152
  18.9 1.4 %shard_map.69 = (f32[4,32,256]{2,1,0:T(8,128)S(1)}, f32[4,32,256]{2,1,0:T(8,128)S(1)}, f32[1,512,256]{2,1,0:T(8,128)S(1)}) custom-call(s32[4,8]{1,0:T(4,128)S(1)} %copy-done, bf16[4,2,32,256]{3,2,1,0:T(8,128)(2,1)S(1)} %pad_maximum_fusion.refs_1_, bf16[4,2,32,256]{3,2,1,0:T(8,128)(2,1)S(1)} %collective-permute-done.5.refs_2_.refs_1_, ...), custom_call_target="tpu_custom_call" | custom-call | tf_op jit(solution)/shard_map/pallas_call | solution.py:137
  20.3 1.3 %shard_map.70 = (f32[4,32,256]{2,1,0:T(8,128)S(1)}, f32[1,512,256]{2,1,0:T(8,128)S(1)}) custom-call(s32[4,8]{1,0:T(4,128)S(1)} %copy-done, bf16[4,2,32,256]{3,2,1,0:T(8,128)(2,1)S(1)} %collective-permute-done.2.refs_1_.refs_2_, bf16[1,512,256]{2,1,0:T(8,128)(2,1)S(1)} %get-tuple-element.17.refs_3_.refs_2_, ...), custom_call_target="tpu_custom_call", output_to_operand_aliasing={{1}: (4, {})} | custom-call | tf_op jit(solution)/shard_map/pallas_call | solution.py:137
  21.6 0.0 collective-permute-done.6.refs_1_.refs_2_
  21.6 1.2 %shard_map.71 = (f32[4,32,256]{2,1,0:T(8,128)S(1)}, f32[1,512,256]{2,1,0:T(8,128)S(1)}) custom-call(s32[4,8]{1,0:T(4,128)S(1)} %copy-done, bf16[4,2,32,256]{3,2,1,0:T(8,128)(2,1)S(1)} %collective-permute-done.6.refs_1_.refs_2_, bf16[1,512,256]{2,1,0:T(8,128)(2,1)S(1)} %get-tuple-element.17.refs_3_.refs_2_, ...), custom_call_target="tpu_custom_call", output_to_operand_aliasing={{1}: (4, {})} | custom-call | tf_op jit(solution)/shard_map/pallas_call | solution.py:137
  22.8 0.0 collective-permute-done.3.refs_3_
  22.8 1.9 %collective-permute-done.4.refs_4_ = bf16[1,512,256]{2,1,0:T(8,128)(2,1)S(1)} collective-permute-done((bf16[1,512,256]{2,1,0:T(8,128)(2,1)}, bf16[1,512,256]{2,1,0:T(8,128)(2,1)S(1)}, u32[]{:S(2)}, u32[]{:S(2)}) %collective-permute-start.4) | collective-permute-done | bytes 262176 | tf_op jit(solution)/shard_map/ppermute | solution.py:21
  24.7 1.4 %shard_map.72 = (f32[4,32,256]{2,1,0:T(8,128)S(1)}, f32[4,32,256]{2,1,0:T(8,128)S(1)}, f32[1,512,256]{2,1,0:T(8,128)S(1)}) custom-call(s32[4,8]{1,0:T(4,128)S(1)} %copy-done, bf16[4,2,32,256]{3,2,1,0:T(8,128)(2,1)S(1)} %collective-permute-done.5.refs_2_.refs_1_, ...), custom_call_target="tpu_custom_call", output_to_operand_aliasing={{0}: (5, {}), {1}: (6, {})} | custom-call | tf_op jit(solution)/shard_map/pallas_call | solution.py:137
  26.2 0.1 collective-permute-start.7
  26.2 0.5 %collective-permute-start.8 = (f32[4,32,256]{2,1,0:T(8,128)S(1)}, f32[4,32,256]{2,1,0:T(8,128)S(1)}, u32[]{:S(2)}, u32[]{:S(2)}) collective-permute-start(f32[4,32,256]{2,1,0:T(8,128)S(1)} %get-tuple-element.29), channel_id=1, source_target_pairs={{0,1},{1,0},{2,3},{3,2},{4,5},{5,4},{6,7},{7,6},{8,9},{9,8},{10,11... | collective-permute-start | bytes 393224 | tf_op jit(solution)/shard_map/ppermute | solution.py:21
  26.7 1.4 %shard_map.73 = (f32[4,32,256]{2,1,0:T(8,128)S(1)}, f32[4,32,256]{2,1,0:T(8,128)S(1)}, f32[1,512,256]{2,1,0:T(8,128)S(1)}) custom-call(s32[4,8]{1,0:T(4,128)S(1)} %copy-done, bf16[4,2,32,256]{3,2,1,0:T(8,128)(2,1)S(1)} %pad_maximum_fusion.refs_1_, ...), custom_call_target="tpu_custom_call", output_to_operand_aliasing={{0}: (5, {}), {1}: (6, {}), {2}: (7, {})} | custom-call | tf_op jit(solution)/shard_map/pallas_call | solution.py:137
  28.2 0.0 collective-permute-done.7
  28.2 1.7 %collective-permute-start.10 = (f32[2,32,256]{2,1,0:T(8,128)S(1)}, f32[2,32,256]{2,1,0:T(8,128)S(1)}, u32[]{:S(2)}, u32[]{:S(2)}) collective-permute-start(f32[2,32,256]{2,1,0:T(8,128)S(1)} %slice.26), channel_id=1, source_target_pairs={{0,4},{1,5},{2,6},{3,7},{4,0},{5,1},{6,2},{7,3},{8,12},{9,13},{10,... | collective-permute-start | bytes 196616 | tf_op jit(solution)/shard_map/ppermute | solution.py:21
  29.9 0.0 collective-permute-done.8
  29.9 0.7 %collective-permute-start.9 = (f32[2,32,256]{2,1,0:T(8,128)S(1)}, f32[2,32,256]{2,1,0:T(8,128)S(1)}, u32[]{:S(2)}, u32[]{:S(2)}) collective-permute-start(f32[2,32,256]{2,1,0:T(8,128)S(1)} %get-tuple-element.32), channel_id=1, source_target_pairs={{0,2},{1,3},{2,0},{3,1},{4,6},{5,7},{6,4},{7,5},{8,10},{9,11},{10,... | collective-permute-start | bytes 196616 | tf_op jit(solution)/shard_map/ppermute | solution.py:21
  30.6 1.3 %collective-permute-start.11 = (f32[2,32,256]{2,1,0:T(8,128)S(1)}, f32[2,32,256]{2,1,0:T(8,128)S(1)}, u32[]{:S(2)}, u32[]{:S(2)}) collective-permute-start(f32[2,32,256]{2,1,0:T(8,128)S(1)} %get-tuple-element.33), channel_id=1, source_target_pairs={{0,6},{1,7},{2,4},{3,5},{4,2},{5,3},{6,0},{7,1},{8,14},{9,15},{10,... | collective-permute-start | bytes 196616 | tf_op jit(solution)/shard_map/ppermute | solution.py:21
  31.9 0.1 shard_map.74
  32.0 1.6 %collective-permute-start.13 = (s16[1,528,256]{2,1,0:T(8,128)(2,1)S(1)}, s16[1,528,256]{2,1,0:T(8,128)(2,1)S(1)}, u32[]{:S(2)}, u32[]{:S(2)}) collective-permute-start(s16[1,528,256]{2,1,0:T(8,128)(2,1)S(1)} %shard_map.74), channel_id=1, source_target_pairs={{0,16},{16,0},{1,17},{17,1},{2,18},{18,2},{3,19},{19,3},{4,20},{20... | collective-permute-start | bytes 811016 | tf_op jit(solution)/shard_map/ppermute | solution.py:21
  33.6 0.0 collective-permute-done.10
  33.6 1.4 %collective-permute-done.9 = f32[2,32,256]{2,1,0:T(8,128)S(1)} collective-permute-done((f32[2,32,256]{2,1,0:T(8,128)S(1)}, f32[2,32,256]{2,1,0:T(8,128)S(1)}, u32[]{:S(2)}, u32[]{:S(2)}) %collective-permute-start.9) | collective-permute-done | bytes 65568 | tf_op jit(solution)/shard_map/ppermute | solution.py:21
  35.0 0.8 %collective-permute-done.11 = f32[2,32,256]{2,1,0:T(8,128)S(1)} collective-permute-done((f32[2,32,256]{2,1,0:T(8,128)S(1)}, f32[2,32,256]{2,1,0:T(8,128)S(1)}, u32[]{:S(2)}, u32[]{:S(2)}) %collective-permute-start.11) | collective-permute-done | bytes 65568 | tf_op jit(solution)/shard_map/ppermute | solution.py:21
  35.8 2.8 %collective-permute-start.12 = (f32[1,32,256]{2,1,0:T(8,128)S(1)}, f32[1,32,256]{2,1,0:T(8,128)S(1)}, u32[]{:S(2)}, u32[]{:S(2)}) collective-permute-start(f32[1,32,256]{2,1,0:T(8,128)S(1)} %slice.29), channel_id=1, source_target_pairs={{0,8},{1,9},{2,10},{3,11},{4,12},{5,13},{6,14},{7,15},{8,0},{9,1},... | collective-permute-start | bytes 98312 | tf_op jit(solution)/shard_map/ppermute | solution.py:21
  38.6 2.2 %collective-permute-done.12 = f32[1,32,256]{2,1,0:T(8,128)S(1)} collective-permute-done((f32[1,32,256]{2,1,0:T(8,128)S(1)}, f32[1,32,256]{2,1,0:T(8,128)S(1)}, u32[]{:S(2)}, u32[]{:S(2)}) %collective-permute-start.12) | collective-permute-done | bytes 32800 | tf_op jit(solution)/shard_map/ppermute | solution.py:21
  40.8 0.6 %fusion.2 = f32[32,256]{1,0:T(8,128)} fusion(f32[1,32,256]{2,1,0:T(8,128)S(1)} %collective-permute-done.12, f32[2,32,256]{2,1,0:T(8,128)S(1)} %fusion.1), kind=kLoop, calls=%fused_computation.6 | loop fusion | flops 8192 | bytes 98304 | tf_op jit(solution)/shard_map/reshape | solution.py:290
  41.4 0.0 collective-permute-done.13.q_ref
  41.4 0.9 %shard_map.75 = f32[1,512,256]{2,1,0:T(8,128)} custom-call(f32[1,512,256]{2,1,0:T(8,128)S(1)} %get-tuple-element.30.x_ref, s16[1,528,256]{2,1,0:T(8,128)(2,1)S(1)} %collective-permute-done.13.q_ref), custom_call_target="tpu_custom_call" | custom-call | tf_op jit(solution)/shard_map/pallas_call | solution.py:212
  (8 shorter events, 0.1 us)
Async XLA Ops:
  0.6 13.2 %copy-start.1 = (bf16[512,256]{1,0:T(8,128)(2,1)S(1)}, bf16[512,256]{1,0:T(8,128)(2,1)}, u32[]{:S(2)}) copy-start(bf16[512,256]{1,0:T(8,128)(2,1)} %param.6) | copy-start | bytes 786436
  1.4 6.3 %collective-permute-start = (bf16[1,2,32,256]{3,2,1,0:T(8,128)(2,1)S(1)}, bf16[1,2,32,256]{3,2,1,0:T(8,128)(2,1)S(1)}, u32[]{:S(2)}, u32[]{:S(2)}) collective-permute-start(bf16[1,2,32,256]{3,2,1,0:T(8,128)(2,1)S(1)} %maximum_bitcast_fusion), channel_id=1, source_target_pairs={{0,8},{1,9},{2,10},{3,11},{4,12},{5,13},{6,14},{7,15},{8,0},{9,1},... | collective-permute-start | bytes 98312 | tf_op jit(solution)/shard_map/ppermute | solution.py:21
  7.7 4.3 %collective-permute-start.1 = (bf16[2,2,32,256]{3,2,1,0:T(8,128)(2,1)S(1)}, bf16[2,2,32,256]{3,2,1,0:T(8,128)(2,1)S(1)}, u32[]{:S(2)}, u32[]{:S(2)}) collective-permute-start(bf16[2,2,32,256]{3,2,1,0:T(8,128)(2,1)S(1)} %pad_maximum_fusion.1), channel_id=1, source_target_pairs={{0,4},{1,5},{2,6},{3,7},{4,0},{5,1},{6,2},{7,3},{8,12},{9,13},{10,... | collective-permute-start | bytes 196616 | tf_op jit(solution)/shard_map/ppermute | solution.py:21
  12.1 5.0 %collective-permute-start.2 = (bf16[4,2,32,256]{3,2,1,0:T(8,128)(2,1)S(1)}, bf16[4,2,32,256]{3,2,1,0:T(8,128)(2,1)S(1)}, u32[]{:S(2)}, u32[]{:S(2)}) collective-permute-start(bf16[4,2,32,256]{3,2,1,0:T(8,128)(2,1)S(1)} %pad_maximum_fusion.refs_1_), channel_id=1, source_target_pairs={{0,2},{1,3},{2,0},{3,1},{4,6},{5,7},{6,4},{7,5},{8,10},{9,11},{10,... | collective-permute-start | bytes 393224 | tf_op jit(solution)/shard_map/ppermute | solution.py:21
  13.9 9.0 %collective-permute-start.3 = (bf16[1,512,256]{2,1,0:T(8,128)(2,1)S(1)}, bf16[1,512,256]{2,1,0:T(8,128)(2,1)S(1)}, u32[]{:S(2)}, u32[]{:S(2)}) collective-permute-start(bf16[1,512,256]{2,1,0:T(8,128)(2,1)S(1)} %bitcast.11), channel_id=1, source_target_pairs={{0,16},{16,0},{1,17},{17,1},{2,18},{18,2},{3,19},{19,3},{4,20},{20... | collective-permute-start | bytes 786440 | tf_op jit(solution)/shard_map/ppermute | solution.py:21
  15.4 9.3 %collective-permute-start.4 = (bf16[1,512,256]{2,1,0:T(8,128)(2,1)}, bf16[1,512,256]{2,1,0:T(8,128)(2,1)S(1)}, u32[]{:S(2)}, u32[]{:S(2)}) collective-permute-start(bf16[1,512,256]{2,1,0:T(8,128)(2,1)} %bitcast.12), channel_id=1, source_target_pairs={{0,16},{16,0},{1,17},{17,1},{2,18},{18,2},{3,19},{19,3},{4,20},{20... | collective-permute-start | bytes 786440 | tf_op jit(solution)/shard_map/ppermute | solution.py:21
  15.9 2.3 %collective-permute-start.5 = (bf16[4,2,32,256]{3,2,1,0:T(8,128)(2,1)S(1)}, bf16[4,2,32,256]{3,2,1,0:T(8,128)(2,1)S(1)}, u32[]{:S(2)}, u32[]{:S(2)}) collective-permute-start(bf16[4,2,32,256]{3,2,1,0:T(8,128)(2,1)S(1)} %pad_maximum_fusion.refs_1_), channel_id=1, source_target_pairs={{0,1},{1,0},{2,3},{3,2},{4,5},{5,4},{6,7},{7,6},{8,9},{9,8},{10,11... | collective-permute-start | bytes 393224 | tf_op jit(solution)/shard_map/ppermute | solution.py:21
  17.1 4.4 %collective-permute-start.6 = (bf16[4,2,32,256]{3,2,1,0:T(8,128)(2,1)S(1)}, bf16[4,2,32,256]{3,2,1,0:T(8,128)(2,1)S(1)}, u32[]{:S(2)}, u32[]{:S(2)}) collective-permute-start(bf16[4,2,32,256]{3,2,1,0:T(8,128)(2,1)S(1)} %collective-permute-done.2.refs_1_.refs_2_), channel_id=1, source_target_pairs={{0,1},{1,0},{2,3},{3,2},{4,5},{5,4},{6,7},{7,6},{8,9},{9,8},{10,11... | collective-permute-start | bytes 393224 | tf_op jit(solution)/shard_map/ppermute | solution.py:21
  18.2 0.7 %copy-start = (s32[4,8]{1,0:T(4,128)S(1)}, s32[4,8]{1,0:T(4,128)}, u32[]{:S(2)}) copy-start(s32[4,8]{1,0:T(4,128)} %refs_0_.9) | copy-start | bytes 388
  26.2 2.0 %collective-permute-start.7 = (f32[4,32,256]{2,1,0:T(8,128)S(1)}, f32[4,32,256]{2,1,0:T(8,128)S(1)}, u32[]{:S(2)}, u32[]{:S(2)}) collective-permute-start(f32[4,32,256]{2,1,0:T(8,128)S(1)} %get-tuple-element.27), channel_id=1, source_target_pairs={{0,1},{1,0},{2,3},{3,2},{4,5},{5,4},{6,7},{7,6},{8,9},{9,8},{10,11... | collective-permute-start | bytes 393224 | tf_op jit(solution)/shard_map/ppermute | solution.py:21
  26.2 3.7 %collective-permute-start.8 = (f32[4,32,256]{2,1,0:T(8,128)S(1)}, f32[4,32,256]{2,1,0:T(8,128)S(1)}, u32[]{:S(2)}, u32[]{:S(2)}) collective-permute-start(f32[4,32,256]{2,1,0:T(8,128)S(1)} %get-tuple-element.29), channel_id=1, source_target_pairs={{0,1},{1,0},{2,3},{3,2},{4,5},{5,4},{6,7},{7,6},{8,9},{9,8},{10,11... | collective-permute-start | bytes 393224 | tf_op jit(solution)/shard_map/ppermute | solution.py:21
  28.2 5.4 %collective-permute-start.10 = (f32[2,32,256]{2,1,0:T(8,128)S(1)}, f32[2,32,256]{2,1,0:T(8,128)S(1)}, u32[]{:S(2)}, u32[]{:S(2)}) collective-permute-start(f32[2,32,256]{2,1,0:T(8,128)S(1)} %slice.26), channel_id=1, source_target_pairs={{0,4},{1,5},{2,6},{3,7},{4,0},{5,1},{6,2},{7,3},{8,12},{9,13},{10,... | collective-permute-start | bytes 196616 | tf_op jit(solution)/shard_map/ppermute | solution.py:21
  29.9 5.0 %collective-permute-start.9 = (f32[2,32,256]{2,1,0:T(8,128)S(1)}, f32[2,32,256]{2,1,0:T(8,128)S(1)}, u32[]{:S(2)}, u32[]{:S(2)}) collective-permute-start(f32[2,32,256]{2,1,0:T(8,128)S(1)} %get-tuple-element.32), channel_id=1, source_target_pairs={{0,2},{1,3},{2,0},{3,1},{4,6},{5,7},{6,4},{7,5},{8,10},{9,11},{10,... | collective-permute-start | bytes 196616 | tf_op jit(solution)/shard_map/ppermute | solution.py:21
  30.6 5.2 %collective-permute-start.11 = (f32[2,32,256]{2,1,0:T(8,128)S(1)}, f32[2,32,256]{2,1,0:T(8,128)S(1)}, u32[]{:S(2)}, u32[]{:S(2)}) collective-permute-start(f32[2,32,256]{2,1,0:T(8,128)S(1)} %get-tuple-element.33), channel_id=1, source_target_pairs={{0,6},{1,7},{2,4},{3,5},{4,2},{5,3},{6,0},{7,1},{8,14},{9,15},{10,... | collective-permute-start | bytes 196616 | tf_op jit(solution)/shard_map/ppermute | solution.py:21
  32.0 9.4 %collective-permute-start.13 = (s16[1,528,256]{2,1,0:T(8,128)(2,1)S(1)}, s16[1,528,256]{2,1,0:T(8,128)(2,1)S(1)}, u32[]{:S(2)}, u32[]{:S(2)}) collective-permute-start(s16[1,528,256]{2,1,0:T(8,128)(2,1)S(1)} %shard_map.74), channel_id=1, source_target_pairs={{0,16},{16,0},{1,17},{17,1},{2,18},{18,2},{3,19},{19,3},{4,20},{20... | collective-permute-start | bytes 811016 | tf_op jit(solution)/shard_map/ppermute | solution.py:21
  35.8 5.0 %collective-permute-start.12 = (f32[1,32,256]{2,1,0:T(8,128)S(1)}, f32[1,32,256]{2,1,0:T(8,128)S(1)}, u32[]{:S(2)}, u32[]{:S(2)}) collective-permute-start(f32[1,32,256]{2,1,0:T(8,128)S(1)} %slice.29), channel_id=1, source_target_pairs={{0,8},{1,9},{2,10},{3,11},{4,12},{5,13},{6,14},{7,15},{8,0},{9,1},... | collective-permute-start | bytes 98312 | tf_op jit(solution)/shard_map/ppermute | solution.py:21

commit v4 on v3

v4 whole, which is shorter than its diff:
```python
import functools
import math

import jax
import jax.numpy as jnp
from jax import lax
from jax.experimental import pallas as pl
from jax.experimental.pallas import tpu as pltpu
from jax.sharding import PartitionSpec as P

f32 = jnp.float32
bf16 = jnp.bfloat16
NN = (((1,), (0,)), ((), ()))
NT = (((1,), (1,)), ((), ()))
TN = (((0,), (0,)), ((), ()))
dot = functools.partial(lax.dot_general, preferred_element_type=f32)
TILE = 256


def swap(x, axis, size, bits):
    return lax.ppermute(x, axis, [(i, i ^ bits) for i in range(size)])


def bits_of(low, high):
    out = []
    bit = high // 2
    while bit >= low:
        out.append(bit)
        bit //= 2
    return out


def relative(bits):
    order = [0]
    for bit in bits:
        order = order + [r ^ bit for r in order]
    return order


def region_kernel(*refs, n_users, sums_at, n_sums, add_item, lanes, cols, scale):
    seen_ref = refs[0]
    users = refs[1 : 1 + n_users]
    at = 1 + n_users
    fac_i, tan_i = refs[at : at + 2]
    at += 2
    user_in = refs[at : at + n_sums]
    at += n_sums
    item_in = refs[at] if add_item else None
    at += add_item
    user_out, item_out, u_all, c_all = refs[at:]

    n_a, _, us, _ = users[0].shape
    n_pieces, it_dev, _ = fac_i.shape
    for b, ref in enumerate(users):
        for k in range(n_a):
            for ft in range(2):
                u_all[ft, pl.ds((b * n_a + k) * us, us), :] = ref[k, ft]
    total_rows = n_users * n_a * us
    tile = min(TILE, total_rows)
    in_tile = tile // us
    blocks = cols[1]
    block = it_dev // blocks
    sub = min(TILE, it_dev)
    for t in range(total_rows // tile):
        rows = pl.ds(t * tile, tile)
        fac = u_all[0, rows, :]
        tan = u_all[1, rows, :]
        total = None
        for k in range(n_pieces):
            for ib in range(it_dev // sub):
                items = pl.ds(ib * sub, sub)
                v = fac_i[k, items, :]
                dv = tan_i[k, items, :]
                if 2 * tile <= TILE:
                    both = dot(v, jnp.concatenate([fac, tan], 0), NT)
                    s = both[:, :tile]
                    tt = both[:, tile:] + dot(dv, fac, NT)
                else:
                    s = dot(v, fac, NT)
                    tt = dot(v, tan, NT) + dot(dv, fac, NT)
                seen = []
                for i in range(sub // block):
                    row = seen_ref[
                        pl.ds((cols[0] + k) * blocks + ib * (sub // block) + i, 1), pl.ds(lanes + t * tile, tile)
                    ]
                    seen.append(jnp.broadcast_to(row, (block, tile)))
                seen = jnp.concatenate(seen, 0)
                e = jnp.exp(jnp.abs(s) * -scale)
                p = 1.0 / (1.0 + e)
                c = (e * p * p * (tt * seen)).astype(bf16)
                c_all[k, items, pl.ds(0, tile)] = c
            r = dot(c_all[k], fac, NN) * scale
            if t > 0:
                r = r + item_out[k]
            elif item_in is not None:
                r = r + item_in[k]
            item_out[k] = r
            part = dot(c_all[k], fac_i[k], TN)
            total = part if total is None else total + part
        total = total * scale
        for j in range(in_tile):
            b, k = divmod(t * in_tile + j, n_a)
            r = total[j * us : (j + 1) * us]
            if n_sums:
                r = r + user_in[sums_at[b][0]][sums_at[b][1], k]
            user_out[b, k] = r


def in_vmem(x):
    return pltpu.with_memory_space_constraint(x, pltpu.VMEM)


VM = pl.BlockSpec(memory_space=pltpu.VMEM)
PARAMS = pltpu.CompilerParams(vmem_limit_bytes=16 * 2**20)


def region(seen, users, items, sums, sums_at, item_sum, **static):
    n_a, _, us, width = users[0].shape
    n_pieces, it_dev, _ = items[0].shape
    given = [in_vmem(x) for x in (seen, *users, *items, *sums)]
    aliases = {}
    if item_sum is not None:
        aliases[len(given)] = 1
        given.append(in_vmem(item_sum))
    total_rows = len(users) * n_a * us
    return pl.pallas_call(
        functools.partial(
            region_kernel,
            n_users=len(users),
            sums_at=sums_at,
            n_sums=len(sums),
            add_item=item_sum is not None,
            **static,
        ),
        in_specs=[VM] * len(given),
        out_specs=[VM] * 2,
        out_shape=[
            pltpu.VMEM((len(users), n_a, us, width), f32),
            pltpu.VMEM((n_pieces, it_dev, width), f32),
        ],
        input_output_aliases=aliases,
        scratch_shapes=[
            pltpu.VMEM((2, total_rows, width), bf16),
            pltpu.VMEM((n_pieces, it_dev, min(TILE, total_rows)), bf16),
        ],
        compiler_params=PARAMS,
    )(*given)


def load_kernel(mask, fac, tan, fac_out, tan_out, seen, sems, *, rows_of, cols_of, us, scale):
    copies = [
        pltpu.make_async_copy(fac, fac_out, sems.at[0]),
        pltpu.make_async_copy(tan, tan_out, sems.at[1]),
    ]
    for c in copies:
        c.start()
    per, order = cols_of
    members, rows = rows_of
    me_row = lax.axis_index("ia") // members
    me_col = lax.axis_index("au")
    lane = lax.broadcasted_iota(jnp.int32, (1, seen.shape[1]), 1)
    for q, rel in enumerate(order):
        for i in range(per):
            value = {r: mask[me_row ^ r, (me_col ^ rel) * per + i].astype(f32) * scale for r in sorted(set(rows))}
            line = None
            for j in reversed(range(len(rows))):
                full = jnp.full(lane.shape, value[rows[j]], f32)
                line = full if line is None else jnp.where(lane < (j + 1) * us, full, line)
            seen[pl.ds(q * per + i, 1), :] = line
    for c in copies:
        c.wait()


def load(mask, fac, tan, **static):
    hbm = [pltpu.with_memory_space_constraint(x, pltpu.HBM) for x in (fac, tan)]
    blocks = static["cols_of"][0] * len(static["cols_of"][1])
    lanes = len(static["rows_of"][1]) * static["us"]
    return pl.pallas_call(
        functools.partial(load_kernel, **static),
        in_specs=[pl.BlockSpec(memory_space=pltpu.SMEM)] + [pl.BlockSpec(memory_space=pltpu.HBM)] * 2,
        out_specs=[VM] * 3,
        out_shape=[pltpu.VMEM(fac.shape, fac.dtype), pltpu.VMEM(tan.shape, tan.dtype), pltpu.VMEM((blocks, lanes), f32)],
        scratch_shapes=[pltpu.SemaphoreType.DMA((2,))],
        compiler_params=PARAMS,
    )(mask, *hbm)


def stack_kernel(a, b, out, sems):
    copies = [
        pltpu.make_async_copy(a, out.at[0, 0], sems.at[0]),
        pltpu.make_async_copy(b, out.at[0, 1], sems.at[1]),
    ]
    for c in copies:
        c.start()
    for c in copies:
        c.wait()


def stack(a, b):
    return pl.pallas_call(
        stack_kernel,
        in_specs=[pl.BlockSpec(memory_space=pltpu.HBM)] * 2,
        out_specs=VM,
        out_shape=pltpu.VMEM((1, 2, *a.shape), a.dtype),
        scratch_shapes=[pltpu.SemaphoreType.DMA((2,))],
        compiler_params=PARAMS,
    )(*[pltpu.with_memory_space_constraint(x, pltpu.HBM) for x in (a, b)])


GROUPS = 16


def encode_kernel(x_ref, out_ref):
    n, rows, _ = x_ref.shape
    step = rows // GROUPS
    for k in range(n):
        exps = []
        for g in range(GROUPS):
            x = x_ref[k, pl.ds(g * step, step), :]
            top = jnp.max(jnp.abs(x), 0, keepdims=True)
            e = 14.0 - jnp.ceil(jnp.log2(jnp.maximum(top, 1e-30)))
            out_ref[k, pl.ds(g * step, step), :] = jnp.round(x * jnp.exp2(e)).astype(jnp.int32).astype(jnp.int16)
            exps.append(e)
        out_ref[k, pl.ds(rows, GROUPS), :] = jnp.concatenate(exps, 0).astype(jnp.int32).astype(jnp.int16)


def encode(x):
    n, rows, width = x.shape
    return pl.pallas_call(
        encode_kernel,
        in_specs=[VM],
        out_specs=VM,
        out_shape=pltpu.VMEM((n, rows + GROUPS, width), jnp.int16),
        compiler_params=PARAMS,
    )(in_vmem(x))


def decode_kernel(x_ref, q_ref, out_ref, *, at):
    n, rows, _ = x_ref.shape
    step = rows // GROUPS
    for k in range(n):
        unit = jnp.exp2(-q_ref[at + k, pl.ds(rows, GROUPS), :].astype(jnp.int32).astype(f32))
        for g in range(GROUPS):
            part = pl.ds(g * step, step)
            out_ref[k, part, :] = x_ref[k, part, :] + q_ref[at + k, part, :].astype(jnp.int32).astype(f32) * unit[g : g + 1]


def add_decoded(x, q, at):
    return pl.pallas_call(
        functools.partial(decode_kernel, at=at),
        in_specs=[VM, VM],
        out_specs=VM,
        out_shape=jax.ShapeDtypeStruct(x.shape, f32),
        compiler_params=PARAMS,
    )(in_vmem(x), in_vmem(q))


def on_device(user_factors, item_factors, user_tangent, item_tangent, block_mask, n_au, n_ia):
    us, width = user_factors.shape
    row_blocks, per = block_mask.shape
    per //= n_au
    members = us * n_ia // row_blocks // us
    assert members == 4
    scale = 1.0 / math.sqrt(width)
    core, near = 1, [0, 2, 4, 6]
    a_bits = bits_of(8, n_ia)
    rel_a = relative(a_bits)

    far = stack(user_factors, user_tangent)
    for bit in a_bits:
        far = jnp.concatenate([far, swap(far, "ia", n_ia, bit)], 0)

    item_bits = bits_of(1, n_au)
    rel_items = relative(item_bits)
    facs, tans = [item_factors[None]], [item_tangent[None]]
    for n, bit in enumerate(item_bits):
        held_f = facs[0] if n == 0 else jnp.concatenate(facs, 0)
        held_t = tans[0] if n == 0 else jnp.concatenate(tans, 0)
        facs.append(swap(held_f, "au", n_au, bit))
        tans.append(swap(held_t, "au", n_au, bit))
    rows = [(b ^ r) // members for b in near for r in rel_a]
    facs[0], tans[0], seen = load(
        block_mask, facs[0], tans[0], rows_of=(members, rows), cols_of=(per, rel_items), us=us, scale=scale
    )
    piece = len(rel_a) * us

    mine = [far] + [swap(far, "ia", n_ia, b) for b in near[1:]]
    other = [swap(x, "ia", n_ia, core) for x in mine]

    def call(users, g, sums, sums_at, item_sum, lanes=0):
        at = sum(f.shape[0] for f in facs[:g])
        return region(
            seen, users, (facs[g], tans[g]), sums, sums_at, item_sum, lanes=lanes, cols=(at, per), scale=scale
        )

    first, item_sum = call([mine[0], other[0]], 0, [], None, None)
    second, item_sum = call([mine[1], other[1], mine[2], other[2]], 0, [], None, item_sum)
    third, own_items = call([mine[3], other[3]], 0, [], None, item_sum, lanes=2 * piece)
    sums = [first, second, third]
    at_mine, at_other = [(0, 0), (1, 0), (1, 2), (2, 0)], [(0, 1), (1, 1), (1, 3), (2, 1)]
    item_sums = [own_items]
    for g in range(1, len(facs)):
        out_other, item_sum = call(other, g, sums, at_other, None)
        out_mine, item_sum = call(mine, g, sums, at_mine, item_sum)
        item_sums.append(item_sum)
        sums = [out_mine, out_other]
        at_mine, at_other = [(0, i) for i in range(4)], [(1, i) for i in range(4)]

    keep = out_mine + swap(out_other, "ia", n_ia, core)
    acc = keep[0]
    for n, b in enumerate(near[1:]):
        acc = acc + swap(keep[n + 1], "ia", n_ia, b)
    for bit in a_bits[::-1]:
        half = acc.shape[0] // 2
        acc = acc[:half] + swap(acc[half:], "ia", n_ia, bit)
    user_product = acc.reshape(us, width)

    for bit in item_bits[::-1]:
        back = swap(encode(item_sums.pop()), "au", n_au, bit)
        sizes = [h.shape[0] for h in item_sums]
        cuts = [sum(sizes[:i]) for i in range(len(sizes))]
        item_sums = [add_decoded(h, back, c) for h, c in zip(item_sums, cuts)]
    item_product = item_sums[0][0]
    return user_product, item_product


def solution(mesh):
    n_au, n_ia = mesh.shape["au"], mesh.shape["ia"]
    placed = (
        P(("au", "ia"), None),
        P(("ia", "au"), None),
        P(("au", "ia"), None),
        P(("ia", "au"), None),
        P("au", "ia"),
    )

    def body(*args):
        return on_device(*args, n_au=n_au, n_ia=n_ia)

    return jax.shard_map(
        body,
        mesh=mesh,
        in_specs=placed,
        out_specs=(P(("au", "ia"), None), P(("ia", "au"), None)),
        check_vma=False,
    )
```

time: 42.5 us -> 35.7 us (0.84)
  waiting for transfers between devices: 12.4 us -> 8.66 us
  Pallas kernels: 8.82 us -> 6.67 us
  other arithmetic: 1.48 us -> 0.68 us
  local copies, waits for them, and re-layouts: 0.69 us -> 0.02 us
  starting transfers between devices: 18 us -> 18.6 us
    ppermute x14 -> x16, waiting for transfers between devices: 12.4 us -> 8.66 us  [swap(): return lax.ppermute(x, axis, [(i, i ^ bits) for i in range(size)])]
    pallas_call x6 -> x7, Pallas kernels: 7.82 us -> 5.67 us  [the longest x5 3.31 us: region(): pl.pallas_call(functools.partial(region_kernel, n_users=len(users), sums_...]
    broadcast_in_dim x1 -> x0, other arithmetic: 0.78 us -> none  [on_device(): far = jnp.stack([user_factors, user_tangent])[None]]
    unnamed x4 -> x2, local copies, waits for them, and re-layouts: 0.67 us -> 0.01 us
    ppermute x14 -> x16, starting transfers between devices: 18 us -> 18.6 us  [swap(): return lax.ppermute(x, axis, [(i, i ^ bits) for i in range(size)])]
  transfers between devices with their start and end apart: 14 -> 16, of which waited for: 7 -> 8; matrix products, arithmetic and copies ran while one was open for 2% -> 0% of each run, Pallas kernels for 15% -> 15%
where the time goes in v4:
time: 35.7 us; the launch traced here: 35.3 us
  starting transfers between devices  18.6 us (52%)
  waiting for transfers between devices  8.66 us (24%)
  Pallas kernels  6.67 us (19%)
  between operations  0.76 us (2%)
  other arithmetic  0.68 us (2%)
    ppermute x16, starting transfers between devices, swap(): return lax.ppermute(x, axis, [(i, i ^ bits) for i in range(size)])  18.6 us
    ppermute x16, waiting for transfers between devices, swap(): return lax.ppermute(x, axis, [(i, i ^ bits) for i in range(size)])  8.66 us
    pallas_call x5, Pallas kernels, region(): pl.pallas_call(functools.partial(region_kernel, n_users=len(users), sums_...  3.31 us
    pallas_call x1, Pallas kernels, load(): pl.pallas_call(functools.partial(load_kernel, **static), in_specs=[pl.Blo...  1.61 us
    pallas_call x1, Pallas kernels, add_decoded(): pl.pallas_call(functools.partial(decode_kernel, at=at), in_specs=[VM, VM]...  0.88 us
    pallas_call x1, Pallas kernels, stack(): pl.pallas_call(stack_kernel, in_specs=[pl.BlockSpec(memory_space=pltpu.HB...  0.75 us
  transfers between devices with their start and end apart: 16, of which 8 were waited for; matrix products, arithmetic and copies ran while one was open for 0% of the time, Pallas kernels for 15%

profile of v4, /device:TPU:0, one launch (start us, length us, event | category | flops | bytes accessed | tf_op | source)
XLA Modules:
  0.0 35.3 jit_solution(16010812035594572027)
XLA Ops:
  0.6 0.8 %shard_map.69 = bf16[1,2,32,256]{3,2,1,0:T(8,128)(2,1)S(1)} custom-call(bf16[32,256]{1,0:T(8,128)(2,1)} %a.1, bf16[32,256]{1,0:T(8,128)(2,1)} %b.1), custom_call_target="tpu_custom_call" | custom-call | tf_op jit(solution)/shard_map/pallas_call | solution.py:200
  1.4 4.1 %collective-permute-start = (bf16[1,2,32,256]{3,2,1,0:T(8,128)(2,1)S(1)}, bf16[1,2,32,256]{3,2,1,0:T(8,128)(2,1)S(1)}, u32[]{:S(2)}, u32[]{:S(2)}) collective-permute-start(bf16[1,2,32,256]{3,2,1,0:T(8,128)(2,1)S(1)} %shard_map.69), channel_id=1, source_target_pairs={{0,8},{1,9},{2,10},{3,11},{4,12},{5,13},{6,14},{7,15},{8,0},{9,1},... | collective-permute-start | bytes 98312 | tf_op jit(solution)/shard_map/ppermute | solution.py:21
  5.5 1.5 %collective-permute-start.4 = (bf16[1,512,256]{2,1,0:T(8,128)(2,1)}, bf16[1,512,256]{2,1,0:T(8,128)(2,1)S(1)}, u32[]{:S(2)}, u32[]{:S(2)}) collective-permute-start(bf16[1,512,256]{2,1,0:T(8,128)(2,1)} %bitcast.20), channel_id=1, source_target_pairs={{0,16},{16,0},{1,17},{17,1},{2,18},{18,2},{3,19},{19,3},{4,20},{20... | collective-permute-start | bytes 786440 | tf_op jit(solution)/shard_map/ppermute | solution.py:21
  7.0 0.0 copy-start
  7.0 0.5 %collective-permute-start.5 = (bf16[1,512,256]{2,1,0:T(8,128)(2,1)}, bf16[1,512,256]{2,1,0:T(8,128)(2,1)S(1)}, u32[]{:S(2)}, u32[]{:S(2)}) collective-permute-start(bf16[1,512,256]{2,1,0:T(8,128)(2,1)} %bitcast.22), channel_id=1, source_target_pairs={{0,16},{16,0},{1,17},{17,1},{2,18},{18,2},{3,19},{19,3},{4,20},{20... | collective-permute-start | bytes 786440 | tf_op jit(solution)/shard_map/ppermute | solution.py:21
  7.5 0.2 collective-permute-done
  7.8 0.1 collective-permute-start.6
  7.9 1.6 %collective-permute-start.2 = (bf16[2,2,32,256]{3,2,1,0:T(8,128)(2,1)S(1)}, bf16[2,2,32,256]{3,2,1,0:T(8,128)(2,1)S(1)}, u32[]{:S(2)}, u32[]{:S(2)}) collective-permute-start(bf16[2,2,32,256]{3,2,1,0:T(8,128)(2,1)S(1)} %pad_maximum_fusion.refs_1_), channel_id=1, source_target_pairs={{0,4},{1,5},{2,6},{3,7},{4,0},{5,1},{6,2},{7,3},{8,12},{9,13},{10,... | collective-permute-start | bytes 196616 | tf_op jit(solution)/shard_map/ppermute | solution.py:21
  9.5 1.5 %collective-permute-start.1 = (bf16[2,2,32,256]{3,2,1,0:T(8,128)(2,1)S(1)}, bf16[2,2,32,256]{3,2,1,0:T(8,128)(2,1)S(1)}, u32[]{:S(2)}, u32[]{:S(2)}) collective-permute-start(bf16[2,2,32,256]{3,2,1,0:T(8,128)(2,1)S(1)} %pad_maximum_fusion.refs_1_), channel_id=1, source_target_pairs={{0,2},{1,3},{2,0},{3,1},{4,6},{5,7},{6,4},{7,5},{8,10},{9,11},{10,... | collective-permute-start | bytes 196616 | tf_op jit(solution)/shard_map/ppermute | solution.py:21
  11.0 0.0 collective-permute-done.6.refs_2_.refs_1_
  11.0 0.6 %collective-permute-start.3 = (bf16[2,2,32,256]{3,2,1,0:T(8,128)(2,1)S(1)}, bf16[2,2,32,256]{3,2,1,0:T(8,128)(2,1)S(1)}, u32[]{:S(2)}, u32[]{:S(2)}) collective-permute-start(bf16[2,2,32,256]{3,2,1,0:T(8,128)(2,1)S(1)} %pad_maximum_fusion.refs_1_), channel_id=1, source_target_pairs={{0,6},{1,7},{2,4},{3,5},{4,2},{5,3},{6,0},{7,1},{8,14},{9,15},{10,... | collective-permute-start | bytes 196616 | tf_op jit(solution)/shard_map/ppermute | solution.py:21
  11.6 0.8 %collective-permute-done.2.refs_3_ = bf16[2,2,32,256]{3,2,1,0:T(8,128)(2,1)S(1)} collective-permute-done((bf16[2,2,32,256]{3,2,1,0:T(8,128)(2,1)S(1)}, bf16[2,2,32,256]{3,2,1,0:T(8,128)(2,1)S(1)}, u32[]{:S(2)}, u32[]{:S(2)}) %collective-permute-start.2) | collective-permute-done | bytes 65568 | tf_op jit(solution)/shard_map/ppermute | solution.py:21
  12.4 0.0 collective-permute-start.8
  12.4 1.4 %collective-permute-done.1.refs_1_.refs_2_ = bf16[2,2,32,256]{3,2,1,0:T(8,128)(2,1)S(1)} collective-permute-done((bf16[2,2,32,256]{3,2,1,0:T(8,128)(2,1)S(1)}, bf16[2,2,32,256]{3,2,1,0:T(8,128)(2,1)S(1)}, u32[]{:S(2)}, u32[]{:S(2)}) %collective-permute-start.1) | collective-permute-done | bytes 65568 | tf_op jit(solution)/shard_map/ppermute | solution.py:21
  13.7 0.0 collective-permute-start.7
  13.7 2.4 %collective-permute-done.3.refs_1_.refs_4_ = bf16[2,2,32,256]{3,2,1,0:T(8,128)(2,1)S(1)} collective-permute-done((bf16[2,2,32,256]{3,2,1,0:T(8,128)(2,1)S(1)}, bf16[2,2,32,256]{3,2,1,0:T(8,128)(2,1)S(1)}, u32[]{:S(2)}, u32[]{:S(2)}) %collective-permute-start.3) | collective-permute-done | bytes 65568 | tf_op jit(solution)/shard_map/ppermute | solution.py:21
  16.1 0.0 collective-permute-start.9
  16.1 0.0 copy-done
  16.1 1.6 %shard_map.68 = (bf16[1,512,256]{2,1,0:T(8,128)(2,1)S(1)}, bf16[1,512,256]{2,1,0:T(8,128)(2,1)S(1)}, f32[8,256]{1,0:T(8,128)S(1)}) custom-call(s32[4,8]{1,0:T(4,128)S(1)} %copy-done, bf16[1,512,256]{2,1,0:T(8,128)(2,1)} %bitcast.21, bf16[1,512,256]{2,1,0:T(8,128)(2,1)} %bitcast.23), custom_call_target="tpu_custom_call" | custom-call | tf_op jit(solution)/shard_map/pallas_call | solution.py:178
  17.8 0.6 %shard_map.70 = (f32[2,2,32,256]{3,2,1,0:T(8,128)S(1)}, f32[1,512,256]{2,1,0:T(8,128)S(1)}) custom-call(f32[8,256]{1,0:T(8,128)S(1)} %get-tuple-element.15.refs_0_, bf16[2,2,32,256]{3,2,1,0:T(8,128)(2,1)S(1)} %pad_maximum_fusion.refs_1_, bf16[2,2,32,256]{3,2,1,0:T(8,128)(2,1)S(1)} %collective-permute-done.6.refs_2_.refs_1_, ...), custom_call_target="tpu_custom_call" | custom-call | tf_op jit(solution)/shard_map/pallas_call | solution.py:126
  18.3 0.0 collective-permute-done.8.refs_4_.refs_3_
  18.3 0.0 collective-permute-done.7.refs_2_
  18.4 0.7 %shard_map.71 = (f32[4,2,32,256]{3,2,1,0:T(8,128)S(1)}, f32[1,512,256]{2,1,0:T(8,128)S(1)}) custom-call(f32[8,256]{1,0:T(8,128)S(1)} %get-tuple-element.15.refs_0_, bf16[2,2,32,256]{3,2,1,0:T(8,128)(2,1)S(1)} %collective-permute-done.1.refs_1_.refs_2_, bf16[2,2,32,256]{3,2,1,0:T(8,128)(2,1)S(1)} %collective-permute-done.7.refs_2_, ...), custom_call_target="tpu_custom_call", output_to_operand_aliasing={{1}: (7, {})} | custom-call | tf_op jit(solution)/shard_map/pallas_call | solution.py:126
  19.1 0.0 collective-permute-done.9.refs_2_.refs_4_
  19.1 0.6 %shard_map.72 = (f32[2,2,32,256]{3,2,1,0:T(8,128)S(1)}, f32[1,512,256]{2,1,0:T(8,128)S(1)}) custom-call(f32[8,256]{1,0:T(8,128)S(1)} %get-tuple-element.15.refs_0_, bf16[2,2,32,256]{3,2,1,0:T(8,128)(2,1)S(1)} %collective-permute-done.3.refs_1_.refs_4_, ...), custom_call_target="tpu_custom_call", output_to_operand_aliasing={{1}: (5, {})} | custom-call | tf_op jit(solution)/shard_map/pallas_call | solution.py:126
  19.7 0.0 collective-permute-done.4.refs_5_
  19.7 0.0 collective-permute-done.5.refs_6_
  19.7 0.7 %shard_map.73 = (f32[4,2,32,256]{3,2,1,0:T(8,128)S(1)}, f32[1,512,256]{2,1,0:T(8,128)S(1)}) custom-call(f32[8,256]{1,0:T(8,128)S(1)} %get-tuple-element.15.refs_0_, bf16[2,2,32,256]{3,2,1,0:T(8,128)(2,1)S(1)} %collective-permute-done.6.refs_2_.refs_1_, bf16[2,2,32,256]{3,2,1,0:T(8,128)(2,1)S(1)} %collective-permute-done.7.refs_2_, ...), custom_call_target="tpu_custom_call" | custom-call | tf_op jit(solution)/shard_map/pallas_call | solution.py:126
  20.4 0.5 %collective-permute-start.10 = (f32[4,2,32,256]{3,2,1,0:T(8,128)S(1)}, f32[4,2,32,256]{3,2,1,0:T(8,128)S(1)}, u32[]{:S(2)}, u32[]{:S(2)}) collective-permute-start(f32[4,2,32,256]{3,2,1,0:T(8,128)S(1)} %get-tuple-element.25), channel_id=1, source_target_pairs={{0,1},{1,0},{2,3},{3,2},{4,5},{5,4},{6,7},{7,6},{8,9},{9,8},{10,11... | collective-permute-start | bytes 786440 | tf_op jit(solution)/shard_map/ppermute | solution.py:21
  21.0 0.7 %shard_map.74 = (f32[4,2,32,256]{3,2,1,0:T(8,128)S(1)}, f32[1,512,256]{2,1,0:T(8,128)S(1)}) custom-call(f32[8,256]{1,0:T(8,128)S(1)} %get-tuple-element.15.refs_0_, bf16[2,2,32,256]{3,2,1,0:T(8,128)(2,1)S(1)} %pad_maximum_fusion.refs_1_, bf16[2,2,32,256]{3,2,1,0:T(8,128)(2,1)S(1)} %collective-permute-done.1.refs_1_.refs_2_, ...), custom_call_target="tpu_custom_call", output_to_operand_aliasing={{1}: (10, {})} | custom-call | tf_op jit(solution)/shard_map/pallas_call | solution.py:126
  21.7 0.4 %collective-permute-done.10 = f32[4,2,32,256]{3,2,1,0:T(8,128)S(1)} collective-permute-done((f32[4,2,32,256]{3,2,1,0:T(8,128)S(1)}, f32[4,2,32,256]{3,2,1,0:T(8,128)S(1)}, u32[]{:S(2)}, u32[]{:S(2)}) %collective-permute-start.10) | collective-permute-done | bytes 262176 | tf_op jit(solution)/shard_map/ppermute | solution.py:21
  22.2 0.9 %collective-permute-start.11 = (f32[2,32,256]{2,1,0:T(8,128)S(1)}, f32[2,32,256]{2,1,0:T(8,128)S(1)}, u32[]{:S(2)}, u32[]{:S(2)}) collective-permute-start(f32[2,32,256]{2,1,0:T(8,128)S(1)} %get-tuple-element.28), channel_id=1, source_target_pairs={{0,2},{1,3},{2,0},{3,1},{4,6},{5,7},{6,4},{7,5},{8,10},{9,11},{10,... | collective-permute-start | bytes 196616 | tf_op jit(solution)/shard_map/ppermute | solution.py:21
  23.1 1.6 %collective-permute-start.13 = (f32[2,32,256]{2,1,0:T(8,128)S(1)}, f32[2,32,256]{2,1,0:T(8,128)S(1)}, u32[]{:S(2)}, u32[]{:S(2)}) collective-permute-start(f32[2,32,256]{2,1,0:T(8,128)S(1)} %get-tuple-element.29), channel_id=1, source_target_pairs={{0,6},{1,7},{2,4},{3,5},{4,2},{5,3},{6,0},{7,1},{8,14},{9,15},{10,... | collective-permute-start | bytes 196616 | tf_op jit(solution)/shard_map/ppermute | solution.py:21
  24.6 1.1 %collective-permute-start.12 = (f32[2,32,256]{2,1,0:T(8,128)S(1)}, f32[2,32,256]{2,1,0:T(8,128)S(1)}, u32[]{:S(2)}, u32[]{:S(2)}) collective-permute-start(f32[2,32,256]{2,1,0:T(8,128)S(1)} %get-tuple-element.30), channel_id=1, source_target_pairs={{0,4},{1,5},{2,6},{3,7},{4,0},{5,1},{6,2},{7,3},{8,12},{9,13},{10,... | collective-permute-start | bytes 196616 | tf_op jit(solution)/shard_map/ppermute | solution.py:21
  25.7 0.1 shard_map.75
  25.9 1.6 %collective-permute-start.15 = (s16[1,528,256]{2,1,0:T(8,128)(2,1)S(1)}, s16[1,528,256]{2,1,0:T(8,128)(2,1)S(1)}, u32[]{:S(2)}, u32[]{:S(2)}) collective-permute-start(s16[1,528,256]{2,1,0:T(8,128)(2,1)S(1)} %shard_map.75), channel_id=1, source_target_pairs={{0,16},{16,0},{1,17},{17,1},{2,18},{18,2},{3,19},{19,3},{4,20},{20... | collective-permute-start | bytes 811016 | tf_op jit(solution)/shard_map/ppermute | solution.py:21
  27.5 0.0 collective-permute-done.11
  27.5 1.3 %collective-permute-done.13 = f32[2,32,256]{2,1,0:T(8,128)S(1)} collective-permute-done((f32[2,32,256]{2,1,0:T(8,128)S(1)}, f32[2,32,256]{2,1,0:T(8,128)S(1)}, u32[]{:S(2)}, u32[]{:S(2)}) %collective-permute-start.13) | collective-permute-done | bytes 65568 | tf_op jit(solution)/shard_map/ppermute | solution.py:21
  28.7 0.5 %collective-permute-done.12 = f32[2,32,256]{2,1,0:T(8,128)S(1)} collective-permute-done((f32[2,32,256]{2,1,0:T(8,128)S(1)}, f32[2,32,256]{2,1,0:T(8,128)S(1)}, u32[]{:S(2)}, u32[]{:S(2)}) %collective-permute-start.12) | collective-permute-done | bytes 65568 | tf_op jit(solution)/shard_map/ppermute | solution.py:21
  29.2 2.9 %collective-permute-start.14 = (f32[1,32,256]{2,1,0:T(8,128)S(1)}, f32[1,32,256]{2,1,0:T(8,128)S(1)}, u32[]{:S(2)}, u32[]{:S(2)}) collective-permute-start(f32[1,32,256]{2,1,0:T(8,128)S(1)} %slice.29), channel_id=1, source_target_pairs={{0,8},{1,9},{2,10},{3,11},{4,12},{5,13},{6,14},{7,15},{8,0},{9,1},... | collective-permute-start | bytes 98312 | tf_op jit(solution)/shard_map/ppermute | solution.py:21
  32.1 1.7 %collective-permute-done.15.q_ref = s16[1,528,256]{2,1,0:T(8,128)(2,1)S(1)} collective-permute-done((s16[1,528,256]{2,1,0:T(8,128)(2,1)S(1)}, s16[1,528,256]{2,1,0:T(8,128)(2,1)S(1)}, u32[]{:S(2)}, u32[]{:S(2)}) %collective-permute-start.15) | collective-permute-done | bytes 270368 | tf_op jit(solution)/shard_map/ppermute | solution.py:21
  33.8 0.9 %shard_map.76 = f32[1,512,256]{2,1,0:T(8,128)} custom-call(f32[1,512,256]{2,1,0:T(8,128)S(1)} %get-tuple-element.26.x_ref, s16[1,528,256]{2,1,0:T(8,128)(2,1)S(1)} %collective-permute-done.15.q_ref), custom_call_target="tpu_custom_call" | custom-call | tf_op jit(solution)/shard_map/pallas_call | solution.py:249
  34.7 0.0 collective-permute-done.14
  34.7 0.6 %fusion.3 = f32[32,256]{1,0:T(8,128)} fusion(f32[1,32,256]{2,1,0:T(8,128)S(1)} %collective-permute-done.14, f32[2,32,256]{2,1,0:T(8,128)S(1)} %fusion.2), kind=kLoop, calls=%fused_computation.9 | loop fusion | flops 8192 | bytes 98304 | tf_op jit(solution)/shard_map/reshape | solution.py:316
  (5 shorter events, 0.1 us)
Async XLA Ops:
  1.4 6.4 %collective-permute-start = (bf16[1,2,32,256]{3,2,1,0:T(8,128)(2,1)S(1)}, bf16[1,2,32,256]{3,2,1,0:T(8,128)(2,1)S(1)}, u32[]{:S(2)}, u32[]{:S(2)}) collective-permute-start(bf16[1,2,32,256]{3,2,1,0:T(8,128)(2,1)S(1)} %shard_map.69), channel_id=1, source_target_pairs={{0,8},{1,9},{2,10},{3,11},{4,12},{5,13},{6,14},{7,15},{8,0},{9,1},... | collective-permute-start | bytes 98312 | tf_op jit(solution)/shard_map/ppermute | solution.py:21
  5.5 14.1 %collective-permute-start.4 = (bf16[1,512,256]{2,1,0:T(8,128)(2,1)}, bf16[1,512,256]{2,1,0:T(8,128)(2,1)S(1)}, u32[]{:S(2)}, u32[]{:S(2)}) collective-permute-start(bf16[1,512,256]{2,1,0:T(8,128)(2,1)} %bitcast.20), channel_id=1, source_target_pairs={{0,16},{16,0},{1,17},{17,1},{2,18},{18,2},{3,19},{19,3},{4,20},{20... | collective-permute-start | bytes 786440 | tf_op jit(solution)/shard_map/ppermute | solution.py:21
  7.0 9.1 %copy-start = (s32[4,8]{1,0:T(4,128)S(1)}, s32[4,8]{1,0:T(4,128)}, u32[]{:S(2)}) copy-start(s32[4,8]{1,0:T(4,128)} %mask.1) | copy-start | bytes 388
  7.0 12.6 %collective-permute-start.5 = (bf16[1,512,256]{2,1,0:T(8,128)(2,1)}, bf16[1,512,256]{2,1,0:T(8,128)(2,1)S(1)}, u32[]{:S(2)}, u32[]{:S(2)}) collective-permute-start(bf16[1,512,256]{2,1,0:T(8,128)(2,1)} %bitcast.22), channel_id=1, source_target_pairs={{0,16},{16,0},{1,17},{17,1},{2,18},{18,2},{3,19},{19,3},{4,20},{20... | collective-permute-start | bytes 786440 | tf_op jit(solution)/shard_map/ppermute | solution.py:21
  7.8 3.2 %collective-permute-start.6 = (bf16[2,2,32,256]{3,2,1,0:T(8,128)(2,1)S(1)}, bf16[2,2,32,256]{3,2,1,0:T(8,128)(2,1)S(1)}, u32[]{:S(2)}, u32[]{:S(2)}) collective-permute-start(bf16[2,2,32,256]{3,2,1,0:T(8,128)(2,1)S(1)} %pad_maximum_fusion.refs_1_), channel_id=1, source_target_pairs={{0,1},{1,0},{2,3},{3,2},{4,5},{5,4},{6,7},{7,6},{8,9},{9,8},{10,11... | collective-permute-start | bytes 196616 | tf_op jit(solution)/shard_map/ppermute | solution.py:21
  7.9 4.5 %collective-permute-start.2 = (bf16[2,2,32,256]{3,2,1,0:T(8,128)(2,1)S(1)}, bf16[2,2,32,256]{3,2,1,0:T(8,128)(2,1)S(1)}, u32[]{:S(2)}, u32[]{:S(2)}) collective-permute-start(bf16[2,2,32,256]{3,2,1,0:T(8,128)(2,1)S(1)} %pad_maximum_fusion.refs_1_), channel_id=1, source_target_pairs={{0,4},{1,5},{2,6},{3,7},{4,0},{5,1},{6,2},{7,3},{8,12},{9,13},{10,... | collective-permute-start | bytes 196616 | tf_op jit(solution)/shard_map/ppermute | solution.py:21
  9.5 4.3 %collective-permute-start.1 = (bf16[2,2,32,256]{3,2,1,0:T(8,128)(2,1)S(1)}, bf16[2,2,32,256]{3,2,1,0:T(8,128)(2,1)S(1)}, u32[]{:S(2)}, u32[]{:S(2)}) collective-permute-start(bf16[2,2,32,256]{3,2,1,0:T(8,128)(2,1)S(1)} %pad_maximum_fusion.refs_1_), channel_id=1, source_target_pairs={{0,2},{1,3},{2,0},{3,1},{4,6},{5,7},{6,4},{7,5},{8,10},{9,11},{10,... | collective-permute-start | bytes 196616 | tf_op jit(solution)/shard_map/ppermute | solution.py:21
  11.0 5.2 %collective-permute-start.3 = (bf16[2,2,32,256]{3,2,1,0:T(8,128)(2,1)S(1)}, bf16[2,2,32,256]{3,2,1,0:T(8,128)(2,1)S(1)}, u32[]{:S(2)}, u32[]{:S(2)}) collective-permute-start(bf16[2,2,32,256]{3,2,1,0:T(8,128)(2,1)S(1)} %pad_maximum_fusion.refs_1_), channel_id=1, source_target_pairs={{0,6},{1,7},{2,4},{3,5},{4,2},{5,3},{6,0},{7,1},{8,14},{9,15},{10,... | collective-permute-start | bytes 196616 | tf_op jit(solution)/shard_map/ppermute | solution.py:21
  12.4 6.0 %collective-permute-start.8 = (bf16[2,2,32,256]{3,2,1,0:T(8,128)(2,1)S(1)}, bf16[2,2,32,256]{3,2,1,0:T(8,128)(2,1)S(1)}, u32[]{:S(2)}, u32[]{:S(2)}) collective-permute-start(bf16[2,2,32,256]{3,2,1,0:T(8,128)(2,1)S(1)} %collective-permute-done.2.refs_3_), channel_id=1, source_target_pairs={{0,1},{1,0},{2,3},{3,2},{4,5},{5,4},{6,7},{7,6},{8,9},{9,8},{10,11... | collective-permute-start | bytes 196616 | tf_op jit(solution)/shard_map/ppermute | solution.py:21
  13.7 4.6 %collective-permute-start.7 = (bf16[2,2,32,256]{3,2,1,0:T(8,128)(2,1)S(1)}, bf16[2,2,32,256]{3,2,1,0:T(8,128)(2,1)S(1)}, u32[]{:S(2)}, u32[]{:S(2)}) collective-permute-start(bf16[2,2,32,256]{3,2,1,0:T(8,128)(2,1)S(1)} %collective-permute-done.1.refs_1_.refs_2_), channel_id=1, source_target_pairs={{0,1},{1,0},{2,3},{3,2},{4,5},{5,4},{6,7},{7,6},{8,9},{9,8},{10,11... | collective-permute-start | bytes 196616 | tf_op jit(solution)/shard_map/ppermute | solution.py:21
  16.1 2.9 %collective-permute-start.9 = (bf16[2,2,32,256]{3,2,1,0:T(8,128)(2,1)S(1)}, bf16[2,2,32,256]{3,2,1,0:T(8,128)(2,1)S(1)}, u32[]{:S(2)}, u32[]{:S(2)}) collective-permute-start(bf16[2,2,32,256]{3,2,1,0:T(8,128)(2,1)S(1)} %collective-permute-done.3.refs_1_.refs_4_), channel_id=1, source_target_pairs={{0,1},{1,0},{2,3},{3,2},{4,5},{5,4},{6,7},{7,6},{8,9},{9,8},{10,11... | collective-permute-start | bytes 196616 | tf_op jit(solution)/shard_map/ppermute | solution.py:21
  20.4 1.7 %collective-permute-start.10 = (f32[4,2,32,256]{3,2,1,0:T(8,128)S(1)}, f32[4,2,32,256]{3,2,1,0:T(8,128)S(1)}, u32[]{:S(2)}, u32[]{:S(2)}) collective-permute-start(f32[4,2,32,256]{3,2,1,0:T(8,128)S(1)} %get-tuple-element.25), channel_id=1, source_target_pairs={{0,1},{1,0},{2,3},{3,2},{4,5},{5,4},{6,7},{7,6},{8,9},{9,8},{10,11... | collective-permute-start | bytes 786440 | tf_op jit(solution)/shard_map/ppermute | solution.py:21
  22.2 5.3 %collective-permute-start.11 = (f32[2,32,256]{2,1,0:T(8,128)S(1)}, f32[2,32,256]{2,1,0:T(8,128)S(1)}, u32[]{:S(2)}, u32[]{:S(2)}) collective-permute-start(f32[2,32,256]{2,1,0:T(8,128)S(1)} %get-tuple-element.28), channel_id=1, source_target_pairs={{0,2},{1,3},{2,0},{3,1},{4,6},{5,7},{6,4},{7,5},{8,10},{9,11},{10,... | collective-permute-start | bytes 196616 | tf_op jit(solution)/shard_map/ppermute | solution.py:21
  23.1 5.7 %collective-permute-start.13 = (f32[2,32,256]{2,1,0:T(8,128)S(1)}, f32[2,32,256]{2,1,0:T(8,128)S(1)}, u32[]{:S(2)}, u32[]{:S(2)}) collective-permute-start(f32[2,32,256]{2,1,0:T(8,128)S(1)} %get-tuple-element.29), channel_id=1, source_target_pairs={{0,6},{1,7},{2,4},{3,5},{4,2},{5,3},{6,0},{7,1},{8,14},{9,15},{10,... | collective-permute-start | bytes 196616 | tf_op jit(solution)/shard_map/ppermute | solution.py:21
  24.6 4.6 %collective-permute-start.12 = (f32[2,32,256]{2,1,0:T(8,128)S(1)}, f32[2,32,256]{2,1,0:T(8,128)S(1)}, u32[]{:S(2)}, u32[]{:S(2)}) collective-permute-start(f32[2,32,256]{2,1,0:T(8,128)S(1)} %get-tuple-element.30), channel_id=1, source_target_pairs={{0,4},{1,5},{2,6},{3,7},{4,0},{5,1},{6,2},{7,3},{8,12},{9,13},{10,... | collective-permute-start | bytes 196616 | tf_op jit(solution)/shard_map/ppermute | solution.py:21
  25.9 8.0 %collective-permute-start.15 = (s16[1,528,256]{2,1,0:T(8,128)(2,1)S(1)}, s16[1,528,256]{2,1,0:T(8,128)(2,1)S(1)}, u32[]{:S(2)}, u32[]{:S(2)}) collective-permute-start(s16[1,528,256]{2,1,0:T(8,128)(2,1)S(1)} %shard_map.75), channel_id=1, source_target_pairs={{0,16},{16,0},{1,17},{17,1},{2,18},{18,2},{3,19},{19,3},{4,20},{20... | collective-permute-start | bytes 811016 | tf_op jit(solution)/shard_map/ppermute | solution.py:21
  29.2 5.5 %collective-permute-start.14 = (f32[1,32,256]{2,1,0:T(8,128)S(1)}, f32[1,32,256]{2,1,0:T(8,128)S(1)}, u32[]{:S(2)}, u32[]{:S(2)}) collective-permute-start(f32[1,32,256]{2,1,0:T(8,128)S(1)} %slice.29), channel_id=1, source_target_pairs={{0,8},{1,9},{2,10},{3,11},{4,12},{5,13},{6,14},{7,15},{8,0},{9,1},... | collective-permute-start | bytes 98312 | tf_op jit(solution)/shard_map/ppermute | solution.py:21

commit v5 on v4

--- a/solution.py
+++ b/solution.py
@@ -210,18 +210,31 @@
 GROUPS = 16
 
 
+def encode_rows(x, out_ref, k):
+    rows = x.shape[0]
+    groups = min(GROUPS, rows // GROUPS)
+    step = rows // groups
+    exps = []
+    for g in range(groups):
+        part = x[g * step : (g + 1) * step]
+        top = jnp.max(jnp.abs(part), 0, keepdims=True)
+        e = 14.0 - jnp.ceil(jnp.log2(jnp.maximum(top, 1e-30)))
+        out_ref[k, pl.ds(g * step, step), :] = jnp.round(part * jnp.exp2(e)).astype(jnp.int32).astype(jnp.int16)
+        exps.append(e)
+    exps += exps[-1:] * (GROUPS - groups)
+    out_ref[k, pl.ds(rows, GROUPS), :] = jnp.concatenate(exps, 0).astype(jnp.int32).astype(jnp.int16)
+
+
+def decode_rows(q_ref, k, g, groups):
+    rows = q_ref.shape[1] - GROUPS
+    step = rows // groups
+    unit = jnp.exp2(-q_ref[k, pl.ds(rows, GROUPS), :].astype(jnp.int32).astype(f32))
+    return q_ref[k, pl.ds(g * step, step), :].astype(jnp.int32).astype(f32) * unit[g : g + 1]
+
+
 def encode_kernel(x_ref, out_ref):
-    n, rows, _ = x_ref.shape
-    step = rows // GROUPS
-    for k in range(n):
-        exps = []
-        for g in range(GROUPS):
-            x = x_ref[k, pl.ds(g * step, step), :]
-            top = jnp.max(jnp.abs(x), 0, keepdims=True)
-            e = 14.0 - jnp.ceil(jnp.log2(jnp.maximum(top, 1e-30)))
-            out_ref[k, pl.ds(g * step, step), :] = jnp.round(x * jnp.exp2(e)).astype(jnp.int32).astype(jnp.int16)
-            exps.append(e)
-        out_ref[k, pl.ds(rows, GROUPS), :] = jnp.concatenate(exps, 0).astype(jnp.int32).astype(jnp.int16)
+    for k in range(x_ref.shape[0]):
+        encode_rows(x_ref[k], out_ref, k)
 
 
 def encode(x):
@@ -237,12 +250,12 @@
 
 def decode_kernel(x_ref, q_ref, out_ref, *, at):
     n, rows, _ = x_ref.shape
-    step = rows // GROUPS
+    groups = min(GROUPS, rows // GROUPS)
+    step = rows // groups
     for k in range(n):
-        unit = jnp.exp2(-q_ref[at + k, pl.ds(rows, GROUPS), :].astype(jnp.int32).astype(f32))
-        for g in range(GROUPS):
+        for g in range(groups):
             part = pl.ds(g * step, step)
-            out_ref[k, part, :] = x_ref[k, part, :] + q_ref[at + k, part, :].astype(jnp.int32).astype(f32) * unit[g : g + 1]
+            out_ref[k, part, :] = x_ref[k, part, :] + decode_rows(q_ref, at + k, g, groups)
 
 
 def add_decoded(x, q, at):
@@ -253,6 +266,51 @@
         out_shape=jax.ShapeDtypeStruct(x.shape, f32),
         compiler_params=PARAMS,
     )(in_vmem(x), in_vmem(q))
+
+
+def fold_kernel(mine, core_in, own, *coded):
+    n, n_a, us, width = mine.shape
+    own[0] = (mine[0] + core_in[0]).reshape(n_a * us, width)
+    for i in range(1, n):
+        encode_rows((mine[i] + core_in[i]).reshape(n_a * us, width), coded[i - 1], 0)
+
+
+def fold(mine, core_in):
+    n, n_a, us, width = mine.shape
+    rows = n_a * us
+    return pl.pallas_call(
+        fold_kernel,
+        in_specs=[VM, VM],
+        out_specs=[VM] * n,
+        out_shape=[pltpu.VMEM((1, rows, width), f32)]
+        + [pltpu.VMEM((1, rows + GROUPS, width), jnp.int16)] * (n - 1),
+        compiler_params=PARAMS,
+    )(in_vmem(mine), in_vmem(core_in))
+
+
+def near_kernel(own, *refs):
+    *coded, keep, send = refs
+    rows = own.shape[1]
+    half = rows // 2
+    groups = min(GROUPS, rows // GROUPS)
+    step = rows // groups
+    for g in range(groups):
+        x = own[0, pl.ds(g * step, step), :]
+        for q in coded:
+            x = x + decode_rows(q, 0, g, groups)
+        to, at = (keep, g * step) if g * step < half else (send, g * step - half)
+        to[pl.ds(at, step), :] = x
+
+
+def near_sum(own, coded):
+    _, rows, width = own.shape
+    return pl.pallas_call(
+        near_kernel,
+        in_specs=[VM] * (1 + len(coded)),
+        out_specs=[VM] * 2,
+        out_shape=[pltpu.VMEM((rows // 2, width), f32)] * 2,
+        compiler_params=PARAMS,
+    )(*[in_vmem(x) for x in (own, *coded)])
 
 
 def on_device(user_factors, item_factors, user_tangent, item_tangent, block_mask, n_au, n_ia):
@@ -306,13 +364,14 @@
         sums = [out_mine, out_other]
         at_mine, at_other = [(0, i) for i in range(4)], [(1, i) for i in range(4)]
 
-    keep = out_mine + swap(out_other, "ia", n_ia, core)
-    acc = keep[0]
-    for n, b in enumerate(near[1:]):
-        acc = acc + swap(keep[n + 1], "ia", n_ia, b)
-    for bit in a_bits[::-1]:
-        half = acc.shape[0] // 2
-        acc = acc[:half] + swap(acc[half:], "ia", n_ia, bit)
+    own, *coded = fold(out_mine, swap(out_other, "ia", n_ia, core))
+    coded = [swap(q, "ia", n_ia, b) for q, b in zip(coded, near[1:])]
+    acc, send = near_sum(own, coded)
+    for n, bit in enumerate(a_bits[::-1]):
+        if n:
+            half = acc.shape[0] // 2
+            acc, send = acc[:half], acc[half:]
+        acc = acc + swap(send, "ia", n_ia, bit)
     user_product = acc.reshape(us, width)
 
     for bit in item_bits[::-1]:

time: 35.7 us -> 36.7 us (1.028)
  waiting for transfers between devices: 8.66 us -> 10.5 us
  starting transfers between devices: 18.6 us -> 17.7 us
    ppermute x16, waiting for transfers between devices: 8.66 us -> 10.5 us  [swap(): return lax.ppermute(x, axis, [(i, i ^ bits) for i in range(size)])]
    ppermute x16, starting transfers between devices: 18.6 us -> 17.7 us  [swap(): return lax.ppermute(x, axis, [(i, i ^ bits) for i in range(size)])]
    reshape x1 -> x0, other arithmetic: 0.62 us -> none  [on_device(): user_product = acc.reshape(us, width)]
    add x2 -> x1, other arithmetic: 0.05 us -> 0.62 us  [on_device(): acc = acc + swap(send, 'ia', n_ia, bit)]
where the time goes in v5:
time: 36.7 us; the launch traced here: 36.4 us
  starting transfers between devices  17.7 us (48%)
  waiting for transfers between devices  10.5 us (29%)
  Pallas kernels  6.79 us (19%)
  between operations  0.76 us (2%)
  other arithmetic  0.63 us (2%)
    ppermute x16, starting transfers between devices, swap(): return lax.ppermute(x, axis, [(i, i ^ bits) for i in range(size)])  17.7 us
    ppermute x16, waiting for transfers between devices, swap(): return lax.ppermute(x, axis, [(i, i ^ bits) for i in range(size)])  10.5 us
    pallas_call x5, Pallas kernels, region(): pl.pallas_call(functools.partial(region_kernel, n_users=len(users), sums_...  3.31 us
    pallas_call x1, Pallas kernels, load(): pl.pallas_call(functools.partial(load_kernel, **static), in_specs=[pl.Blo...  1.61 us
    pallas_call x1, Pallas kernels, add_decoded(): pl.pallas_call(functools.partial(decode_kernel, at=at), in_specs=[VM, VM]...  0.87 us
    pallas_call x1, Pallas kernels, stack(): pl.pallas_call(stack_kernel, in_specs=[pl.BlockSpec(memory_space=pltpu.HB...  0.75 us
  transfers between devices with their start and end apart: 16, of which 8 were waited for; matrix products, arithmetic and copies ran while one was open for 0% of the time, Pallas kernels for 15%

profile of v5, /device:TPU:0, one launch (start us, length us, event | category | flops | bytes accessed | tf_op | source)
XLA Modules:
  0.0 36.4 jit_solution(10315571243725505812)
XLA Ops:
  0.6 0.8 %shard_map.69 = bf16[1,2,32,256]{3,2,1,0:T(8,128)(2,1)S(1)} custom-call(bf16[32,256]{1,0:T(8,128)(2,1)} %a.1, bf16[32,256]{1,0:T(8,128)(2,1)} %b.1), custom_call_target="tpu_custom_call" | custom-call | tf_op jit(solution)/shard_map/pallas_call | solution.py:200
  1.4 4.1 %collective-permute-start = (bf16[1,2,32,256]{3,2,1,0:T(8,128)(2,1)S(1)}, bf16[1,2,32,256]{3,2,1,0:T(8,128)(2,1)S(1)}, u32[]{:S(2)}, u32[]{:S(2)}) collective-permute-start(bf16[1,2,32,256]{3,2,1,0:T(8,128)(2,1)S(1)} %shard_map.69), channel_id=1, source_target_pairs={{0,8},{1,9},{2,10},{3,11},{4,12},{5,13},{6,14},{7,15},{8,0},{9,1},... | collective-permute-start | bytes 98312 | tf_op jit(solution)/shard_map/ppermute | solution.py:21
  5.5 1.5 %collective-permute-start.4 = (bf16[1,512,256]{2,1,0:T(8,128)(2,1)}, bf16[1,512,256]{2,1,0:T(8,128)(2,1)S(1)}, u32[]{:S(2)}, u32[]{:S(2)}) collective-permute-start(bf16[1,512,256]{2,1,0:T(8,128)(2,1)} %bitcast.4), channel_id=1, source_target_pairs={{0,16},{16,0},{1,17},{17,1},{2,18},{18,2},{3,19},{19,3},{4,20},{20... | collective-permute-start | bytes 786440 | tf_op jit(solution)/shard_map/ppermute | solution.py:21
  7.0 0.0 copy-start
  7.0 0.5 %collective-permute-start.5 = (bf16[1,512,256]{2,1,0:T(8,128)(2,1)}, bf16[1,512,256]{2,1,0:T(8,128)(2,1)S(1)}, u32[]{:S(2)}, u32[]{:S(2)}) collective-permute-start(bf16[1,512,256]{2,1,0:T(8,128)(2,1)} %bitcast.6), channel_id=1, source_target_pairs={{0,16},{16,0},{1,17},{17,1},{2,18},{18,2},{3,19},{19,3},{4,20},{20... | collective-permute-start | bytes 786440 | tf_op jit(solution)/shard_map/ppermute | solution.py:21
  7.5 0.2 collective-permute-done
  7.8 0.1 collective-permute-start.6
  7.9 1.6 %collective-permute-start.2 = (bf16[2,2,32,256]{3,2,1,0:T(8,128)(2,1)S(1)}, bf16[2,2,32,256]{3,2,1,0:T(8,128)(2,1)S(1)}, u32[]{:S(2)}, u32[]{:S(2)}) collective-permute-start(bf16[2,2,32,256]{3,2,1,0:T(8,128)(2,1)S(1)} %pad_maximum_fusion.refs_1_), channel_id=1, source_target_pairs={{0,4},{1,5},{2,6},{3,7},{4,0},{5,1},{6,2},{7,3},{8,12},{9,13},{10,... | collective-permute-start | bytes 196616 | tf_op jit(solution)/shard_map/ppermute | solution.py:21
  9.5 1.5 %collective-permute-start.1 = (bf16[2,2,32,256]{3,2,1,0:T(8,128)(2,1)S(1)}, bf16[2,2,32,256]{3,2,1,0:T(8,128)(2,1)S(1)}, u32[]{:S(2)}, u32[]{:S(2)}) collective-permute-start(bf16[2,2,32,256]{3,2,1,0:T(8,128)(2,1)S(1)} %pad_maximum_fusion.refs_1_), channel_id=1, source_target_pairs={{0,2},{1,3},{2,0},{3,1},{4,6},{5,7},{6,4},{7,5},{8,10},{9,11},{10,... | collective-permute-start | bytes 196616 | tf_op jit(solution)/shard_map/ppermute | solution.py:21
  11.0 0.0 collective-permute-done.6.refs_2_.refs_1_
  11.0 0.6 %collective-permute-start.3 = (bf16[2,2,32,256]{3,2,1,0:T(8,128)(2,1)S(1)}, bf16[2,2,32,256]{3,2,1,0:T(8,128)(2,1)S(1)}, u32[]{:S(2)}, u32[]{:S(2)}) collective-permute-start(bf16[2,2,32,256]{3,2,1,0:T(8,128)(2,1)S(1)} %pad_maximum_fusion.refs_1_), channel_id=1, source_target_pairs={{0,6},{1,7},{2,4},{3,5},{4,2},{5,3},{6,0},{7,1},{8,14},{9,15},{10,... | collective-permute-start | bytes 196616 | tf_op jit(solution)/shard_map/ppermute | solution.py:21
  11.6 0.8 %collective-permute-done.2.refs_3_ = bf16[2,2,32,256]{3,2,1,0:T(8,128)(2,1)S(1)} collective-permute-done((bf16[2,2,32,256]{3,2,1,0:T(8,128)(2,1)S(1)}, bf16[2,2,32,256]{3,2,1,0:T(8,128)(2,1)S(1)}, u32[]{:S(2)}, u32[]{:S(2)}) %collective-permute-start.2) | collective-permute-done | bytes 65568 | tf_op jit(solution)/shard_map/ppermute | solution.py:21
  12.4 0.0 collective-permute-start.8
  12.4 1.4 %collective-permute-done.1.refs_1_.refs_2_ = bf16[2,2,32,256]{3,2,1,0:T(8,128)(2,1)S(1)} collective-permute-done((bf16[2,2,32,256]{3,2,1,0:T(8,128)(2,1)S(1)}, bf16[2,2,32,256]{3,2,1,0:T(8,128)(2,1)S(1)}, u32[]{:S(2)}, u32[]{:S(2)}) %collective-permute-start.1) | collective-permute-done | bytes 65568 | tf_op jit(solution)/shard_map/ppermute | solution.py:21
  13.7 0.0 collective-permute-start.7
  13.7 2.4 %collective-permute-done.3.refs_1_.refs_4_ = bf16[2,2,32,256]{3,2,1,0:T(8,128)(2,1)S(1)} collective-permute-done((bf16[2,2,32,256]{3,2,1,0:T(8,128)(2,1)S(1)}, bf16[2,2,32,256]{3,2,1,0:T(8,128)(2,1)S(1)}, u32[]{:S(2)}, u32[]{:S(2)}) %collective-permute-start.3) | collective-permute-done | bytes 65568 | tf_op jit(solution)/shard_map/ppermute | solution.py:21
  16.1 0.0 collective-permute-start.9
  16.1 0.0 copy-done
  16.1 1.6 %shard_map.68 = (bf16[1,512,256]{2,1,0:T(8,128)(2,1)S(1)}, bf16[1,512,256]{2,1,0:T(8,128)(2,1)S(1)}, f32[8,256]{1,0:T(8,128)S(1)}) custom-call(s32[4,8]{1,0:T(4,128)S(1)} %copy-done, bf16[1,512,256]{2,1,0:T(8,128)(2,1)} %bitcast.5, bf16[1,512,256]{2,1,0:T(8,128)(2,1)} %bitcast.7), custom_call_target="tpu_custom_call" | custom-call | tf_op jit(solution)/shard_map/pallas_call | solution.py:178
  17.8 0.6 %shard_map.70 = (f32[2,2,32,256]{3,2,1,0:T(8,128)S(1)}, f32[1,512,256]{2,1,0:T(8,128)S(1)}) custom-call(f32[8,256]{1,0:T(8,128)S(1)} %get-tuple-element.21.refs_0_, bf16[2,2,32,256]{3,2,1,0:T(8,128)(2,1)S(1)} %pad_maximum_fusion.refs_1_, bf16[2,2,32,256]{3,2,1,0:T(8,128)(2,1)S(1)} %collective-permute-done.6.refs_2_.refs_1_, ...), custom_call_target="tpu_custom_call" | custom-call | tf_op jit(solution)/shard_map/pallas_call | solution.py:126
  18.3 0.0 collective-permute-done.8.refs_4_.refs_3_
  18.3 0.0 collective-permute-done.7.refs_2_
  18.4 0.7 %shard_map.71 = (f32[4,2,32,256]{3,2,1,0:T(8,128)S(1)}, f32[1,512,256]{2,1,0:T(8,128)S(1)}) custom-call(f32[8,256]{1,0:T(8,128)S(1)} %get-tuple-element.21.refs_0_, bf16[2,2,32,256]{3,2,1,0:T(8,128)(2,1)S(1)} %collective-permute-done.1.refs_1_.refs_2_, bf16[2,2,32,256]{3,2,1,0:T(8,128)(2,1)S(1)} %collective-permute-done.7.refs_2_, ...), custom_call_target="tpu_custom_call", output_to_operand_aliasing={{1}: (7, {})} | custom-call | tf_op jit(solution)/shard_map/pallas_call | solution.py:126
  19.1 0.0 collective-permute-done.9.refs_2_.refs_4_
  19.1 0.6 %shard_map.72 = (f32[2,2,32,256]{3,2,1,0:T(8,128)S(1)}, f32[1,512,256]{2,1,0:T(8,128)S(1)}) custom-call(f32[8,256]{1,0:T(8,128)S(1)} %get-tuple-element.21.refs_0_, bf16[2,2,32,256]{3,2,1,0:T(8,128)(2,1)S(1)} %collective-permute-done.3.refs_1_.refs_4_, ...), custom_call_target="tpu_custom_call", output_to_operand_aliasing={{1}: (5, {})} | custom-call | tf_op jit(solution)/shard_map/pallas_call | solution.py:126
  19.7 0.0 collective-permute-done.4.refs_5_
  19.7 0.0 collective-permute-done.5.refs_6_
  19.7 0.7 %shard_map.73 = (f32[4,2,32,256]{3,2,1,0:T(8,128)S(1)}, f32[1,512,256]{2,1,0:T(8,128)S(1)}) custom-call(f32[8,256]{1,0:T(8,128)S(1)} %get-tuple-element.21.refs_0_, bf16[2,2,32,256]{3,2,1,0:T(8,128)(2,1)S(1)} %collective-permute-done.6.refs_2_.refs_1_, bf16[2,2,32,256]{3,2,1,0:T(8,128)(2,1)S(1)} %collective-permute-done.7.refs_2_, ...), custom_call_target="tpu_custom_call" | custom-call | tf_op jit(solution)/shard_map/pallas_call | solution.py:126
  20.4 0.5 %collective-permute-start.10 = (f32[4,2,32,256]{3,2,1,0:T(8,128)S(1)}, f32[4,2,32,256]{3,2,1,0:T(8,128)S(1)}, u32[]{:S(2)}, u32[]{:S(2)}) collective-permute-start(f32[4,2,32,256]{3,2,1,0:T(8,128)S(1)} %get-tuple-element.31), channel_id=1, source_target_pairs={{0,1},{1,0},{2,3},{3,2},{4,5},{5,4},{6,7},{7,6},{8,9},{9,8},{10,11... | collective-permute-start | bytes 786440 | tf_op jit(solution)/shard_map/ppermute | solution.py:21
  21.0 0.7 %shard_map.74 = (f32[4,2,32,256]{3,2,1,0:T(8,128)S(1)}, f32[1,512,256]{2,1,0:T(8,128)S(1)}) custom-call(f32[8,256]{1,0:T(8,128)S(1)} %get-tuple-element.21.refs_0_, bf16[2,2,32,256]{3,2,1,0:T(8,128)(2,1)S(1)} %pad_maximum_fusion.refs_1_, bf16[2,2,32,256]{3,2,1,0:T(8,128)(2,1)S(1)} %collective-permute-done.1.refs_1_.refs_2_, ...), custom_call_target="tpu_custom_call", output_to_operand_aliasing={{1}: (10, {})} | custom-call | tf_op jit(solution)/shard_map/pallas_call | solution.py:126
  21.7 0.1 shard_map.77
  21.8 1.6 %collective-permute-start.15 = (s16[1,528,256]{2,1,0:T(8,128)(2,1)S(1)}, s16[1,528,256]{2,1,0:T(8,128)(2,1)S(1)}, u32[]{:S(2)}, u32[]{:S(2)}) collective-permute-start(s16[1,528,256]{2,1,0:T(8,128)(2,1)S(1)} %shard_map.77), channel_id=1, source_target_pairs={{0,16},{16,0},{1,17},{17,1},{2,18},{18,2},{3,19},{19,3},{4,20},{20... | collective-permute-start | bytes 811016 | tf_op jit(solution)/shard_map/ppermute | solution.py:21
  23.4 0.0 collective-permute-done.10.core_in
  23.4 0.1 shard_map.75
  23.5 0.6 %collective-permute-start.11 = (s16[1,80,256]{2,1,0:T(8,128)(2,1)S(1)}, s16[1,80,256]{2,1,0:T(8,128)(2,1)S(1)}, u32[]{:S(2)}, u32[]{:S(2)}) collective-permute-start(s16[1,80,256]{2,1,0:T(8,128)(2,1)S(1)} %get-tuple-element.33), channel_id=1, source_target_pairs={{0,2},{1,3},{2,0},{3,1},{4,6},{5,7},{6,4},{7,5},{8,10},{9,11},{10,... | collective-permute-start | bytes 122888 | tf_op jit(solution)/shard_map/ppermute | solution.py:21
  24.1 1.5 %collective-permute-start.12 = (s16[1,80,256]{2,1,0:T(8,128)(2,1)S(1)}, s16[1,80,256]{2,1,0:T(8,128)(2,1)S(1)}, u32[]{:S(2)}, u32[]{:S(2)}) collective-permute-start(s16[1,80,256]{2,1,0:T(8,128)(2,1)S(1)} %get-tuple-element.34), channel_id=1, source_target_pairs={{0,4},{1,5},{2,6},{3,7},{4,0},{5,1},{6,2},{7,3},{8,12},{9,13},{10,... | collective-permute-start | bytes 122888 | tf_op jit(solution)/shard_map/ppermute | solution.py:21
  25.6 1.5 %collective-permute-start.13 = (s16[1,80,256]{2,1,0:T(8,128)(2,1)S(1)}, s16[1,80,256]{2,1,0:T(8,128)(2,1)S(1)}, u32[]{:S(2)}, u32[]{:S(2)}) collective-permute-start(s16[1,80,256]{2,1,0:T(8,128)(2,1)S(1)} %get-tuple-element.35), channel_id=1, source_target_pairs={{0,6},{1,7},{2,4},{3,5},{4,2},{5,3},{6,0},{7,1},{8,14},{9,15},{10,... | collective-permute-start | bytes 122888 | tf_op jit(solution)/shard_map/ppermute | solution.py:21
  27.1 0.5 %collective-permute-done.11.refs_0_ = s16[1,80,256]{2,1,0:T(8,128)(2,1)S(1)} collective-permute-done((s16[1,80,256]{2,1,0:T(8,128)(2,1)S(1)}, s16[1,80,256]{2,1,0:T(8,128)(2,1)S(1)}, u32[]{:S(2)}, u32[]{:S(2)}) %collective-permute-start.11) | collective-permute-done | bytes 40992 | tf_op jit(solution)/shard_map/ppermute | solution.py:21
  27.6 0.8 %collective-permute-done.12.refs_1_ = s16[1,80,256]{2,1,0:T(8,128)(2,1)S(1)} collective-permute-done((s16[1,80,256]{2,1,0:T(8,128)(2,1)S(1)}, s16[1,80,256]{2,1,0:T(8,128)(2,1)S(1)}, u32[]{:S(2)}, u32[]{:S(2)}) %collective-permute-start.12) | collective-permute-done | bytes 40992 | tf_op jit(solution)/shard_map/ppermute | solution.py:21
  28.4 2.1 %collective-permute-done.13.refs_2_ = s16[1,80,256]{2,1,0:T(8,128)(2,1)S(1)} collective-permute-done((s16[1,80,256]{2,1,0:T(8,128)(2,1)S(1)}, s16[1,80,256]{2,1,0:T(8,128)(2,1)S(1)}, u32[]{:S(2)}, u32[]{:S(2)}) %collective-permute-start.13) | collective-permute-done | bytes 40992 | tf_op jit(solution)/shard_map/ppermute | solution.py:21
  30.5 2.1 %collective-permute-start.14 = (f32[32,256]{1,0:T(8,128)S(1)}, f32[32,256]{1,0:T(8,128)S(1)}, u32[]{:S(2)}, u32[]{:S(2)}) collective-permute-start(f32[32,256]{1,0:T(8,128)S(1)} %get-tuple-element.37), channel_id=1, source_target_pairs={{0,8},{1,9},{2,10},{3,11},{4,12},{5,13},{6,14},{7,15},{8,0},{9,1},... | collective-permute-start | bytes 98312 | tf_op jit(solution)/shard_map/ppermute | solution.py:21
  32.6 0.0 collective-permute-done.15.q_ref
  32.6 0.9 %shard_map.78 = f32[1,512,256]{2,1,0:T(8,128)} custom-call(f32[1,512,256]{2,1,0:T(8,128)S(1)} %get-tuple-element.38.x_ref, s16[1,528,256]{2,1,0:T(8,128)(2,1)S(1)} %collective-permute-done.15.q_ref), custom_call_target="tpu_custom_call" | custom-call | tf_op jit(solution)/shard_map/pallas_call | solution.py:262
  33.5 2.3 %collective-permute-done.14 = f32[32,256]{1,0:T(8,128)S(1)} collective-permute-done((f32[32,256]{1,0:T(8,128)S(1)}, f32[32,256]{1,0:T(8,128)S(1)}, u32[]{:S(2)}, u32[]{:S(2)}) %collective-permute-start.14) | collective-permute-done | bytes 32800 | tf_op jit(solution)/shard_map/ppermute | solution.py:21
  35.8 0.6 %add.3 = f32[32,256]{1,0:T(8,128)} add(f32[32,256]{1,0:T(8,128)S(1)} %get-tuple-element.36, f32[32,256]{1,0:T(8,128)S(1)} %collective-permute-done.14) | non-fusion elementwise | flops 8192 | bytes 98304 | tf_op jit(solution)/shard_map/add | solution.py:374
  (2 shorter events, 0.0 us)
Async XLA Ops:
  1.4 6.4 %collective-permute-start = (bf16[1,2,32,256]{3,2,1,0:T(8,128)(2,1)S(1)}, bf16[1,2,32,256]{3,2,1,0:T(8,128)(2,1)S(1)}, u32[]{:S(2)}, u32[]{:S(2)}) collective-permute-start(bf16[1,2,32,256]{3,2,1,0:T(8,128)(2,1)S(1)} %shard_map.69), channel_id=1, source_target_pairs={{0,8},{1,9},{2,10},{3,11},{4,12},{5,13},{6,14},{7,15},{8,0},{9,1},... | collective-permute-start | bytes 98312 | tf_op jit(solution)/shard_map/ppermute | solution.py:21
  5.5 14.1 %collective-permute-start.4 = (bf16[1,512,256]{2,1,0:T(8,128)(2,1)}, bf16[1,512,256]{2,1,0:T(8,128)(2,1)S(1)}, u32[]{:S(2)}, u32[]{:S(2)}) collective-permute-start(bf16[1,512,256]{2,1,0:T(8,128)(2,1)} %bitcast.4), channel_id=1, source_target_pairs={{0,16},{16,0},{1,17},{17,1},{2,18},{18,2},{3,19},{19,3},{4,20},{20... | collective-permute-start | bytes 786440 | tf_op jit(solution)/shard_map/ppermute | solution.py:21
  7.0 9.1 %copy-start = (s32[4,8]{1,0:T(4,128)S(1)}, s32[4,8]{1,0:T(4,128)}, u32[]{:S(2)}) copy-start(s32[4,8]{1,0:T(4,128)} %mask.1) | copy-start | bytes 388
  7.0 12.6 %collective-permute-start.5 = (bf16[1,512,256]{2,1,0:T(8,128)(2,1)}, bf16[1,512,256]{2,1,0:T(8,128)(2,1)S(1)}, u32[]{:S(2)}, u32[]{:S(2)}) collective-permute-start(bf16[1,512,256]{2,1,0:T(8,128)(2,1)} %bitcast.6), channel_id=1, source_target_pairs={{0,16},{16,0},{1,17},{17,1},{2,18},{18,2},{3,19},{19,3},{4,20},{20... | collective-permute-start | bytes 786440 | tf_op jit(solution)/shard_map/ppermute | solution.py:21
  7.8 3.2 %collective-permute-start.6 = (bf16[2,2,32,256]{3,2,1,0:T(8,128)(2,1)S(1)}, bf16[2,2,32,256]{3,2,1,0:T(8,128)(2,1)S(1)}, u32[]{:S(2)}, u32[]{:S(2)}) collective-permute-start(bf16[2,2,32,256]{3,2,1,0:T(8,128)(2,1)S(1)} %pad_maximum_fusion.refs_1_), channel_id=1, source_target_pairs={{0,1},{1,0},{2,3},{3,2},{4,5},{5,4},{6,7},{7,6},{8,9},{9,8},{10,11... | collective-permute-start | bytes 196616 | tf_op jit(solution)/shard_map/ppermute | solution.py:21
  7.9 4.5 %collective-permute-start.2 = (bf16[2,2,32,256]{3,2,1,0:T(8,128)(2,1)S(1)}, bf16[2,2,32,256]{3,2,1,0:T(8,128)(2,1)S(1)}, u32[]{:S(2)}, u32[]{:S(2)}) collective-permute-start(bf16[2,2,32,256]{3,2,1,0:T(8,128)(2,1)S(1)} %pad_maximum_fusion.refs_1_), channel_id=1, source_target_pairs={{0,4},{1,5},{2,6},{3,7},{4,0},{5,1},{6,2},{7,3},{8,12},{9,13},{10,... | collective-permute-start | bytes 196616 | tf_op jit(solution)/shard_map/ppermute | solution.py:21
  9.5 4.3 %collective-permute-start.1 = (bf16[2,2,32,256]{3,2,1,0:T(8,128)(2,1)S(1)}, bf16[2,2,32,256]{3,2,1,0:T(8,128)(2,1)S(1)}, u32[]{:S(2)}, u32[]{:S(2)}) collective-permute-start(bf16[2,2,32,256]{3,2,1,0:T(8,128)(2,1)S(1)} %pad_maximum_fusion.refs_1_), channel_id=1, source_target_pairs={{0,2},{1,3},{2,0},{3,1},{4,6},{5,7},{6,4},{7,5},{8,10},{9,11},{10,... | collective-permute-start | bytes 196616 | tf_op jit(solution)/shard_map/ppermute | solution.py:21
  11.0 5.2 %collective-permute-start.3 = (bf16[2,2,32,256]{3,2,1,0:T(8,128)(2,1)S(1)}, bf16[2,2,32,256]{3,2,1,0:T(8,128)(2,1)S(1)}, u32[]{:S(2)}, u32[]{:S(2)}) collective-permute-start(bf16[2,2,32,256]{3,2,1,0:T(8,128)(2,1)S(1)} %pad_maximum_fusion.refs_1_), channel_id=1, source_target_pairs={{0,6},{1,7},{2,4},{3,5},{4,2},{5,3},{6,0},{7,1},{8,14},{9,15},{10,... | collective-permute-start | bytes 196616 | tf_op jit(solution)/shard_map/ppermute | solution.py:21
  12.4 6.0 %collective-permute-start.8 = (bf16[2,2,32,256]{3,2,1,0:T(8,128)(2,1)S(1)}, bf16[2,2,32,256]{3,2,1,0:T(8,128)(2,1)S(1)}, u32[]{:S(2)}, u32[]{:S(2)}) collective-permute-start(bf16[2,2,32,256]{3,2,1,0:T(8,128)(2,1)S(1)} %collective-permute-done.2.refs_3_), channel_id=1, source_target_pairs={{0,1},{1,0},{2,3},{3,2},{4,5},{5,4},{6,7},{7,6},{8,9},{9,8},{10,11... | collective-permute-start | bytes 196616 | tf_op jit(solution)/shard_map/ppermute | solution.py:21
  13.7 4.6 %collective-permute-start.7 = (bf16[2,2,32,256]{3,2,1,0:T(8,128)(2,1)S(1)}, bf16[2,2,32,256]{3,2,1,0:T(8,128)(2,1)S(1)}, u32[]{:S(2)}, u32[]{:S(2)}) collective-permute-start(bf16[2,2,32,256]{3,2,1,0:T(8,128)(2,1)S(1)} %collective-permute-done.1.refs_1_.refs_2_), channel_id=1, source_target_pairs={{0,1},{1,0},{2,3},{3,2},{4,5},{5,4},{6,7},{7,6},{8,9},{9,8},{10,11... | collective-permute-start | bytes 196616 | tf_op jit(solution)/shard_map/ppermute | solution.py:21
  16.1 2.9 %collective-permute-start.9 = (bf16[2,2,32,256]{3,2,1,0:T(8,128)(2,1)S(1)}, bf16[2,2,32,256]{3,2,1,0:T(8,128)(2,1)S(1)}, u32[]{:S(2)}, u32[]{:S(2)}) collective-permute-start(bf16[2,2,32,256]{3,2,1,0:T(8,128)(2,1)S(1)} %collective-permute-done.3.refs_1_.refs_4_), channel_id=1, source_target_pairs={{0,1},{1,0},{2,3},{3,2},{4,5},{5,4},{6,7},{7,6},{8,9},{9,8},{10,11... | collective-permute-start | bytes 196616 | tf_op jit(solution)/shard_map/ppermute | solution.py:21
  20.4 3.0 %collective-permute-start.10 = (f32[4,2,32,256]{3,2,1,0:T(8,128)S(1)}, f32[4,2,32,256]{3,2,1,0:T(8,128)S(1)}, u32[]{:S(2)}, u32[]{:S(2)}) collective-permute-start(f32[4,2,32,256]{3,2,1,0:T(8,128)S(1)} %get-tuple-element.31), channel_id=1, source_target_pairs={{0,1},{1,0},{2,3},{3,2},{4,5},{5,4},{6,7},{7,6},{8,9},{9,8},{10,11... | collective-permute-start | bytes 786440 | tf_op jit(solution)/shard_map/ppermute | solution.py:21
  21.8 10.8 %collective-permute-start.15 = (s16[1,528,256]{2,1,0:T(8,128)(2,1)S(1)}, s16[1,528,256]{2,1,0:T(8,128)(2,1)S(1)}, u32[]{:S(2)}, u32[]{:S(2)}) collective-permute-start(s16[1,528,256]{2,1,0:T(8,128)(2,1)S(1)} %shard_map.77), channel_id=1, source_target_pairs={{0,16},{16,0},{1,17},{17,1},{2,18},{18,2},{3,19},{19,3},{4,20},{20... | collective-permute-start | bytes 811016 | tf_op jit(solution)/shard_map/ppermute | solution.py:21
  23.5 4.1 %collective-permute-start.11 = (s16[1,80,256]{2,1,0:T(8,128)(2,1)S(1)}, s16[1,80,256]{2,1,0:T(8,128)(2,1)S(1)}, u32[]{:S(2)}, u32[]{:S(2)}) collective-permute-start(s16[1,80,256]{2,1,0:T(8,128)(2,1)S(1)} %get-tuple-element.33), channel_id=1, source_target_pairs={{0,2},{1,3},{2,0},{3,1},{4,6},{5,7},{6,4},{7,5},{8,10},{9,11},{10,... | collective-permute-start | bytes 122888 | tf_op jit(solution)/shard_map/ppermute | solution.py:21
  24.1 4.3 %collective-permute-start.12 = (s16[1,80,256]{2,1,0:T(8,128)(2,1)S(1)}, s16[1,80,256]{2,1,0:T(8,128)(2,1)S(1)}, u32[]{:S(2)}, u32[]{:S(2)}) collective-permute-start(s16[1,80,256]{2,1,0:T(8,128)(2,1)S(1)} %get-tuple-element.34), channel_id=1, source_target_pairs={{0,4},{1,5},{2,6},{3,7},{4,0},{5,1},{6,2},{7,3},{8,12},{9,13},{10,... | collective-permute-start | bytes 122888 | tf_op jit(solution)/shard_map/ppermute | solution.py:21
  25.6 4.9 %collective-permute-start.13 = (s16[1,80,256]{2,1,0:T(8,128)(2,1)S(1)}, s16[1,80,256]{2,1,0:T(8,128)(2,1)S(1)}, u32[]{:S(2)}, u32[]{:S(2)}) collective-permute-start(s16[1,80,256]{2,1,0:T(8,128)(2,1)S(1)} %get-tuple-element.35), channel_id=1, source_target_pairs={{0,6},{1,7},{2,4},{3,5},{4,2},{5,3},{6,0},{7,1},{8,14},{9,15},{10,... | collective-permute-start | bytes 122888 | tf_op jit(solution)/shard_map/ppermute | solution.py:21
  30.5 5.2 %collective-permute-start.14 = (f32[32,256]{1,0:T(8,128)S(1)}, f32[32,256]{1,0:T(8,128)S(1)}, u32[]{:S(2)}, u32[]{:S(2)}) collective-permute-start(f32[32,256]{1,0:T(8,128)S(1)} %get-tuple-element.37), channel_id=1, source_target_pairs={{0,8},{1,9},{2,10},{3,11},{4,12},{5,13},{6,14},{7,15},{8,0},{9,1},... | collective-permute-start | bytes 98312 | tf_op jit(solution)/shard_map/ppermute | solution.py:21

commit v6 on v5

--- a/solution.py
+++ b/solution.py
@@ -268,11 +268,19 @@
     )(in_vmem(x), in_vmem(q))
 
 
-def fold_kernel(mine, core_in, own, *coded):
+def decoded(q_ref, k):
+    rows = q_ref.shape[1] - GROUPS
+    groups = min(GROUPS, rows // GROUPS)
+    return jnp.concatenate([decode_rows(q_ref, k, g, groups) for g in range(groups)], 0)
+
+
+def fold_kernel(mine, core_in, keep, coded):
     n, n_a, us, width = mine.shape
-    own[0] = (mine[0] + core_in[0]).reshape(n_a * us, width)
-    for i in range(1, n):
-        encode_rows((mine[i] + core_in[i]).reshape(n_a * us, width), coded[i - 1], 0)
+    rows = n_a * us
+    both = [(mine[i] + core_in[i]).reshape(rows, width) for i in range(n)]
+    for i in range(0, n, 2):
+        keep[i // 2] = both[i]
+    encode_rows(jnp.concatenate(both[1::2], 0), coded, 0)
 
 
 def fold(mine, core_in):
@@ -281,34 +289,51 @@
     return pl.pallas_call(
         fold_kernel,
         in_specs=[VM, VM],
-        out_specs=[VM] * n,
-        out_shape=[pltpu.VMEM((1, rows, width), f32)]
-        + [pltpu.VMEM((1, rows + GROUPS, width), jnp.int16)] * (n - 1),
+        out_specs=[VM] * 2,
+        out_shape=[pltpu.VMEM((n // 2, rows, width), f32), pltpu.VMEM((1, n // 2 * rows + GROUPS, width), jnp.int16)],
         compiler_params=PARAMS,
     )(in_vmem(mine), in_vmem(core_in))
 
 
-def near_kernel(own, *refs):
-    *coded, keep, send = refs
-    rows = own.shape[1]
+def spread_kernel(keep, q, own, *coded):
+    n, rows, _ = keep.shape
     half = rows // 2
-    groups = min(GROUPS, rows // GROUPS)
-    step = rows // groups
-    for g in range(groups):
-        x = own[0, pl.ds(g * step, step), :]
-        for q in coded:
-            x = x + decode_rows(q, 0, g, groups)
-        to, at = (keep, g * step) if g * step < half else (send, g * step - half)
-        to[pl.ds(at, step), :] = x
-
-
-def near_sum(own, coded):
-    _, rows, width = own.shape
-    return pl.pallas_call(
-        near_kernel,
+    came = decoded(q, 0)
+    for i in range(n):
+        x = keep[i] + came[i * rows : (i + 1) * rows]
+        for j in range(2):
+            part = x[j * half : (j + 1) * half]
+            if i == 0 and j == 0:
+                own[...] = part
+            else:
+                encode_rows(part, coded[2 * i + j - 1], 0)
+
+
+def spread(keep, q):
+    _, rows, width = keep.shape
+    half = rows // 2
+    return pl.pallas_call(
+        spread_kernel,
+        in_specs=[VM] * 2,
+        out_specs=[VM] * 4,
+        out_shape=[pltpu.VMEM((half, width), f32)] + [pltpu.VMEM((1, half + GROUPS, width), jnp.int16)] * 3,
+        compiler_params=PARAMS,
+    )(in_vmem(keep), in_vmem(q))
+
+
+def total_kernel(own, *refs):
+    x = own[...]
+    for q in refs[:-1]:
+        x = x + decoded(q, 0)
+    refs[-1][...] = x
+
+
+def total(own, coded):
+    return pl.pallas_call(
+        total_kernel,
         in_specs=[VM] * (1 + len(coded)),
-        out_specs=[VM] * 2,
-        out_shape=[pltpu.VMEM((rows // 2, width), f32)] * 2,
+        out_specs=VM,
+        out_shape=jax.ShapeDtypeStruct(own.shape, f32),
         compiler_params=PARAMS,
     )(*[in_vmem(x) for x in (own, *coded)])
 
@@ -364,14 +389,14 @@
         sums = [out_mine, out_other]
         at_mine, at_other = [(0, i) for i in range(4)], [(1, i) for i in range(4)]
 
-    own, *coded = fold(out_mine, swap(out_other, "ia", n_ia, core))
-    coded = [swap(q, "ia", n_ia, b) for q, b in zip(coded, near[1:])]
-    acc, send = near_sum(own, coded)
-    for n, bit in enumerate(a_bits[::-1]):
-        if n:
-            half = acc.shape[0] // 2
-            acc, send = acc[:half], acc[half:]
-        acc = acc + swap(send, "ia", n_ia, bit)
+    keep, odd = fold(out_mine, swap(out_other, "ia", n_ia, core))
+    own, *coded = spread(keep, swap(odd, "ia", n_ia, near[1]))
+    far_bit = a_bits[-1]
+    coded = [swap(q, "ia", n_ia, b) for q, b in zip(coded, [far_bit, near[2], far_bit ^ near[2]])]
+    acc = total(own, coded)
+    for bit in a_bits[:-1][::-1]:
+        half = acc.shape[0] // 2
+        acc = acc[:half] + swap(acc[half:], "ia", n_ia, bit)
     user_product = acc.reshape(us, width)
 
     for bit in item_bits[::-1]:

time: 36.7 us -> 37.7 us (1.027)
  waiting for transfers between devices: 10.5 us -> 12 us
  Pallas kernels: 6.79 us -> 7.44 us
  other arithmetic: 0.63 us -> 0.01 us
  starting transfers between devices: 17.7 us -> 17.2 us
    ppermute x16, waiting for transfers between devices: 10.5 us -> 12 us  [swap(): return lax.ppermute(x, axis, [(i, i ^ bits) for i in range(size)])]
    pallas_call x2 -> x3, Pallas kernels: 0.13 us -> 0.78 us  [the longest x1 0.64 us: total(): pl.pallas_call(total_kernel, in_specs=[VM] * (1 + len(coded)), out_specs=...]
    add x1 -> x0, other arithmetic: 0.62 us -> none  [on_device(): acc = acc + swap(send, 'ia', n_ia, bit)]
    ppermute x16, starting transfers between devices: 17.7 us -> 17.2 us  [swap(): return lax.ppermute(x, axis, [(i, i ^ bits) for i in range(size)])]
  transfers between devices with their start and end apart: 16 -> 16, of which waited for: 8 -> 7; matrix products, arithmetic and copies ran while one was open for 0% -> 0% of each run, Pallas kernels for 15% -> 14%
where the time goes in v6:
time: 37.7 us; the launch traced here: 37.4 us
  starting transfers between devices  17.2 us (46%)
  waiting for transfers between devices  12 us (32%)
  Pallas kernels  7.44 us (20%)
  between operations  0.75 us (2%)
    ppermute x16, starting transfers between devices, swap(): return lax.ppermute(x, axis, [(i, i ^ bits) for i in range(size)])  17.2 us
    ppermute x16, waiting for transfers between devices, swap(): return lax.ppermute(x, axis, [(i, i ^ bits) for i in range(size)])  12 us
    pallas_call x5, Pallas kernels, region(): pl.pallas_call(functools.partial(region_kernel, n_users=len(users), sums_...  3.31 us
    pallas_call x1, Pallas kernels, load(): pl.pallas_call(functools.partial(load_kernel, **static), in_specs=[pl.Blo...  1.61 us
    pallas_call x1, Pallas kernels, add_decoded(): pl.pallas_call(functools.partial(decode_kernel, at=at), in_specs=[VM, VM]...  0.87 us
  transfers between devices with their start and end apart: 16, of which 7 were waited for; matrix products, arithmetic and copies ran while one was open for 0% of the time, Pallas kernels for 14%

profile of v6, /device:TPU:0, one launch (start us, length us, event | category | flops | bytes accessed | tf_op | source)
XLA Modules:
  0.0 37.4 jit_solution(4609172412159647198)
XLA Ops:
  0.6 0.8 %shard_map.69 = bf16[1,2,32,256]{3,2,1,0:T(8,128)(2,1)S(1)} custom-call(bf16[32,256]{1,0:T(8,128)(2,1)} %a.1, bf16[32,256]{1,0:T(8,128)(2,1)} %b.1), custom_call_target="tpu_custom_call" | custom-call | tf_op jit(solution)/shard_map/pallas_call | solution.py:200
  1.4 4.1 %collective-permute-start = (bf16[1,2,32,256]{3,2,1,0:T(8,128)(2,1)S(1)}, bf16[1,2,32,256]{3,2,1,0:T(8,128)(2,1)S(1)}, u32[]{:S(2)}, u32[]{:S(2)}) collective-permute-start(bf16[1,2,32,256]{3,2,1,0:T(8,128)(2,1)S(1)} %shard_map.69), channel_id=1, source_target_pairs={{0,8},{1,9},{2,10},{3,11},{4,12},{5,13},{6,14},{7,15},{8,0},{9,1},... | collective-permute-start | bytes 98312 | tf_op jit(solution)/shard_map/ppermute | solution.py:21
  5.5 1.5 %collective-permute-start.4 = (bf16[1,512,256]{2,1,0:T(8,128)(2,1)}, bf16[1,512,256]{2,1,0:T(8,128)(2,1)S(1)}, u32[]{:S(2)}, u32[]{:S(2)}) collective-permute-start(bf16[1,512,256]{2,1,0:T(8,128)(2,1)} %bitcast.4), channel_id=1, source_target_pairs={{0,16},{16,0},{1,17},{17,1},{2,18},{18,2},{3,19},{19,3},{4,20},{20... | collective-permute-start | bytes 786440 | tf_op jit(solution)/shard_map/ppermute | solution.py:21
  7.0 0.0 copy-start
  7.0 0.5 %collective-permute-start.5 = (bf16[1,512,256]{2,1,0:T(8,128)(2,1)}, bf16[1,512,256]{2,1,0:T(8,128)(2,1)S(1)}, u32[]{:S(2)}, u32[]{:S(2)}) collective-permute-start(bf16[1,512,256]{2,1,0:T(8,128)(2,1)} %bitcast.6), channel_id=1, source_target_pairs={{0,16},{16,0},{1,17},{17,1},{2,18},{18,2},{3,19},{19,3},{4,20},{20... | collective-permute-start | bytes 786440 | tf_op jit(solution)/shard_map/ppermute | solution.py:21
  7.5 0.2 collective-permute-done
  7.8 0.1 collective-permute-start.6
  7.9 1.6 %collective-permute-start.2 = (bf16[2,2,32,256]{3,2,1,0:T(8,128)(2,1)S(1)}, bf16[2,2,32,256]{3,2,1,0:T(8,128)(2,1)S(1)}, u32[]{:S(2)}, u32[]{:S(2)}) collective-permute-start(bf16[2,2,32,256]{3,2,1,0:T(8,128)(2,1)S(1)} %pad_maximum_fusion.refs_1_), channel_id=1, source_target_pairs={{0,4},{1,5},{2,6},{3,7},{4,0},{5,1},{6,2},{7,3},{8,12},{9,13},{10,... | collective-permute-start | bytes 196616 | tf_op jit(solution)/shard_map/ppermute | solution.py:21
  9.5 1.5 %collective-permute-start.1 = (bf16[2,2,32,256]{3,2,1,0:T(8,128)(2,1)S(1)}, bf16[2,2,32,256]{3,2,1,0:T(8,128)(2,1)S(1)}, u32[]{:S(2)}, u32[]{:S(2)}) collective-permute-start(bf16[2,2,32,256]{3,2,1,0:T(8,128)(2,1)S(1)} %pad_maximum_fusion.refs_1_), channel_id=1, source_target_pairs={{0,2},{1,3},{2,0},{3,1},{4,6},{5,7},{6,4},{7,5},{8,10},{9,11},{10,... | collective-permute-start | bytes 196616 | tf_op jit(solution)/shard_map/ppermute | solution.py:21
  11.0 0.0 collective-permute-done.6.refs_2_.refs_1_
  11.0 0.6 %collective-permute-start.3 = (bf16[2,2,32,256]{3,2,1,0:T(8,128)(2,1)S(1)}, bf16[2,2,32,256]{3,2,1,0:T(8,128)(2,1)S(1)}, u32[]{:S(2)}, u32[]{:S(2)}) collective-permute-start(bf16[2,2,32,256]{3,2,1,0:T(8,128)(2,1)S(1)} %pad_maximum_fusion.refs_1_), channel_id=1, source_target_pairs={{0,6},{1,7},{2,4},{3,5},{4,2},{5,3},{6,0},{7,1},{8,14},{9,15},{10,... | collective-permute-start | bytes 196616 | tf_op jit(solution)/shard_map/ppermute | solution.py:21
  11.6 0.8 %collective-permute-done.2.refs_3_ = bf16[2,2,32,256]{3,2,1,0:T(8,128)(2,1)S(1)} collective-permute-done((bf16[2,2,32,256]{3,2,1,0:T(8,128)(2,1)S(1)}, bf16[2,2,32,256]{3,2,1,0:T(8,128)(2,1)S(1)}, u32[]{:S(2)}, u32[]{:S(2)}) %collective-permute-start.2) | collective-permute-done | bytes 65568 | tf_op jit(solution)/shard_map/ppermute | solution.py:21
  12.4 0.0 collective-permute-start.8
  12.4 1.4 %collective-permute-done.1.refs_1_.refs_2_ = bf16[2,2,32,256]{3,2,1,0:T(8,128)(2,1)S(1)} collective-permute-done((bf16[2,2,32,256]{3,2,1,0:T(8,128)(2,1)S(1)}, bf16[2,2,32,256]{3,2,1,0:T(8,128)(2,1)S(1)}, u32[]{:S(2)}, u32[]{:S(2)}) %collective-permute-start.1) | collective-permute-done | bytes 65568 | tf_op jit(solution)/shard_map/ppermute | solution.py:21
  13.7 0.0 collective-permute-start.7
  13.7 2.4 %collective-permute-done.3.refs_1_.refs_4_ = bf16[2,2,32,256]{3,2,1,0:T(8,128)(2,1)S(1)} collective-permute-done((bf16[2,2,32,256]{3,2,1,0:T(8,128)(2,1)S(1)}, bf16[2,2,32,256]{3,2,1,0:T(8,128)(2,1)S(1)}, u32[]{:S(2)}, u32[]{:S(2)}) %collective-permute-start.3) | collective-permute-done | bytes 65568 | tf_op jit(solution)/shard_map/ppermute | solution.py:21
  16.1 0.0 collective-permute-start.9
  16.1 0.0 copy-done
  16.1 1.6 %shard_map.68 = (bf16[1,512,256]{2,1,0:T(8,128)(2,1)S(1)}, bf16[1,512,256]{2,1,0:T(8,128)(2,1)S(1)}, f32[8,256]{1,0:T(8,128)S(1)}) custom-call(s32[4,8]{1,0:T(4,128)S(1)} %copy-done, bf16[1,512,256]{2,1,0:T(8,128)(2,1)} %bitcast.5, bf16[1,512,256]{2,1,0:T(8,128)(2,1)} %bitcast.7), custom_call_target="tpu_custom_call" | custom-call | tf_op jit(solution)/shard_map/pallas_call | solution.py:178
  17.8 0.6 %shard_map.70 = (f32[2,2,32,256]{3,2,1,0:T(8,128)S(1)}, f32[1,512,256]{2,1,0:T(8,128)S(1)}) custom-call(f32[8,256]{1,0:T(8,128)S(1)} %get-tuple-element.21.refs_0_, bf16[2,2,32,256]{3,2,1,0:T(8,128)(2,1)S(1)} %pad_maximum_fusion.refs_1_, bf16[2,2,32,256]{3,2,1,0:T(8,128)(2,1)S(1)} %collective-permute-done.6.refs_2_.refs_1_, ...), custom_call_target="tpu_custom_call" | custom-call | tf_op jit(solution)/shard_map/pallas_call | solution.py:126
  18.3 0.0 collective-permute-done.8.refs_4_.refs_3_
  18.3 0.0 collective-permute-done.7.refs_2_
  18.4 0.7 %shard_map.71 = (f32[4,2,32,256]{3,2,1,0:T(8,128)S(1)}, f32[1,512,256]{2,1,0:T(8,128)S(1)}) custom-call(f32[8,256]{1,0:T(8,128)S(1)} %get-tuple-element.21.refs_0_, bf16[2,2,32,256]{3,2,1,0:T(8,128)(2,1)S(1)} %collective-permute-done.1.refs_1_.refs_2_, bf16[2,2,32,256]{3,2,1,0:T(8,128)(2,1)S(1)} %collective-permute-done.7.refs_2_, ...), custom_call_target="tpu_custom_call", output_to_operand_aliasing={{1}: (7, {})} | custom-call | tf_op jit(solution)/shard_map/pallas_call | solution.py:126
  19.1 0.0 collective-permute-done.9.refs_2_.refs_4_
  19.1 0.6 %shard_map.72 = (f32[2,2,32,256]{3,2,1,0:T(8,128)S(1)}, f32[1,512,256]{2,1,0:T(8,128)S(1)}) custom-call(f32[8,256]{1,0:T(8,128)S(1)} %get-tuple-element.21.refs_0_, bf16[2,2,32,256]{3,2,1,0:T(8,128)(2,1)S(1)} %collective-permute-done.3.refs_1_.refs_4_, ...), custom_call_target="tpu_custom_call", output_to_operand_aliasing={{1}: (5, {})} | custom-call | tf_op jit(solution)/shard_map/pallas_call | solution.py:126
  19.7 0.0 collective-permute-done.4.refs_5_
  19.7 0.0 collective-permute-done.5.refs_6_
  19.7 0.7 %shard_map.73 = (f32[4,2,32,256]{3,2,1,0:T(8,128)S(1)}, f32[1,512,256]{2,1,0:T(8,128)S(1)}) custom-call(f32[8,256]{1,0:T(8,128)S(1)} %get-tuple-element.21.refs_0_, bf16[2,2,32,256]{3,2,1,0:T(8,128)(2,1)S(1)} %collective-permute-done.6.refs_2_.refs_1_, bf16[2,2,32,256]{3,2,1,0:T(8,128)(2,1)S(1)} %collective-permute-done.7.refs_2_, ...), custom_call_target="tpu_custom_call" | custom-call | tf_op jit(solution)/shard_map/pallas_call | solution.py:126
  20.4 0.5 %collective-permute-start.10 = (f32[4,2,32,256]{3,2,1,0:T(8,128)S(1)}, f32[4,2,32,256]{3,2,1,0:T(8,128)S(1)}, u32[]{:S(2)}, u32[]{:S(2)}) collective-permute-start(f32[4,2,32,256]{3,2,1,0:T(8,128)S(1)} %get-tuple-element.31), channel_id=1, source_target_pairs={{0,1},{1,0},{2,3},{3,2},{4,5},{5,4},{6,7},{7,6},{8,9},{9,8},{10,11... | collective-permute-start | bytes 786440 | tf_op jit(solution)/shard_map/ppermute | solution.py:21
  21.0 0.7 %shard_map.74 = (f32[4,2,32,256]{3,2,1,0:T(8,128)S(1)}, f32[1,512,256]{2,1,0:T(8,128)S(1)}) custom-call(f32[8,256]{1,0:T(8,128)S(1)} %get-tuple-element.21.refs_0_, bf16[2,2,32,256]{3,2,1,0:T(8,128)(2,1)S(1)} %pad_maximum_fusion.refs_1_, bf16[2,2,32,256]{3,2,1,0:T(8,128)(2,1)S(1)} %collective-permute-done.1.refs_1_.refs_2_, ...), custom_call_target="tpu_custom_call", output_to_operand_aliasing={{1}: (10, {})} | custom-call | tf_op jit(solution)/shard_map/pallas_call | solution.py:126
  21.7 0.1 shard_map.78
  21.8 1.6 %collective-permute-start.15 = (s16[1,528,256]{2,1,0:T(8,128)(2,1)S(1)}, s16[1,528,256]{2,1,0:T(8,128)(2,1)S(1)}, u32[]{:S(2)}, u32[]{:S(2)}) collective-permute-start(s16[1,528,256]{2,1,0:T(8,128)(2,1)S(1)} %shard_map.78), channel_id=1, source_target_pairs={{0,16},{16,0},{1,17},{17,1},{2,18},{18,2},{3,19},{19,3},{4,20},{20... | collective-permute-start | bytes 811016 | tf_op jit(solution)/shard_map/ppermute | solution.py:21
  23.4 0.0 collective-permute-done.10.core_in
  23.4 0.1 shard_map.75
  23.5 0.6 %collective-permute-start.11 = (s16[1,144,256]{2,1,0:T(8,128)(2,1)S(1)}, s16[1,144,256]{2,1,0:T(8,128)(2,1)S(1)}, u32[]{:S(2)}, u32[]{:S(2)}) collective-permute-start(s16[1,144,256]{2,1,0:T(8,128)(2,1)S(1)} %get-tuple-element.33), channel_id=1, source_target_pairs={{0,2},{1,3},{2,0},{3,1},{4,6},{5,7},{6,4},{7,5},{8,10},{9,11},{10,... | collective-permute-start | bytes 221192 | tf_op jit(solution)/shard_map/ppermute | solution.py:21
  24.1 3.8 %collective-permute-done.11.q = s16[1,144,256]{2,1,0:T(8,128)(2,1)S(1)} collective-permute-done((s16[1,144,256]{2,1,0:T(8,128)(2,1)S(1)}, s16[1,144,256]{2,1,0:T(8,128)(2,1)S(1)}, u32[]{:S(2)}, u32[]{:S(2)}) %collective-permute-start.11) | collective-permute-done | bytes 73760 | tf_op jit(solution)/shard_map/ppermute | solution.py:21
  27.9 0.1 shard_map.76
  28.0 2.9 %collective-permute-start.12 = (s16[1,48,256]{2,1,0:T(8,128)(2,1)S(1)}, s16[1,48,256]{2,1,0:T(8,128)(2,1)S(1)}, u32[]{:S(2)}, u32[]{:S(2)}) collective-permute-start(s16[1,48,256]{2,1,0:T(8,128)(2,1)S(1)} %get-tuple-element.35), channel_id=1, source_target_pairs={{0,8},{1,9},{2,10},{3,11},{4,12},{5,13},{6,14},{7,15},{8,0},{9,1},... | collective-permute-start | bytes 73736 | tf_op jit(solution)/shard_map/ppermute | solution.py:21
  30.9 0.2 collective-permute-start.13
  31.1 1.3 %collective-permute-start.14 = (s16[1,48,256]{2,1,0:T(8,128)(2,1)S(1)}, s16[1,48,256]{2,1,0:T(8,128)(2,1)S(1)}, u32[]{:S(2)}, u32[]{:S(2)}) collective-permute-start(s16[1,48,256]{2,1,0:T(8,128)(2,1)S(1)} %get-tuple-element.37), channel_id=1, source_target_pairs={{0,12},{1,13},{2,14},{3,15},{4,8},{5,9},{6,10},{7,11},{8,4},{9,5},... | collective-permute-start | bytes 73736 | tf_op jit(solution)/shard_map/ppermute | solution.py:21
  32.5 0.0 collective-permute-done.15.q_ref
  32.5 0.9 %shard_map.79 = f32[1,512,256]{2,1,0:T(8,128)} custom-call(f32[1,512,256]{2,1,0:T(8,128)S(1)} %get-tuple-element.38.x_ref, s16[1,528,256]{2,1,0:T(8,128)(2,1)S(1)} %collective-permute-done.15.q_ref), custom_call_target="tpu_custom_call" | custom-call | tf_op jit(solution)/shard_map/pallas_call | solution.py:262
  33.3 0.0 collective-permute-done.12.refs_0_
  33.3 1.4 %collective-permute-done.13.refs_1_ = s16[1,48,256]{2,1,0:T(8,128)(2,1)S(1)} collective-permute-done((s16[1,48,256]{2,1,0:T(8,128)(2,1)S(1)}, s16[1,48,256]{2,1,0:T(8,128)(2,1)S(1)}, u32[]{:S(2)}, u32[]{:S(2)}) %collective-permute-start.13) | collective-permute-done | bytes 24608 | tf_op jit(solution)/shard_map/ppermute | solution.py:21
  34.7 2.0 %collective-permute-done.14.refs_2_ = s16[1,48,256]{2,1,0:T(8,128)(2,1)S(1)} collective-permute-done((s16[1,48,256]{2,1,0:T(8,128)(2,1)S(1)}, s16[1,48,256]{2,1,0:T(8,128)(2,1)S(1)}, u32[]{:S(2)}, u32[]{:S(2)}) %collective-permute-start.14) | collective-permute-done | bytes 24608 | tf_op jit(solution)/shard_map/ppermute | solution.py:21
  36.8 0.6 %shard_map.77 = f32[32,256]{1,0:T(8,128)} custom-call(f32[32,256]{1,0:T(8,128)S(1)} %get-tuple-element.34.own, s16[1,48,256]{2,1,0:T(8,128)(2,1)S(1)} %collective-permute-done.12.refs_0_, s16[1,48,256]{2,1,0:T(8,128)(2,1)S(1)} %collective-permute-done.13.refs_1_, s16[1,48,256]{2,1,0:T(8,128)(2,1)S(1)} %collective-permute-done.14.refs_2_), custom_call_target="tpu_custom_call" | custom-call | tf_op jit(solution)/shard_map/pallas_call | solution.py:332
  (1 shorter events, 0.0 us)
Async XLA Ops:
  1.4 6.4 %collective-permute-start = (bf16[1,2,32,256]{3,2,1,0:T(8,128)(2,1)S(1)}, bf16[1,2,32,256]{3,2,1,0:T(8,128)(2,1)S(1)}, u32[]{:S(2)}, u32[]{:S(2)}) collective-permute-start(bf16[1,2,32,256]{3,2,1,0:T(8,128)(2,1)S(1)} %shard_map.69), channel_id=1, source_target_pairs={{0,8},{1,9},{2,10},{3,11},{4,12},{5,13},{6,14},{7,15},{8,0},{9,1},... | collective-permute-start | bytes 98312 | tf_op jit(solution)/shard_map/ppermute | solution.py:21
  5.5 14.1 %collective-permute-start.4 = (bf16[1,512,256]{2,1,0:T(8,128)(2,1)}, bf16[1,512,256]{2,1,0:T(8,128)(2,1)S(1)}, u32[]{:S(2)}, u32[]{:S(2)}) collective-permute-start(bf16[1,512,256]{2,1,0:T(8,128)(2,1)} %bitcast.4), channel_id=1, source_target_pairs={{0,16},{16,0},{1,17},{17,1},{2,18},{18,2},{3,19},{19,3},{4,20},{20... | collective-permute-start | bytes 786440 | tf_op jit(solution)/shard_map/ppermute | solution.py:21
  7.0 9.1 %copy-start = (s32[4,8]{1,0:T(4,128)S(1)}, s32[4,8]{1,0:T(4,128)}, u32[]{:S(2)}) copy-start(s32[4,8]{1,0:T(4,128)} %mask.1) | copy-start | bytes 388
  7.0 12.6 %collective-permute-start.5 = (bf16[1,512,256]{2,1,0:T(8,128)(2,1)}, bf16[1,512,256]{2,1,0:T(8,128)(2,1)S(1)}, u32[]{:S(2)}, u32[]{:S(2)}) collective-permute-start(bf16[1,512,256]{2,1,0:T(8,128)(2,1)} %bitcast.6), channel_id=1, source_target_pairs={{0,16},{16,0},{1,17},{17,1},{2,18},{18,2},{3,19},{19,3},{4,20},{20... | collective-permute-start | bytes 786440 | tf_op jit(solution)/shard_map/ppermute | solution.py:21
  7.8 3.2 %collective-permute-start.6 = (bf16[2,2,32,256]{3,2,1,0:T(8,128)(2,1)S(1)}, bf16[2,2,32,256]{3,2,1,0:T(8,128)(2,1)S(1)}, u32[]{:S(2)}, u32[]{:S(2)}) collective-permute-start(bf16[2,2,32,256]{3,2,1,0:T(8,128)(2,1)S(1)} %pad_maximum_fusion.refs_1_), channel_id=1, source_target_pairs={{0,1},{1,0},{2,3},{3,2},{4,5},{5,4},{6,7},{7,6},{8,9},{9,8},{10,11... | collective-permute-start | bytes 196616 | tf_op jit(solution)/shard_map/ppermute | solution.py:21
  7.9 4.5 %collective-permute-start.2 = (bf16[2,2,32,256]{3,2,1,0:T(8,128)(2,1)S(1)}, bf16[2,2,32,256]{3,2,1,0:T(8,128)(2,1)S(1)}, u32[]{:S(2)}, u32[]{:S(2)}) collective-permute-start(bf16[2,2,32,256]{3,2,1,0:T(8,128)(2,1)S(1)} %pad_maximum_fusion.refs_1_), channel_id=1, source_target_pairs={{0,4},{1,5},{2,6},{3,7},{4,0},{5,1},{6,2},{7,3},{8,12},{9,13},{10,... | collective-permute-start | bytes 196616 | tf_op jit(solution)/shard_map/ppermute | solution.py:21
  9.5 4.3 %collective-permute-start.1 = (bf16[2,2,32,256]{3,2,1,0:T(8,128)(2,1)S(1)}, bf16[2,2,32,256]{3,2,1,0:T(8,128)(2,1)S(1)}, u32[]{:S(2)}, u32[]{:S(2)}) collective-permute-start(bf16[2,2,32,256]{3,2,1,0:T(8,128)(2,1)S(1)} %pad_maximum_fusion.refs_1_), channel_id=1, source_target_pairs={{0,2},{1,3},{2,0},{3,1},{4,6},{5,7},{6,4},{7,5},{8,10},{9,11},{10,... | collective-permute-start | bytes 196616 | tf_op jit(solution)/shard_map/ppermute | solution.py:21
  11.0 5.2 %collective-permute-start.3 = (bf16[2,2,32,256]{3,2,1,0:T(8,128)(2,1)S(1)}, bf16[2,2,32,256]{3,2,1,0:T(8,128)(2,1)S(1)}, u32[]{:S(2)}, u32[]{:S(2)}) collective-permute-start(bf16[2,2,32,256]{3,2,1,0:T(8,128)(2,1)S(1)} %pad_maximum_fusion.refs_1_), channel_id=1, source_target_pairs={{0,6},{1,7},{2,4},{3,5},{4,2},{5,3},{6,0},{7,1},{8,14},{9,15},{10,... | collective-permute-start | bytes 196616 | tf_op jit(solution)/shard_map/ppermute | solution.py:21
  12.4 6.0 %collective-permute-start.8 = (bf16[2,2,32,256]{3,2,1,0:T(8,128)(2,1)S(1)}, bf16[2,2,32,256]{3,2,1,0:T(8,128)(2,1)S(1)}, u32[]{:S(2)}, u32[]{:S(2)}) collective-permute-start(bf16[2,2,32,256]{3,2,1,0:T(8,128)(2,1)S(1)} %collective-permute-done.2.refs_3_), channel_id=1, source_target_pairs={{0,1},{1,0},{2,3},{3,2},{4,5},{5,4},{6,7},{7,6},{8,9},{9,8},{10,11... | collective-permute-start | bytes 196616 | tf_op jit(solution)/shard_map/ppermute | solution.py:21
  13.7 4.6 %collective-permute-start.7 = (bf16[2,2,32,256]{3,2,1,0:T(8,128)(2,1)S(1)}, bf16[2,2,32,256]{3,2,1,0:T(8,128)(2,1)S(1)}, u32[]{:S(2)}, u32[]{:S(2)}) collective-permute-start(bf16[2,2,32,256]{3,2,1,0:T(8,128)(2,1)S(1)} %collective-permute-done.1.refs_1_.refs_2_), channel_id=1, source_target_pairs={{0,1},{1,0},{2,3},{3,2},{4,5},{5,4},{6,7},{7,6},{8,9},{9,8},{10,11... | collective-permute-start | bytes 196616 | tf_op jit(solution)/shard_map/ppermute | solution.py:21
  16.1 2.9 %collective-permute-start.9 = (bf16[2,2,32,256]{3,2,1,0:T(8,128)(2,1)S(1)}, bf16[2,2,32,256]{3,2,1,0:T(8,128)(2,1)S(1)}, u32[]{:S(2)}, u32[]{:S(2)}) collective-permute-start(bf16[2,2,32,256]{3,2,1,0:T(8,128)(2,1)S(1)} %collective-permute-done.3.refs_1_.refs_4_), channel_id=1, source_target_pairs={{0,1},{1,0},{2,3},{3,2},{4,5},{5,4},{6,7},{7,6},{8,9},{9,8},{10,11... | collective-permute-start | bytes 196616 | tf_op jit(solution)/shard_map/ppermute | solution.py:21
  20.4 3.0 %collective-permute-start.10 = (f32[4,2,32,256]{3,2,1,0:T(8,128)S(1)}, f32[4,2,32,256]{3,2,1,0:T(8,128)S(1)}, u32[]{:S(2)}, u32[]{:S(2)}) collective-permute-start(f32[4,2,32,256]{3,2,1,0:T(8,128)S(1)} %get-tuple-element.31), channel_id=1, source_target_pairs={{0,1},{1,0},{2,3},{3,2},{4,5},{5,4},{6,7},{7,6},{8,9},{9,8},{10,11... | collective-permute-start | bytes 786440 | tf_op jit(solution)/shard_map/ppermute | solution.py:21
  21.8 10.6 %collective-permute-start.15 = (s16[1,528,256]{2,1,0:T(8,128)(2,1)S(1)}, s16[1,528,256]{2,1,0:T(8,128)(2,1)S(1)}, u32[]{:S(2)}, u32[]{:S(2)}) collective-permute-start(s16[1,528,256]{2,1,0:T(8,128)(2,1)S(1)} %shard_map.78), channel_id=1, source_target_pairs={{0,16},{16,0},{1,17},{17,1},{2,18},{18,2},{3,19},{19,3},{4,20},{20... | collective-permute-start | bytes 811016 | tf_op jit(solution)/shard_map/ppermute | solution.py:21
  23.5 4.4 %collective-permute-start.11 = (s16[1,144,256]{2,1,0:T(8,128)(2,1)S(1)}, s16[1,144,256]{2,1,0:T(8,128)(2,1)S(1)}, u32[]{:S(2)}, u32[]{:S(2)}) collective-permute-start(s16[1,144,256]{2,1,0:T(8,128)(2,1)S(1)} %get-tuple-element.33), channel_id=1, source_target_pairs={{0,2},{1,3},{2,0},{3,1},{4,6},{5,7},{6,4},{7,5},{8,10},{9,11},{10,... | collective-permute-start | bytes 221192 | tf_op jit(solution)/shard_map/ppermute | solution.py:21
  28.0 5.3 %collective-permute-start.12 = (s16[1,48,256]{2,1,0:T(8,128)(2,1)S(1)}, s16[1,48,256]{2,1,0:T(8,128)(2,1)S(1)}, u32[]{:S(2)}, u32[]{:S(2)}) collective-permute-start(s16[1,48,256]{2,1,0:T(8,128)(2,1)S(1)} %get-tuple-element.35), channel_id=1, source_target_pairs={{0,8},{1,9},{2,10},{3,11},{4,12},{5,13},{6,14},{7,15},{8,0},{9,1},... | collective-permute-start | bytes 73736 | tf_op jit(solution)/shard_map/ppermute | solution.py:21
  30.9 3.8 %collective-permute-start.13 = (s16[1,48,256]{2,1,0:T(8,128)(2,1)S(1)}, s16[1,48,256]{2,1,0:T(8,128)(2,1)S(1)}, u32[]{:S(2)}, u32[]{:S(2)}) collective-permute-start(s16[1,48,256]{2,1,0:T(8,128)(2,1)S(1)} %get-tuple-element.36), channel_id=1, source_target_pairs={{0,4},{1,5},{2,6},{3,7},{4,0},{5,1},{6,2},{7,3},{8,12},{9,13},{10,... | collective-permute-start | bytes 73736 | tf_op jit(solution)/shard_map/ppermute | solution.py:21
  31.1 5.6 %collective-permute-start.14 = (s16[1,48,256]{2,1,0:T(8,128)(2,1)S(1)}, s16[1,48,256]{2,1,0:T(8,128)(2,1)S(1)}, u32[]{:S(2)}, u32[]{:S(2)}) collective-permute-start(s16[1,48,256]{2,1,0:T(8,128)(2,1)S(1)} %get-tuple-element.37), channel_id=1, source_target_pairs={{0,12},{1,13},{2,14},{3,15},{4,8},{5,9},{6,10},{7,11},{8,4},{9,5},... | collective-permute-start | bytes 73736 | tf_op jit(solution)/shard_map/ppermute | solution.py:21

commit v7 on v6

--- a/solution.py
+++ b/solution.py
@@ -248,22 +248,32 @@
     )(in_vmem(x))
 
 
-def decode_kernel(x_ref, q_ref, out_ref, *, at):
+def decode_kernel(x_ref, q_ref, out_ref, buf, sems, *, at):
     n, rows, _ = x_ref.shape
     groups = min(GROUPS, rows // GROUPS)
     step = rows // groups
+    parts = sems.shape[1]
+    copies = []
     for k in range(n):
         for g in range(groups):
             part = pl.ds(g * step, step)
-            out_ref[k, part, :] = x_ref[k, part, :] + decode_rows(q_ref, at + k, g, groups)
+            buf[k, part, :] = x_ref[k, part, :] + decode_rows(q_ref, at + k, g, groups)
+            if (g + 1) % (groups // parts) == 0:
+                c = g // (groups // parts)
+                done = pl.ds(c * (rows // parts), rows // parts)
+                copies.append(pltpu.make_async_copy(buf.at[k, done], out_ref.at[k, done], sems.at[k, c]))
+                copies[-1].start()
+    for c in copies:
+        c.wait()
 
 
 def add_decoded(x, q, at):
     return pl.pallas_call(
         functools.partial(decode_kernel, at=at),
         in_specs=[VM, VM],
-        out_specs=VM,
+        out_specs=pl.BlockSpec(memory_space=pltpu.HBM),
         out_shape=jax.ShapeDtypeStruct(x.shape, f32),
+        scratch_shapes=[pltpu.VMEM(x.shape, f32), pltpu.SemaphoreType.DMA((x.shape[0], 4))],
         compiler_params=PARAMS,
     )(in_vmem(x), in_vmem(q))
 

time: 37.7 us -> 37.7 us (level)
  no operation moved by 1% of the time
where the time goes in v7:
time: 37.7 us; the launch traced here: 37.4 us
  starting transfers between devices  17.2 us (46%)
  waiting for transfers between devices  12.1 us (32%)
  Pallas kernels  7.41 us (20%)
  between operations  0.77 us (2%)
    ppermute x16, starting transfers between devices, swap(): return lax.ppermute(x, axis, [(i, i ^ bits) for i in range(size)])  17.2 us
    ppermute x16, waiting for transfers between devices, swap(): return lax.ppermute(x, axis, [(i, i ^ bits) for i in range(size)])  12.1 us
    pallas_call x5, Pallas kernels, region(): pl.pallas_call(functools.partial(region_kernel, n_users=len(users), sums_...  3.31 us
    pallas_call x1, Pallas kernels, load(): pl.pallas_call(functools.partial(load_kernel, **static), in_specs=[pl.Blo...  1.61 us
    pallas_call x1, Pallas kernels, add_decoded(): pl.pallas_call(functools.partial(decode_kernel, at=at), in_specs=[VM, VM]...  0.84 us
  transfers between devices with their start and end apart: 16, of which 7 were waited for; matrix products, arithmetic and copies ran while one was open for 0% of the time, Pallas kernels for 14%

profile of v7, /device:TPU:0, one launch (start us, length us, event | category | flops | bytes accessed | tf_op | source)
XLA Modules:
  0.0 37.4 jit_solution(496142955958790907)
XLA Ops:
  0.6 0.8 %shard_map.69 = bf16[1,2,32,256]{3,2,1,0:T(8,128)(2,1)S(1)} custom-call(bf16[32,256]{1,0:T(8,128)(2,1)} %a.1, bf16[32,256]{1,0:T(8,128)(2,1)} %b.1), custom_call_target="tpu_custom_call" | custom-call | tf_op jit(solution)/shard_map/pallas_call | solution.py:200
  1.4 4.1 %collective-permute-start = (bf16[1,2,32,256]{3,2,1,0:T(8,128)(2,1)S(1)}, bf16[1,2,32,256]{3,2,1,0:T(8,128)(2,1)S(1)}, u32[]{:S(2)}, u32[]{:S(2)}) collective-permute-start(bf16[1,2,32,256]{3,2,1,0:T(8,128)(2,1)S(1)} %shard_map.69), channel_id=1, source_target_pairs={{0,8},{1,9},{2,10},{3,11},{4,12},{5,13},{6,14},{7,15},{8,0},{9,1},... | collective-permute-start | bytes 98312 | tf_op jit(solution)/shard_map/ppermute | solution.py:21
  5.5 1.5 %collective-permute-start.4 = (bf16[1,512,256]{2,1,0:T(8,128)(2,1)}, bf16[1,512,256]{2,1,0:T(8,128)(2,1)S(1)}, u32[]{:S(2)}, u32[]{:S(2)}) collective-permute-start(bf16[1,512,256]{2,1,0:T(8,128)(2,1)} %bitcast.4), channel_id=1, source_target_pairs={{0,16},{16,0},{1,17},{17,1},{2,18},{18,2},{3,19},{19,3},{4,20},{20... | collective-permute-start | bytes 786440 | tf_op jit(solution)/shard_map/ppermute | solution.py:21
  7.0 0.0 copy-start
  7.0 0.5 %collective-permute-start.5 = (bf16[1,512,256]{2,1,0:T(8,128)(2,1)}, bf16[1,512,256]{2,1,0:T(8,128)(2,1)S(1)}, u32[]{:S(2)}, u32[]{:S(2)}) collective-permute-start(bf16[1,512,256]{2,1,0:T(8,128)(2,1)} %bitcast.6), channel_id=1, source_target_pairs={{0,16},{16,0},{1,17},{17,1},{2,18},{18,2},{3,19},{19,3},{4,20},{20... | collective-permute-start | bytes 786440 | tf_op jit(solution)/shard_map/ppermute | solution.py:21
  7.5 0.2 collective-permute-done
  7.8 0.1 collective-permute-start.6
  7.9 1.6 %collective-permute-start.2 = (bf16[2,2,32,256]{3,2,1,0:T(8,128)(2,1)S(1)}, bf16[2,2,32,256]{3,2,1,0:T(8,128)(2,1)S(1)}, u32[]{:S(2)}, u32[]{:S(2)}) collective-permute-start(bf16[2,2,32,256]{3,2,1,0:T(8,128)(2,1)S(1)} %pad_maximum_fusion.refs_1_), channel_id=1, source_target_pairs={{0,4},{1,5},{2,6},{3,7},{4,0},{5,1},{6,2},{7,3},{8,12},{9,13},{10,... | collective-permute-start | bytes 196616 | tf_op jit(solution)/shard_map/ppermute | solution.py:21
  9.5 1.5 %collective-permute-start.1 = (bf16[2,2,32,256]{3,2,1,0:T(8,128)(2,1)S(1)}, bf16[2,2,32,256]{3,2,1,0:T(8,128)(2,1)S(1)}, u32[]{:S(2)}, u32[]{:S(2)}) collective-permute-start(bf16[2,2,32,256]{3,2,1,0:T(8,128)(2,1)S(1)} %pad_maximum_fusion.refs_1_), channel_id=1, source_target_pairs={{0,2},{1,3},{2,0},{3,1},{4,6},{5,7},{6,4},{7,5},{8,10},{9,11},{10,... | collective-permute-start | bytes 196616 | tf_op jit(solution)/shard_map/ppermute | solution.py:21
  11.0 0.0 collective-permute-done.6.refs_2_.refs_1_
  11.0 0.6 %collective-permute-start.3 = (bf16[2,2,32,256]{3,2,1,0:T(8,128)(2,1)S(1)}, bf16[2,2,32,256]{3,2,1,0:T(8,128)(2,1)S(1)}, u32[]{:S(2)}, u32[]{:S(2)}) collective-permute-start(bf16[2,2,32,256]{3,2,1,0:T(8,128)(2,1)S(1)} %pad_maximum_fusion.refs_1_), channel_id=1, source_target_pairs={{0,6},{1,7},{2,4},{3,5},{4,2},{5,3},{6,0},{7,1},{8,14},{9,15},{10,... | collective-permute-start | bytes 196616 | tf_op jit(solution)/shard_map/ppermute | solution.py:21
  11.6 0.8 %collective-permute-done.2.refs_3_ = bf16[2,2,32,256]{3,2,1,0:T(8,128)(2,1)S(1)} collective-permute-done((bf16[2,2,32,256]{3,2,1,0:T(8,128)(2,1)S(1)}, bf16[2,2,32,256]{3,2,1,0:T(8,128)(2,1)S(1)}, u32[]{:S(2)}, u32[]{:S(2)}) %collective-permute-start.2) | collective-permute-done | bytes 65568 | tf_op jit(solution)/shard_map/ppermute | solution.py:21
  12.4 0.0 collective-permute-start.8
  12.4 1.4 %collective-permute-done.1.refs_1_.refs_2_ = bf16[2,2,32,256]{3,2,1,0:T(8,128)(2,1)S(1)} collective-permute-done((bf16[2,2,32,256]{3,2,1,0:T(8,128)(2,1)S(1)}, bf16[2,2,32,256]{3,2,1,0:T(8,128)(2,1)S(1)}, u32[]{:S(2)}, u32[]{:S(2)}) %collective-permute-start.1) | collective-permute-done | bytes 65568 | tf_op jit(solution)/shard_map/ppermute | solution.py:21
  13.7 0.0 collective-permute-start.7
  13.7 2.4 %collective-permute-done.3.refs_1_.refs_4_ = bf16[2,2,32,256]{3,2,1,0:T(8,128)(2,1)S(1)} collective-permute-done((bf16[2,2,32,256]{3,2,1,0:T(8,128)(2,1)S(1)}, bf16[2,2,32,256]{3,2,1,0:T(8,128)(2,1)S(1)}, u32[]{:S(2)}, u32[]{:S(2)}) %collective-permute-start.3) | collective-permute-done | bytes 65568 | tf_op jit(solution)/shard_map/ppermute | solution.py:21
  16.1 0.0 collective-permute-start.9
  16.1 0.0 copy-done
  16.1 1.6 %shard_map.68 = (bf16[1,512,256]{2,1,0:T(8,128)(2,1)S(1)}, bf16[1,512,256]{2,1,0:T(8,128)(2,1)S(1)}, f32[8,256]{1,0:T(8,128)S(1)}) custom-call(s32[4,8]{1,0:T(4,128)S(1)} %copy-done, bf16[1,512,256]{2,1,0:T(8,128)(2,1)} %bitcast.5, bf16[1,512,256]{2,1,0:T(8,128)(2,1)} %bitcast.7), custom_call_target="tpu_custom_call" | custom-call | tf_op jit(solution)/shard_map/pallas_call | solution.py:178
  17.8 0.6 %shard_map.70 = (f32[2,2,32,256]{3,2,1,0:T(8,128)S(1)}, f32[1,512,256]{2,1,0:T(8,128)S(1)}) custom-call(f32[8,256]{1,0:T(8,128)S(1)} %get-tuple-element.21.refs_0_, bf16[2,2,32,256]{3,2,1,0:T(8,128)(2,1)S(1)} %pad_maximum_fusion.refs_1_, bf16[2,2,32,256]{3,2,1,0:T(8,128)(2,1)S(1)} %collective-permute-done.6.refs_2_.refs_1_, ...), custom_call_target="tpu_custom_call" | custom-call | tf_op jit(solution)/shard_map/pallas_call | solution.py:126
  18.3 0.0 collective-permute-done.8.refs_4_.refs_3_
  18.3 0.0 collective-permute-done.7.refs_2_
  18.4 0.7 %shard_map.71 = (f32[4,2,32,256]{3,2,1,0:T(8,128)S(1)}, f32[1,512,256]{2,1,0:T(8,128)S(1)}) custom-call(f32[8,256]{1,0:T(8,128)S(1)} %get-tuple-element.21.refs_0_, bf16[2,2,32,256]{3,2,1,0:T(8,128)(2,1)S(1)} %collective-permute-done.1.refs_1_.refs_2_, bf16[2,2,32,256]{3,2,1,0:T(8,128)(2,1)S(1)} %collective-permute-done.7.refs_2_, ...), custom_call_target="tpu_custom_call", output_to_operand_aliasing={{1}: (7, {})} | custom-call | tf_op jit(solution)/shard_map/pallas_call | solution.py:126
  19.1 0.0 collective-permute-done.9.refs_2_.refs_4_
  19.1 0.6 %shard_map.72 = (f32[2,2,32,256]{3,2,1,0:T(8,128)S(1)}, f32[1,512,256]{2,1,0:T(8,128)S(1)}) custom-call(f32[8,256]{1,0:T(8,128)S(1)} %get-tuple-element.21.refs_0_, bf16[2,2,32,256]{3,2,1,0:T(8,128)(2,1)S(1)} %collective-permute-done.3.refs_1_.refs_4_, ...), custom_call_target="tpu_custom_call", output_to_operand_aliasing={{1}: (5, {})} | custom-call | tf_op jit(solution)/shard_map/pallas_call | solution.py:126
  19.7 0.0 collective-permute-done.4.refs_5_
  19.7 0.0 collective-permute-done.5.refs_6_
  19.7 0.7 %shard_map.73 = (f32[4,2,32,256]{3,2,1,0:T(8,128)S(1)}, f32[1,512,256]{2,1,0:T(8,128)S(1)}) custom-call(f32[8,256]{1,0:T(8,128)S(1)} %get-tuple-element.21.refs_0_, bf16[2,2,32,256]{3,2,1,0:T(8,128)(2,1)S(1)} %collective-permute-done.6.refs_2_.refs_1_, bf16[2,2,32,256]{3,2,1,0:T(8,128)(2,1)S(1)} %collective-permute-done.7.refs_2_, ...), custom_call_target="tpu_custom_call" | custom-call | tf_op jit(solution)/shard_map/pallas_call | solution.py:126
  20.4 0.5 %collective-permute-start.10 = (f32[4,2,32,256]{3,2,1,0:T(8,128)S(1)}, f32[4,2,32,256]{3,2,1,0:T(8,128)S(1)}, u32[]{:S(2)}, u32[]{:S(2)}) collective-permute-start(f32[4,2,32,256]{3,2,1,0:T(8,128)S(1)} %get-tuple-element.31), channel_id=1, source_target_pairs={{0,1},{1,0},{2,3},{3,2},{4,5},{5,4},{6,7},{7,6},{8,9},{9,8},{10,11... | collective-permute-start | bytes 786440 | tf_op jit(solution)/shard_map/ppermute | solution.py:21
  21.0 0.7 %shard_map.74 = (f32[4,2,32,256]{3,2,1,0:T(8,128)S(1)}, f32[1,512,256]{2,1,0:T(8,128)S(1)}) custom-call(f32[8,256]{1,0:T(8,128)S(1)} %get-tuple-element.21.refs_0_, bf16[2,2,32,256]{3,2,1,0:T(8,128)(2,1)S(1)} %pad_maximum_fusion.refs_1_, bf16[2,2,32,256]{3,2,1,0:T(8,128)(2,1)S(1)} %collective-permute-done.1.refs_1_.refs_2_, ...), custom_call_target="tpu_custom_call", output_to_operand_aliasing={{1}: (10, {})} | custom-call | tf_op jit(solution)/shard_map/pallas_call | solution.py:126
  21.7 0.1 shard_map.78
  21.8 1.6 %collective-permute-start.15 = (s16[1,528,256]{2,1,0:T(8,128)(2,1)S(1)}, s16[1,528,256]{2,1,0:T(8,128)(2,1)S(1)}, u32[]{:S(2)}, u32[]{:S(2)}) collective-permute-start(s16[1,528,256]{2,1,0:T(8,128)(2,1)S(1)} %shard_map.78), channel_id=1, source_target_pairs={{0,16},{16,0},{1,17},{17,1},{2,18},{18,2},{3,19},{19,3},{4,20},{20... | collective-permute-start | bytes 811016 | tf_op jit(solution)/shard_map/ppermute | solution.py:21
  23.4 0.0 collective-permute-done.10.core_in
  23.4 0.1 shard_map.75
  23.5 0.6 %collective-permute-start.11 = (s16[1,144,256]{2,1,0:T(8,128)(2,1)S(1)}, s16[1,144,256]{2,1,0:T(8,128)(2,1)S(1)}, u32[]{:S(2)}, u32[]{:S(2)}) collective-permute-start(s16[1,144,256]{2,1,0:T(8,128)(2,1)S(1)} %get-tuple-element.33), channel_id=1, source_target_pairs={{0,2},{1,3},{2,0},{3,1},{4,6},{5,7},{6,4},{7,5},{8,10},{9,11},{10,... | collective-permute-start | bytes 221192 | tf_op jit(solution)/shard_map/ppermute | solution.py:21
  24.1 3.8 %collective-permute-done.11.q = s16[1,144,256]{2,1,0:T(8,128)(2,1)S(1)} collective-permute-done((s16[1,144,256]{2,1,0:T(8,128)(2,1)S(1)}, s16[1,144,256]{2,1,0:T(8,128)(2,1)S(1)}, u32[]{:S(2)}, u32[]{:S(2)}) %collective-permute-start.11) | collective-permute-done | bytes 73760 | tf_op jit(solution)/shard_map/ppermute | solution.py:21
  27.9 0.1 shard_map.76
  28.0 2.9 %collective-permute-start.12 = (s16[1,48,256]{2,1,0:T(8,128)(2,1)S(1)}, s16[1,48,256]{2,1,0:T(8,128)(2,1)S(1)}, u32[]{:S(2)}, u32[]{:S(2)}) collective-permute-start(s16[1,48,256]{2,1,0:T(8,128)(2,1)S(1)} %get-tuple-element.35), channel_id=1, source_target_pairs={{0,8},{1,9},{2,10},{3,11},{4,12},{5,13},{6,14},{7,15},{8,0},{9,1},... | collective-permute-start | bytes 73736 | tf_op jit(solution)/shard_map/ppermute | solution.py:21
  30.9 0.2 collective-permute-start.13
  31.1 1.3 %collective-permute-start.14 = (s16[1,48,256]{2,1,0:T(8,128)(2,1)S(1)}, s16[1,48,256]{2,1,0:T(8,128)(2,1)S(1)}, u32[]{:S(2)}, u32[]{:S(2)}) collective-permute-start(s16[1,48,256]{2,1,0:T(8,128)(2,1)S(1)} %get-tuple-element.37), channel_id=1, source_target_pairs={{0,12},{1,13},{2,14},{3,15},{4,8},{5,9},{6,10},{7,11},{8,4},{9,5},... | collective-permute-start | bytes 73736 | tf_op jit(solution)/shard_map/ppermute | solution.py:21
  32.5 0.0 collective-permute-done.15.q_ref
  32.5 0.8 %shard_map.79 = f32[1,512,256]{2,1,0:T(8,128)} custom-call(f32[1,512,256]{2,1,0:T(8,128)S(1)} %get-tuple-element.38.x_ref, s16[1,528,256]{2,1,0:T(8,128)(2,1)S(1)} %collective-permute-done.15.q_ref), custom_call_target="tpu_custom_call" | custom-call | tf_op jit(solution)/shard_map/pallas_call | solution.py:271
  33.3 0.0 collective-permute-done.12.refs_0_
  33.3 1.4 %collective-permute-done.13.refs_1_ = s16[1,48,256]{2,1,0:T(8,128)(2,1)S(1)} collective-permute-done((s16[1,48,256]{2,1,0:T(8,128)(2,1)S(1)}, s16[1,48,256]{2,1,0:T(8,128)(2,1)S(1)}, u32[]{:S(2)}, u32[]{:S(2)}) %collective-permute-start.13) | collective-permute-done | bytes 24608 | tf_op jit(solution)/shard_map/ppermute | solution.py:21
  34.7 2.0 %collective-permute-done.14.refs_2_ = s16[1,48,256]{2,1,0:T(8,128)(2,1)S(1)} collective-permute-done((s16[1,48,256]{2,1,0:T(8,128)(2,1)S(1)}, s16[1,48,256]{2,1,0:T(8,128)(2,1)S(1)}, u32[]{:S(2)}, u32[]{:S(2)}) %collective-permute-start.14) | collective-permute-done | bytes 24608 | tf_op jit(solution)/shard_map/ppermute | solution.py:21
  36.8 0.6 %shard_map.77 = f32[32,256]{1,0:T(8,128)} custom-call(f32[32,256]{1,0:T(8,128)S(1)} %get-tuple-element.34.own, s16[1,48,256]{2,1,0:T(8,128)(2,1)S(1)} %collective-permute-done.12.refs_0_, s16[1,48,256]{2,1,0:T(8,128)(2,1)S(1)} %collective-permute-done.13.refs_1_, s16[1,48,256]{2,1,0:T(8,128)(2,1)S(1)} %collective-permute-done.14.refs_2_), custom_call_target="tpu_custom_call" | custom-call | tf_op jit(solution)/shard_map/pallas_call | solution.py:342
  (1 shorter events, 0.0 us)
Async XLA Ops:
  1.4 6.4 %collective-permute-start = (bf16[1,2,32,256]{3,2,1,0:T(8,128)(2,1)S(1)}, bf16[1,2,32,256]{3,2,1,0:T(8,128)(2,1)S(1)}, u32[]{:S(2)}, u32[]{:S(2)}) collective-permute-start(bf16[1,2,32,256]{3,2,1,0:T(8,128)(2,1)S(1)} %shard_map.69), channel_id=1, source_target_pairs={{0,8},{1,9},{2,10},{3,11},{4,12},{5,13},{6,14},{7,15},{8,0},{9,1},... | collective-permute-start | bytes 98312 | tf_op jit(solution)/shard_map/ppermute | solution.py:21
  5.5 14.1 %collective-permute-start.4 = (bf16[1,512,256]{2,1,0:T(8,128)(2,1)}, bf16[1,512,256]{2,1,0:T(8,128)(2,1)S(1)}, u32[]{:S(2)}, u32[]{:S(2)}) collective-permute-start(bf16[1,512,256]{2,1,0:T(8,128)(2,1)} %bitcast.4), channel_id=1, source_target_pairs={{0,16},{16,0},{1,17},{17,1},{2,18},{18,2},{3,19},{19,3},{4,20},{20... | collective-permute-start | bytes 786440 | tf_op jit(solution)/shard_map/ppermute | solution.py:21
  7.0 9.1 %copy-start = (s32[4,8]{1,0:T(4,128)S(1)}, s32[4,8]{1,0:T(4,128)}, u32[]{:S(2)}) copy-start(s32[4,8]{1,0:T(4,128)} %mask.1) | copy-start | bytes 388
  7.0 12.6 %collective-permute-start.5 = (bf16[1,512,256]{2,1,0:T(8,128)(2,1)}, bf16[1,512,256]{2,1,0:T(8,128)(2,1)S(1)}, u32[]{:S(2)}, u32[]{:S(2)}) collective-permute-start(bf16[1,512,256]{2,1,0:T(8,128)(2,1)} %bitcast.6), channel_id=1, source_target_pairs={{0,16},{16,0},{1,17},{17,1},{2,18},{18,2},{3,19},{19,3},{4,20},{20... | collective-permute-start | bytes 786440 | tf_op jit(solution)/shard_map/ppermute | solution.py:21
  7.8 3.2 %collective-permute-start.6 = (bf16[2,2,32,256]{3,2,1,0:T(8,128)(2,1)S(1)}, bf16[2,2,32,256]{3,2,1,0:T(8,128)(2,1)S(1)}, u32[]{:S(2)}, u32[]{:S(2)}) collective-permute-start(bf16[2,2,32,256]{3,2,1,0:T(8,128)(2,1)S(1)} %pad_maximum_fusion.refs_1_), channel_id=1, source_target_pairs={{0,1},{1,0},{2,3},{3,2},{4,5},{5,4},{6,7},{7,6},{8,9},{9,8},{10,11... | collective-permute-start | bytes 196616 | tf_op jit(solution)/shard_map/ppermute | solution.py:21
  7.9 4.5 %collective-permute-start.2 = (bf16[2,2,32,256]{3,2,1,0:T(8,128)(2,1)S(1)}, bf16[2,2,32,256]{3,2,1,0:T(8,128)(2,1)S(1)}, u32[]{:S(2)}, u32[]{:S(2)}) collective-permute-start(bf16[2,2,32,256]{3,2,1,0:T(8,128)(2,1)S(1)} %pad_maximum_fusion.refs_1_), channel_id=1, source_target_pairs={{0,4},{1,5},{2,6},{3,7},{4,0},{5,1},{6,2},{7,3},{8,12},{9,13},{10,... | collective-permute-start | bytes 196616 | tf_op jit(solution)/shard_map/ppermute | solution.py:21
  9.5 4.3 %collective-permute-start.1 = (bf16[2,2,32,256]{3,2,1,0:T(8,128)(2,1)S(1)}, bf16[2,2,32,256]{3,2,1,0:T(8,128)(2,1)S(1)}, u32[]{:S(2)}, u32[]{:S(2)}) collective-permute-start(bf16[2,2,32,256]{3,2,1,0:T(8,128)(2,1)S(1)} %pad_maximum_fusion.refs_1_), channel_id=1, source_target_pairs={{0,2},{1,3},{2,0},{3,1},{4,6},{5,7},{6,4},{7,5},{8,10},{9,11},{10,... | collective-permute-start | bytes 196616 | tf_op jit(solution)/shard_map/ppermute | solution.py:21
  11.0 5.2 %collective-permute-start.3 = (bf16[2,2,32,256]{3,2,1,0:T(8,128)(2,1)S(1)}, bf16[2,2,32,256]{3,2,1,0:T(8,128)(2,1)S(1)}, u32[]{:S(2)}, u32[]{:S(2)}) collective-permute-start(bf16[2,2,32,256]{3,2,1,0:T(8,128)(2,1)S(1)} %pad_maximum_fusion.refs_1_), channel_id=1, source_target_pairs={{0,6},{1,7},{2,4},{3,5},{4,2},{5,3},{6,0},{7,1},{8,14},{9,15},{10,... | collective-permute-start | bytes 196616 | tf_op jit(solution)/shard_map/ppermute | solution.py:21
  12.4 6.0 %collective-permute-start.8 = (bf16[2,2,32,256]{3,2,1,0:T(8,128)(2,1)S(1)}, bf16[2,2,32,256]{3,2,1,0:T(8,128)(2,1)S(1)}, u32[]{:S(2)}, u32[]{:S(2)}) collective-permute-start(bf16[2,2,32,256]{3,2,1,0:T(8,128)(2,1)S(1)} %collective-permute-done.2.refs_3_), channel_id=1, source_target_pairs={{0,1},{1,0},{2,3},{3,2},{4,5},{5,4},{6,7},{7,6},{8,9},{9,8},{10,11... | collective-permute-start | bytes 196616 | tf_op jit(solution)/shard_map/ppermute | solution.py:21
  13.7 4.6 %collective-permute-start.7 = (bf16[2,2,32,256]{3,2,1,0:T(8,128)(2,1)S(1)}, bf16[2,2,32,256]{3,2,1,0:T(8,128)(2,1)S(1)}, u32[]{:S(2)}, u32[]{:S(2)}) collective-permute-start(bf16[2,2,32,256]{3,2,1,0:T(8,128)(2,1)S(1)} %collective-permute-done.1.refs_1_.refs_2_), channel_id=1, source_target_pairs={{0,1},{1,0},{2,3},{3,2},{4,5},{5,4},{6,7},{7,6},{8,9},{9,8},{10,11... | collective-permute-start | bytes 196616 | tf_op jit(solution)/shard_map/ppermute | solution.py:21
  16.1 2.9 %collective-permute-start.9 = (bf16[2,2,32,256]{3,2,1,0:T(8,128)(2,1)S(1)}, bf16[2,2,32,256]{3,2,1,0:T(8,128)(2,1)S(1)}, u32[]{:S(2)}, u32[]{:S(2)}) collective-permute-start(bf16[2,2,32,256]{3,2,1,0:T(8,128)(2,1)S(1)} %collective-permute-done.3.refs_1_.refs_4_), channel_id=1, source_target_pairs={{0,1},{1,0},{2,3},{3,2},{4,5},{5,4},{6,7},{7,6},{8,9},{9,8},{10,11... | collective-permute-start | bytes 196616 | tf_op jit(solution)/shard_map/ppermute | solution.py:21
  20.4 3.0 %collective-permute-start.10 = (f32[4,2,32,256]{3,2,1,0:T(8,128)S(1)}, f32[4,2,32,256]{3,2,1,0:T(8,128)S(1)}, u32[]{:S(2)}, u32[]{:S(2)}) collective-permute-start(f32[4,2,32,256]{3,2,1,0:T(8,128)S(1)} %get-tuple-element.31), channel_id=1, source_target_pairs={{0,1},{1,0},{2,3},{3,2},{4,5},{5,4},{6,7},{7,6},{8,9},{9,8},{10,11... | collective-permute-start | bytes 786440 | tf_op jit(solution)/shard_map/ppermute | solution.py:21
  21.8 10.6 %collective-permute-start.15 = (s16[1,528,256]{2,1,0:T(8,128)(2,1)S(1)}, s16[1,528,256]{2,1,0:T(8,128)(2,1)S(1)}, u32[]{:S(2)}, u32[]{:S(2)}) collective-permute-start(s16[1,528,256]{2,1,0:T(8,128)(2,1)S(1)} %shard_map.78), channel_id=1, source_target_pairs={{0,16},{16,0},{1,17},{17,1},{2,18},{18,2},{3,19},{19,3},{4,20},{20... | collective-permute-start | bytes 811016 | tf_op jit(solution)/shard_map/ppermute | solution.py:21
  23.5 4.4 %collective-permute-start.11 = (s16[1,144,256]{2,1,0:T(8,128)(2,1)S(1)}, s16[1,144,256]{2,1,0:T(8,128)(2,1)S(1)}, u32[]{:S(2)}, u32[]{:S(2)}) collective-permute-start(s16[1,144,256]{2,1,0:T(8,128)(2,1)S(1)} %get-tuple-element.33), channel_id=1, source_target_pairs={{0,2},{1,3},{2,0},{3,1},{4,6},{5,7},{6,4},{7,5},{8,10},{9,11},{10,... | collective-permute-start | bytes 221192 | tf_op jit(solution)/shard_map/ppermute | solution.py:21
  28.0 5.3 %collective-permute-start.12 = (s16[1,48,256]{2,1,0:T(8,128)(2,1)S(1)}, s16[1,48,256]{2,1,0:T(8,128)(2,1)S(1)}, u32[]{:S(2)}, u32[]{:S(2)}) collective-permute-start(s16[1,48,256]{2,1,0:T(8,128)(2,1)S(1)} %get-tuple-element.35), channel_id=1, source_target_pairs={{0,8},{1,9},{2,10},{3,11},{4,12},{5,13},{6,14},{7,15},{8,0},{9,1},... | collective-permute-start | bytes 73736 | tf_op jit(solution)/shard_map/ppermute | solution.py:21
  30.9 3.8 %collective-permute-start.13 = (s16[1,48,256]{2,1,0:T(8,128)(2,1)S(1)}, s16[1,48,256]{2,1,0:T(8,128)(2,1)S(1)}, u32[]{:S(2)}, u32[]{:S(2)}) collective-permute-start(s16[1,48,256]{2,1,0:T(8,128)(2,1)S(1)} %get-tuple-element.36), channel_id=1, source_target_pairs={{0,4},{1,5},{2,6},{3,7},{4,0},{5,1},{6,2},{7,3},{8,12},{9,13},{10,... | collective-permute-start | bytes 73736 | tf_op jit(solution)/shard_map/ppermute | solution.py:21
  31.1 5.6 %collective-permute-start.14 = (s16[1,48,256]{2,1,0:T(8,128)(2,1)S(1)}, s16[1,48,256]{2,1,0:T(8,128)(2,1)S(1)}, u32[]{:S(2)}, u32[]{:S(2)}) collective-permute-start(s16[1,48,256]{2,1,0:T(8,128)(2,1)S(1)} %get-tuple-element.37), channel_id=1, source_target_pairs={{0,12},{1,13},{2,14},{3,15},{4,8},{5,9},{6,10},{7,11},{8,4},{9,5},... | collective-permute-start | bytes 73736 | tf_op jit(solution)/shard_map/ppermute | solution.py:21

commit v8 on v7

--- a/solution.py
+++ b/solution.py
@@ -37,7 +37,12 @@
     return order
 
 
-def region_kernel(*refs, n_users, sums_at, n_sums, add_item, lanes, cols, scale):
+def spread_seen(seen_ref, at, n, block, lanes, tile):
+    rows = [jnp.broadcast_to(seen_ref[pl.ds(at + i, 1), pl.ds(lanes, tile)], (block, tile)) for i in range(n)]
+    return jnp.concatenate(rows, 0)
+
+
+def region_kernel(*refs, n_users, sums_at, n_sums, add_item, lanes, cols, scale, prepared):
     seen_ref = refs[0]
     users = refs[1 : 1 + n_users]
     at = 1 + n_users
@@ -47,6 +52,10 @@
     at += n_sums
     item_in = refs[at] if add_item else None
     at += add_item
+    ready = None
+    if prepared is not None:
+        ready = refs[at : at + 2]
+        at += 2
     user_out, item_out, u_all, c_all = refs[at:]
 
     n_a, _, us, _ = users[0].shape
@@ -71,6 +80,11 @@
                 items = pl.ds(ib * sub, sub)
                 v = fac_i[k, items, :]
                 dv = tan_i[k, items, :]
+                if ready is not None:
+                    weight, tt = (x[prepared + t, items, :] for x in ready)
+                    c = (weight * (tt + dot(dv, fac, NT))).astype(bf16)
+                    c_all[k, items, pl.ds(0, tile)] = c
+                    continue
                 if 2 * tile <= TILE:
                     both = dot(v, jnp.concatenate([fac, tan], 0), NT)
                     s = both[:, :tile]
@@ -78,13 +92,8 @@
                 else:
                     s = dot(v, fac, NT)
                     tt = dot(v, tan, NT) + dot(dv, fac, NT)
-                seen = []
-                for i in range(sub // block):
-                    row = seen_ref[
-                        pl.ds((cols[0] + k) * blocks + ib * (sub // block) + i, 1), pl.ds(lanes + t * tile, tile)
-                    ]
-                    seen.append(jnp.broadcast_to(row, (block, tile)))
-                seen = jnp.concatenate(seen, 0)
+                at_col = (cols[0] + k) * blocks + ib * (sub // block)
+                seen = spread_seen(seen_ref, at_col, sub // block, block, lanes + t * tile, tile)
                 e = jnp.exp(jnp.abs(s) * -scale)
                 p = 1.0 / (1.0 + e)
                 c = (e * p * p * (tt * seen)).astype(bf16)
@@ -106,6 +115,34 @@
             user_out[b, k] = r
 
 
+def prepare_kernel(*refs, n_users, cols, scale):
+    seen_ref = refs[0]
+    users = refs[1 : 1 + n_users]
+    fac_i, weight, part, u_all = refs[1 + n_users :]
+    n_a, _, us, _ = users[0].shape
+    tile = weight.shape[2]
+    it_dev = fac_i.shape[1]
+    block = it_dev // cols[1]
+    for b, ref in enumerate(users):
+        for k in range(n_a):
+            for ft in range(2):
+                u_all[ft, pl.ds((b * n_a + k) * us, us), :] = ref[k, ft]
+    sub = min(TILE, it_dev)
+    for t in range(weight.shape[0]):
+        fac = u_all[0, pl.ds(t * tile, tile), :]
+        tan = u_all[1, pl.ds(t * tile, tile), :]
+        for ib in range(it_dev // sub):
+            items = pl.ds(ib * sub, sub)
+            v = fac_i[0, items, :]
+            s = dot(v, fac, NT)
+            part[t, items, :] = dot(v, tan, NT)
+            at_col = cols[0] * cols[1] + ib * (sub // block)
+            seen = spread_seen(seen_ref, at_col, sub // block, block, t * tile % seen_ref.shape[1], tile)
+            e = jnp.exp(jnp.abs(s) * -scale)
+            p = 1.0 / (1.0 + e)
+            weight[t, items, :] = e * p * p * seen
+
+
 def in_vmem(x):
     return pltpu.with_memory_space_constraint(x, pltpu.VMEM)
 
@@ -114,7 +151,7 @@
 PARAMS = pltpu.CompilerParams(vmem_limit_bytes=16 * 2**20)
 
 
-def region(seen, users, items, sums, sums_at, item_sum, **static):
+def region(seen, users, items, sums, sums_at, item_sum, ready=(), prepared=None, **static):
     n_a, _, us, width = users[0].shape
     n_pieces, it_dev, _ = items[0].shape
     given = [in_vmem(x) for x in (seen, *users, *items, *sums)]
@@ -122,6 +159,7 @@
     if item_sum is not None:
         aliases[len(given)] = 1
         given.append(in_vmem(item_sum))
+    given += [in_vmem(x) for x in ready]
     total_rows = len(users) * n_a * us
     return pl.pallas_call(
         functools.partial(
@@ -130,6 +168,7 @@
             sums_at=sums_at,
             n_sums=len(sums),
             add_item=item_sum is not None,
+            prepared=prepared,
             **static,
         ),
         in_specs=[VM] * len(given),
@@ -147,6 +186,21 @@
     )(*given)
 
 
+def prepare(seen, users, fac, **static):
+    n_a, _, us, width = users[0].shape
+    rows = len(users) * n_a * us
+    tile = min(TILE, rows // 2)
+    shape = (rows // tile, fac.shape[1], tile)
+    return pl.pallas_call(
+        functools.partial(prepare_kernel, n_users=len(users), **static),
+        in_specs=[VM] * (2 + len(users)),
+        out_specs=[VM] * 2,
+        out_shape=[pltpu.VMEM(shape, f32)] * 2,
+        scratch_shapes=[pltpu.VMEM((2, rows, width), bf16)],
+        compiler_params=PARAMS,
+    )(*[in_vmem(x) for x in (seen, *users, fac)])
+
+
 def load_kernel(mask, fac, tan, fac_out, tan_out, seen, sems, *, rows_of, cols_of, us, scale):
     copies = [
         pltpu.make_async_copy(fac, fac_out, sems.at[0]),
@@ -159,12 +213,15 @@
     me_row = lax.axis_index("ia") // members
     me_col = lax.axis_index("au")
     lane = lax.broadcasted_iota(jnp.int32, (1, seen.shape[1]), 1)
+    col = lax.broadcasted_iota(jnp.int32, (1, mask.shape[1]), 1)
+    lines = {r: mask[pl.ds(me_row ^ r, 1), :].astype(f32) * scale for r in sorted(set(rows))}
     for q, rel in enumerate(order):
         for i in range(per):
-            value = {r: mask[me_row ^ r, (me_col ^ rel) * per + i].astype(f32) * scale for r in sorted(set(rows))}
+            here = col == (me_col ^ rel) * per + i
+            value = {r: jnp.sum(jnp.where(here, x, 0.0), 1, keepdims=True) for r, x in lines.items()}
             line = None
             for j in reversed(range(len(rows))):
-                full = jnp.full(lane.shape, value[rows[j]], f32)
+                full = jnp.broadcast_to(value[rows[j]], lane.shape)
                 line = full if line is None else jnp.where(lane < (j + 1) * us, full, line)
             seen[pl.ds(q * per + i, 1), :] = line
     for c in copies:
@@ -177,12 +234,12 @@
     lanes = len(static["rows_of"][1]) * static["us"]
     return pl.pallas_call(
         functools.partial(load_kernel, **static),
-        in_specs=[pl.BlockSpec(memory_space=pltpu.SMEM)] + [pl.BlockSpec(memory_space=pltpu.HBM)] * 2,
+        in_specs=[VM] + [pl.BlockSpec(memory_space=pltpu.HBM)] * 2,
         out_specs=[VM] * 3,
         out_shape=[pltpu.VMEM(fac.shape, fac.dtype), pltpu.VMEM(tan.shape, tan.dtype), pltpu.VMEM((blocks, lanes), f32)],
         scratch_shapes=[pltpu.SemaphoreType.DMA((2,))],
         compiler_params=PARAMS,
-    )(mask, *hbm)
+    )(in_vmem(mask), *hbm)
 
 
 def stack_kernel(a, b, out, sems):
@@ -380,10 +437,10 @@
     mine = [far] + [swap(far, "ia", n_ia, b) for b in near[1:]]
     other = [swap(x, "ia", n_ia, core) for x in mine]
 
-    def call(users, g, sums, sums_at, item_sum, lanes=0):
+    def call(users, g, sums, sums_at, item_sum, lanes=0, **extra):
         at = sum(f.shape[0] for f in facs[:g])
         return region(
-            seen, users, (facs[g], tans[g]), sums, sums_at, item_sum, lanes=lanes, cols=(at, per), scale=scale
+            seen, users, (facs[g], tans[g]), sums, sums_at, item_sum, lanes=lanes, cols=(at, per), scale=scale, **extra
         )
 
     first, item_sum = call([mine[0], other[0]], 0, [], None, None)
@@ -393,8 +450,13 @@
     at_mine, at_other = [(0, 0), (1, 0), (1, 2), (2, 0)], [(0, 1), (1, 1), (1, 3), (2, 1)]
     item_sums = [own_items]
     for g in range(1, len(facs)):
-        out_other, item_sum = call(other, g, sums, at_other, None)
-        out_mine, item_sum = call(mine, g, sums, at_mine, item_sum)
+        first, second = {}, {}
+        if facs[g].shape[0] == 1:
+            ready = prepare(seen, [*other, *mine], facs[g], cols=(g, per), scale=scale)
+            first = {"ready": ready, "prepared": 0}
+            second = {"ready": ready, "prepared": ready[0].shape[0] // 2}
+        out_other, item_sum = call(other, g, sums, at_other, None, **first)
+        out_mine, item_sum = call(mine, g, sums, at_mine, item_sum, **second)
         item_sums.append(item_sum)
         sums = [out_mine, out_other]
         at_mine, at_other = [(0, i) for i in range(4)], [(1, i) for i in range(4)]

time: 37.7 us -> 37.4 us (level)
    pallas_call x1 -> x2, Pallas kernels: 1.61 us -> 1.58 us  [the longest x1 1.05 us: load(): pl.pallas_call(functools.partial(load_kernel, **static), in_specs=[VM] +...]
where the time goes in v8:
time: 37.4 us; the launch traced here: 37 us
  starting transfers between devices  17.1 us (46%)
  waiting for transfers between devices  12.1 us (32%)
  Pallas kernels  7.06 us (19%)
  between operations  0.77 us (2%)
    ppermute x16, starting transfers between devices, swap(): return lax.ppermute(x, axis, [(i, i ^ bits) for i in range(size)])  17.1 us
    ppermute x16, waiting for transfers between devices, swap(): return lax.ppermute(x, axis, [(i, i ^ bits) for i in range(size)])  12.1 us
    pallas_call x5, Pallas kernels, region(): pl.pallas_call(functools.partial(region_kernel, n_users=len(users), sums_...  2.98 us
    pallas_call x1, Pallas kernels, load(): pl.pallas_call(functools.partial(load_kernel, **static), in_specs=[VM] +...  1.05 us
    pallas_call x1, Pallas kernels, add_decoded(): pl.pallas_call(functools.partial(decode_kernel, at=at), in_specs=[VM, VM]...  0.84 us
    pallas_call x1, Pallas kernels, stack(): pl.pallas_call(stack_kernel, in_specs=[pl.BlockSpec(memory_space=pltpu.HB...  0.75 us
  transfers between devices with their start and end apart: 16, of which 7 were waited for; matrix products, arithmetic and copies ran while one was open for 0% of the time, Pallas kernels for 14%

profile of v8, /device:TPU:0, one launch (start us, length us, event | category | flops | bytes accessed | tf_op | source)
XLA Modules:
  0.0 37.0 jit_solution(14956430058825895490)
XLA Ops:
  0.6 0.8 %shard_map.69 = bf16[1,2,32,256]{3,2,1,0:T(8,128)(2,1)S(1)} custom-call(bf16[32,256]{1,0:T(8,128)(2,1)} %a.1, bf16[32,256]{1,0:T(8,128)(2,1)} %b.1), custom_call_target="tpu_custom_call" | custom-call | tf_op jit(solution)/shard_map/pallas_call | solution.py:257
  1.4 4.1 %collective-permute-start = (bf16[1,2,32,256]{3,2,1,0:T(8,128)(2,1)S(1)}, bf16[1,2,32,256]{3,2,1,0:T(8,128)(2,1)S(1)}, u32[]{:S(2)}, u32[]{:S(2)}) collective-permute-start(bf16[1,2,32,256]{3,2,1,0:T(8,128)(2,1)S(1)} %shard_map.69), channel_id=1, source_target_pairs={{0,8},{1,9},{2,10},{3,11},{4,12},{5,13},{6,14},{7,15},{8,0},{9,1},... | collective-permute-start | bytes 98312 | tf_op jit(solution)/shard_map/ppermute | solution.py:21
  5.5 1.5 %collective-permute-start.4 = (bf16[1,512,256]{2,1,0:T(8,128)(2,1)}, bf16[1,512,256]{2,1,0:T(8,128)(2,1)S(1)}, u32[]{:S(2)}, u32[]{:S(2)}) collective-permute-start(bf16[1,512,256]{2,1,0:T(8,128)(2,1)} %bitcast.4), channel_id=1, source_target_pairs={{0,16},{16,0},{1,17},{17,1},{2,18},{18,2},{3,19},{19,3},{4,20},{20... | collective-permute-start | bytes 786440 | tf_op jit(solution)/shard_map/ppermute | solution.py:21
  7.0 0.0 copy-start
  7.0 0.5 %collective-permute-start.5 = (bf16[1,512,256]{2,1,0:T(8,128)(2,1)}, bf16[1,512,256]{2,1,0:T(8,128)(2,1)S(1)}, u32[]{:S(2)}, u32[]{:S(2)}) collective-permute-start(bf16[1,512,256]{2,1,0:T(8,128)(2,1)} %bitcast.6), channel_id=1, source_target_pairs={{0,16},{16,0},{1,17},{17,1},{2,18},{18,2},{3,19},{19,3},{4,20},{20... | collective-permute-start | bytes 786440 | tf_op jit(solution)/shard_map/ppermute | solution.py:21
  7.5 0.2 collective-permute-done
  7.8 0.1 collective-permute-start.6
  7.9 1.6 %collective-permute-start.2 = (bf16[2,2,32,256]{3,2,1,0:T(8,128)(2,1)S(1)}, bf16[2,2,32,256]{3,2,1,0:T(8,128)(2,1)S(1)}, u32[]{:S(2)}, u32[]{:S(2)}) collective-permute-start(bf16[2,2,32,256]{3,2,1,0:T(8,128)(2,1)S(1)} %pad_maximum_fusion.refs_1_.refs_5_), channel_id=1, source_target_pairs={{0,4},{1,5},{2,6},{3,7},{4,0},{5,1},{6,2},{7,3},{8,12},{9,13},{10,... | collective-permute-start | bytes 196616 | tf_op jit(solution)/shard_map/ppermute | solution.py:21
  9.5 1.5 %collective-permute-start.1 = (bf16[2,2,32,256]{3,2,1,0:T(8,128)(2,1)S(1)}, bf16[2,2,32,256]{3,2,1,0:T(8,128)(2,1)S(1)}, u32[]{:S(2)}, u32[]{:S(2)}) collective-permute-start(bf16[2,2,32,256]{3,2,1,0:T(8,128)(2,1)S(1)} %pad_maximum_fusion.refs_1_.refs_5_), channel_id=1, source_target_pairs={{0,2},{1,3},{2,0},{3,1},{4,6},{5,7},{6,4},{7,5},{8,10},{9,11},{10,... | collective-permute-start | bytes 196616 | tf_op jit(solution)/shard_map/ppermute | solution.py:21
  11.0 0.0 collective-permute-done.6.refs_2_.refs_1_
  11.0 0.6 %collective-permute-start.3 = (bf16[2,2,32,256]{3,2,1,0:T(8,128)(2,1)S(1)}, bf16[2,2,32,256]{3,2,1,0:T(8,128)(2,1)S(1)}, u32[]{:S(2)}, u32[]{:S(2)}) collective-permute-start(bf16[2,2,32,256]{3,2,1,0:T(8,128)(2,1)S(1)} %pad_maximum_fusion.refs_1_.refs_5_), channel_id=1, source_target_pairs={{0,6},{1,7},{2,4},{3,5},{4,2},{5,3},{6,0},{7,1},{8,14},{9,15},{10,... | collective-permute-start | bytes 196616 | tf_op jit(solution)/shard_map/ppermute | solution.py:21
  11.6 0.8 %collective-permute-done.2.refs_3_.refs_7_ = bf16[2,2,32,256]{3,2,1,0:T(8,128)(2,1)S(1)} collective-permute-done((bf16[2,2,32,256]{3,2,1,0:T(8,128)(2,1)S(1)}, bf16[2,2,32,256]{3,2,1,0:T(8,128)(2,1)S(1)}, u32[]{:S(2)}, u32[]{:S(2)}) %collective-permute-start.2) | collective-permute-done | bytes 65568 | tf_op jit(solution)/shard_map/ppermute | solution.py:21
  12.4 0.0 collective-permute-start.8
  12.4 1.4 %collective-permute-done.1.refs_1_.refs_6_.refs_2_ = bf16[2,2,32,256]{3,2,1,0:T(8,128)(2,1)S(1)} collective-permute-done((bf16[2,2,32,256]{3,2,1,0:T(8,128)(2,1)S(1)}, bf16[2,2,32,256]{3,2,1,0:T(8,128)(2,1)S(1)}, u32[]{:S(2)}, u32[]{:S(2)}) %collective-permute-start.1) | collective-permute-done | bytes 65568 | tf_op jit(solution)/shard_map/ppermute | solution.py:21
  13.7 0.0 collective-permute-start.7
  13.7 2.4 %collective-permute-done.3.refs_1_.refs_8_.refs_4_ = bf16[2,2,32,256]{3,2,1,0:T(8,128)(2,1)S(1)} collective-permute-done((bf16[2,2,32,256]{3,2,1,0:T(8,128)(2,1)S(1)}, bf16[2,2,32,256]{3,2,1,0:T(8,128)(2,1)S(1)}, u32[]{:S(2)}, u32[]{:S(2)}) %collective-permute-start.3) | collective-permute-done | bytes 65568 | tf_op jit(solution)/shard_map/ppermute | solution.py:21
  16.1 0.0 collective-permute-start.9
  16.1 0.0 copy-done
  16.1 1.0 %shard_map.68 = (bf16[1,512,256]{2,1,0:T(8,128)(2,1)S(1)}, bf16[1,512,256]{2,1,0:T(8,128)(2,1)S(1)}, f32[8,256]{1,0:T(8,128)S(1)}) custom-call(s32[4,8]{1,0:T(4,128)S(1)} %copy-done, bf16[1,512,256]{2,1,0:T(8,128)(2,1)} %bitcast.5, bf16[1,512,256]{2,1,0:T(8,128)(2,1)} %bitcast.7), custom_call_target="tpu_custom_call" | custom-call | tf_op jit(solution)/shard_map/pallas_call | solution.py:235
  17.2 0.6 %shard_map.70 = (f32[2,2,32,256]{3,2,1,0:T(8,128)S(1)}, f32[1,512,256]{2,1,0:T(8,128)S(1)}) custom-call(f32[8,256]{1,0:T(8,128)S(1)} %get-tuple-element.23.refs_0_, bf16[2,2,32,256]{3,2,1,0:T(8,128)(2,1)S(1)} %pad_maximum_fusion.refs_1_.refs_5_, bf16[2,2,32,256]{3,2,1,0:T(8,128)(2,1)S(1)} %collective-permute-done.6.refs_2_.refs_1_, ...), custom_call_target="tpu_custom_call" | custom-call | tf_op jit(solution)/shard_map/pallas_call | solution.py:164
  17.8 0.0 collective-permute-done.8.refs_4_.refs_3_
  17.8 0.0 collective-permute-done.7.refs_2_
  17.8 0.7 %shard_map.71 = (f32[4,2,32,256]{3,2,1,0:T(8,128)S(1)}, f32[1,512,256]{2,1,0:T(8,128)S(1)}) custom-call(f32[8,256]{1,0:T(8,128)S(1)} %get-tuple-element.23.refs_0_, bf16[2,2,32,256]{3,2,1,0:T(8,128)(2,1)S(1)} %collective-permute-done.1.refs_1_.refs_6_.refs_2_, ...), custom_call_target="tpu_custom_call", output_to_operand_aliasing={{1}: (7, {})} | custom-call | tf_op jit(solution)/shard_map/pallas_call | solution.py:164
  18.5 0.0 collective-permute-done.9.refs_2_.refs_4_
  18.5 0.6 %shard_map.72 = (f32[2,2,32,256]{3,2,1,0:T(8,128)S(1)}, f32[1,512,256]{2,1,0:T(8,128)S(1)}) custom-call(f32[8,256]{1,0:T(8,128)S(1)} %get-tuple-element.23.refs_0_, bf16[2,2,32,256]{3,2,1,0:T(8,128)(2,1)S(1)} %collective-permute-done.3.refs_1_.refs_8_.refs_4_, ...), custom_call_target="tpu_custom_call", output_to_operand_aliasing={{1}: (5, {})} | custom-call | tf_op jit(solution)/shard_map/pallas_call | solution.py:164
  19.1 0.0 collective-permute-done.4.refs_9_.refs_5_
  19.1 0.5 %shard_map.73 = (f32[2,512,256]{2,1,0:T(8,128)S(1)}, f32[2,512,256]{2,1,0:T(8,128)S(1)}) custom-call(f32[8,256]{1,0:T(8,128)S(1)} %get-tuple-element.23.refs_0_, bf16[2,2,32,256]{3,2,1,0:T(8,128)(2,1)S(1)} %collective-permute-done.6.refs_2_.refs_1_, bf16[2,2,32,256]{3,2,1,0:T(8,128)(2,1)S(1)} %collective-permute-done.7.refs_2_, ...), custom_call_target="tpu_custom_call" | custom-call | tf_op jit(solution)/shard_map/pallas_call | solution.py:194
  19.6 0.0 collective-permute-done.5.refs_6_
  19.7 0.6 %shard_map.74 = (f32[4,2,32,256]{3,2,1,0:T(8,128)S(1)}, f32[1,512,256]{2,1,0:T(8,128)S(1)}) custom-call(f32[8,256]{1,0:T(8,128)S(1)} %get-tuple-element.23.refs_0_, bf16[2,2,32,256]{3,2,1,0:T(8,128)(2,1)S(1)} %collective-permute-done.6.refs_2_.refs_1_, bf16[2,2,32,256]{3,2,1,0:T(8,128)(2,1)S(1)} %collective-permute-done.7.refs_2_, ...), custom_call_target="tpu_custom_call" | custom-call | tf_op jit(solution)/shard_map/pallas_call | solution.py:164
  20.2 0.6 %collective-permute-start.10 = (f32[4,2,32,256]{3,2,1,0:T(8,128)S(1)}, f32[4,2,32,256]{3,2,1,0:T(8,128)S(1)}, u32[]{:S(2)}, u32[]{:S(2)}) collective-permute-start(f32[4,2,32,256]{3,2,1,0:T(8,128)S(1)} %get-tuple-element.35), channel_id=1, source_target_pairs={{0,1},{1,0},{2,3},{3,2},{4,5},{5,4},{6,7},{7,6},{8,9},{9,8},{10,11... | collective-permute-start | bytes 786440 | tf_op jit(solution)/shard_map/ppermute | solution.py:21
  20.8 0.6 %shard_map.75 = (f32[4,2,32,256]{3,2,1,0:T(8,128)S(1)}, f32[1,512,256]{2,1,0:T(8,128)S(1)}) custom-call(f32[8,256]{1,0:T(8,128)S(1)} %get-tuple-element.23.refs_0_, bf16[2,2,32,256]{3,2,1,0:T(8,128)(2,1)S(1)} %pad_maximum_fusion.refs_1_.refs_5_, ...), custom_call_target="tpu_custom_call", output_to_operand_aliasing={{1}: (10, {})} | custom-call | tf_op jit(solution)/shard_map/pallas_call | solution.py:164
  21.4 0.1 shard_map.79
  21.5 1.6 %collective-permute-start.15 = (s16[1,528,256]{2,1,0:T(8,128)(2,1)S(1)}, s16[1,528,256]{2,1,0:T(8,128)(2,1)S(1)}, u32[]{:S(2)}, u32[]{:S(2)}) collective-permute-start(s16[1,528,256]{2,1,0:T(8,128)(2,1)S(1)} %shard_map.79), channel_id=1, source_target_pairs={{0,16},{16,0},{1,17},{17,1},{2,18},{18,2},{3,19},{19,3},{4,20},{20... | collective-permute-start | bytes 811016 | tf_op jit(solution)/shard_map/ppermute | solution.py:21
  23.1 0.0 collective-permute-done.10.core_in
  23.1 0.1 shard_map.76
  23.2 0.6 %collective-permute-start.11 = (s16[1,144,256]{2,1,0:T(8,128)(2,1)S(1)}, s16[1,144,256]{2,1,0:T(8,128)(2,1)S(1)}, u32[]{:S(2)}, u32[]{:S(2)}) collective-permute-start(s16[1,144,256]{2,1,0:T(8,128)(2,1)S(1)} %get-tuple-element.37), channel_id=1, source_target_pairs={{0,2},{1,3},{2,0},{3,1},{4,6},{5,7},{6,4},{7,5},{8,10},{9,11},{10,... | collective-permute-start | bytes 221192 | tf_op jit(solution)/shard_map/ppermute | solution.py:21
  23.7 3.8 %collective-permute-done.11.q = s16[1,144,256]{2,1,0:T(8,128)(2,1)S(1)} collective-permute-done((s16[1,144,256]{2,1,0:T(8,128)(2,1)S(1)}, s16[1,144,256]{2,1,0:T(8,128)(2,1)S(1)}, u32[]{:S(2)}, u32[]{:S(2)}) %collective-permute-start.11) | collective-permute-done | bytes 73760 | tf_op jit(solution)/shard_map/ppermute | solution.py:21
  27.6 0.1 shard_map.77
  27.7 2.9 %collective-permute-start.12 = (s16[1,48,256]{2,1,0:T(8,128)(2,1)S(1)}, s16[1,48,256]{2,1,0:T(8,128)(2,1)S(1)}, u32[]{:S(2)}, u32[]{:S(2)}) collective-permute-start(s16[1,48,256]{2,1,0:T(8,128)(2,1)S(1)} %get-tuple-element.39), channel_id=1, source_target_pairs={{0,8},{1,9},{2,10},{3,11},{4,12},{5,13},{6,14},{7,15},{8,0},{9,1},... | collective-permute-start | bytes 73736 | tf_op jit(solution)/shard_map/ppermute | solution.py:21
  30.5 0.2 collective-permute-start.13
  30.8 1.3 %collective-permute-start.14 = (s16[1,48,256]{2,1,0:T(8,128)(2,1)S(1)}, s16[1,48,256]{2,1,0:T(8,128)(2,1)S(1)}, u32[]{:S(2)}, u32[]{:S(2)}) collective-permute-start(s16[1,48,256]{2,1,0:T(8,128)(2,1)S(1)} %get-tuple-element.41), channel_id=1, source_target_pairs={{0,12},{1,13},{2,14},{3,15},{4,8},{5,9},{6,10},{7,11},{8,4},{9,5},... | collective-permute-start | bytes 73736 | tf_op jit(solution)/shard_map/ppermute | solution.py:21
  32.1 0.0 collective-permute-done.15.q_ref
  32.1 0.8 %shard_map.80 = f32[1,512,256]{2,1,0:T(8,128)} custom-call(f32[1,512,256]{2,1,0:T(8,128)S(1)} %get-tuple-element.42.x_ref, s16[1,528,256]{2,1,0:T(8,128)(2,1)S(1)} %collective-permute-done.15.q_ref), custom_call_target="tpu_custom_call" | custom-call | tf_op jit(solution)/shard_map/pallas_call | solution.py:328
  33.0 0.0 collective-permute-done.12.refs_0_
  33.0 1.4 %collective-permute-done.13.refs_1_ = s16[1,48,256]{2,1,0:T(8,128)(2,1)S(1)} collective-permute-done((s16[1,48,256]{2,1,0:T(8,128)(2,1)S(1)}, s16[1,48,256]{2,1,0:T(8,128)(2,1)S(1)}, u32[]{:S(2)}, u32[]{:S(2)}) %collective-permute-start.13) | collective-permute-done | bytes 24608 | tf_op jit(solution)/shard_map/ppermute | solution.py:21
  34.4 2.0 %collective-permute-done.14.refs_2_ = s16[1,48,256]{2,1,0:T(8,128)(2,1)S(1)} collective-permute-done((s16[1,48,256]{2,1,0:T(8,128)(2,1)S(1)}, s16[1,48,256]{2,1,0:T(8,128)(2,1)S(1)}, u32[]{:S(2)}, u32[]{:S(2)}) %collective-permute-start.14) | collective-permute-done | bytes 24608 | tf_op jit(solution)/shard_map/ppermute | solution.py:21
  36.4 0.6 %shard_map.78 = f32[32,256]{1,0:T(8,128)} custom-call(f32[32,256]{1,0:T(8,128)S(1)} %get-tuple-element.38.own, s16[1,48,256]{2,1,0:T(8,128)(2,1)S(1)} %collective-permute-done.12.refs_0_, s16[1,48,256]{2,1,0:T(8,128)(2,1)S(1)} %collective-permute-done.13.refs_1_, s16[1,48,256]{2,1,0:T(8,128)(2,1)S(1)} %collective-permute-done.14.refs_2_), custom_call_target="tpu_custom_call" | custom-call | tf_op jit(solution)/shard_map/pallas_call | solution.py:399
  (1 shorter events, 0.0 us)
Async XLA Ops:
  1.4 6.4 %collective-permute-start = (bf16[1,2,32,256]{3,2,1,0:T(8,128)(2,1)S(1)}, bf16[1,2,32,256]{3,2,1,0:T(8,128)(2,1)S(1)}, u32[]{:S(2)}, u32[]{:S(2)}) collective-permute-start(bf16[1,2,32,256]{3,2,1,0:T(8,128)(2,1)S(1)} %shard_map.69), channel_id=1, source_target_pairs={{0,8},{1,9},{2,10},{3,11},{4,12},{5,13},{6,14},{7,15},{8,0},{9,1},... | collective-permute-start | bytes 98312 | tf_op jit(solution)/shard_map/ppermute | solution.py:21
  5.5 13.6 %collective-permute-start.4 = (bf16[1,512,256]{2,1,0:T(8,128)(2,1)}, bf16[1,512,256]{2,1,0:T(8,128)(2,1)S(1)}, u32[]{:S(2)}, u32[]{:S(2)}) collective-permute-start(bf16[1,512,256]{2,1,0:T(8,128)(2,1)} %bitcast.4), channel_id=1, source_target_pairs={{0,16},{16,0},{1,17},{17,1},{2,18},{18,2},{3,19},{19,3},{4,20},{20... | collective-permute-start | bytes 786440 | tf_op jit(solution)/shard_map/ppermute | solution.py:21
  7.0 9.1 %copy-start = (s32[4,8]{1,0:T(4,128)S(1)}, s32[4,8]{1,0:T(4,128)}, u32[]{:S(2)}) copy-start(s32[4,8]{1,0:T(4,128)} %mask.1) | copy-start | bytes 388
  7.0 12.6 %collective-permute-start.5 = (bf16[1,512,256]{2,1,0:T(8,128)(2,1)}, bf16[1,512,256]{2,1,0:T(8,128)(2,1)S(1)}, u32[]{:S(2)}, u32[]{:S(2)}) collective-permute-start(bf16[1,512,256]{2,1,0:T(8,128)(2,1)} %bitcast.6), channel_id=1, source_target_pairs={{0,16},{16,0},{1,17},{17,1},{2,18},{18,2},{3,19},{19,3},{4,20},{20... | collective-permute-start | bytes 786440 | tf_op jit(solution)/shard_map/ppermute | solution.py:21
  7.8 3.2 %collective-permute-start.6 = (bf16[2,2,32,256]{3,2,1,0:T(8,128)(2,1)S(1)}, bf16[2,2,32,256]{3,2,1,0:T(8,128)(2,1)S(1)}, u32[]{:S(2)}, u32[]{:S(2)}) collective-permute-start(bf16[2,2,32,256]{3,2,1,0:T(8,128)(2,1)S(1)} %pad_maximum_fusion.refs_1_.refs_5_), channel_id=1, source_target_pairs={{0,1},{1,0},{2,3},{3,2},{4,5},{5,4},{6,7},{7,6},{8,9},{9,8},{10,11... | collective-permute-start | bytes 196616 | tf_op jit(solution)/shard_map/ppermute | solution.py:21
  7.9 4.5 %collective-permute-start.2 = (bf16[2,2,32,256]{3,2,1,0:T(8,128)(2,1)S(1)}, bf16[2,2,32,256]{3,2,1,0:T(8,128)(2,1)S(1)}, u32[]{:S(2)}, u32[]{:S(2)}) collective-permute-start(bf16[2,2,32,256]{3,2,1,0:T(8,128)(2,1)S(1)} %pad_maximum_fusion.refs_1_.refs_5_), channel_id=1, source_target_pairs={{0,4},{1,5},{2,6},{3,7},{4,0},{5,1},{6,2},{7,3},{8,12},{9,13},{10,... | collective-permute-start | bytes 196616 | tf_op jit(solution)/shard_map/ppermute | solution.py:21
  9.5 4.3 %collective-permute-start.1 = (bf16[2,2,32,256]{3,2,1,0:T(8,128)(2,1)S(1)}, bf16[2,2,32,256]{3,2,1,0:T(8,128)(2,1)S(1)}, u32[]{:S(2)}, u32[]{:S(2)}) collective-permute-start(bf16[2,2,32,256]{3,2,1,0:T(8,128)(2,1)S(1)} %pad_maximum_fusion.refs_1_.refs_5_), channel_id=1, source_target_pairs={{0,2},{1,3},{2,0},{3,1},{4,6},{5,7},{6,4},{7,5},{8,10},{9,11},{10,... | collective-permute-start | bytes 196616 | tf_op jit(solution)/shard_map/ppermute | solution.py:21
  11.0 5.2 %collective-permute-start.3 = (bf16[2,2,32,256]{3,2,1,0:T(8,128)(2,1)S(1)}, bf16[2,2,32,256]{3,2,1,0:T(8,128)(2,1)S(1)}, u32[]{:S(2)}, u32[]{:S(2)}) collective-permute-start(bf16[2,2,32,256]{3,2,1,0:T(8,128)(2,1)S(1)} %pad_maximum_fusion.refs_1_.refs_5_), channel_id=1, source_target_pairs={{0,6},{1,7},{2,4},{3,5},{4,2},{5,3},{6,0},{7,1},{8,14},{9,15},{10,... | collective-permute-start | bytes 196616 | tf_op jit(solution)/shard_map/ppermute | solution.py:21
  12.4 5.4 %collective-permute-start.8 = (bf16[2,2,32,256]{3,2,1,0:T(8,128)(2,1)S(1)}, bf16[2,2,32,256]{3,2,1,0:T(8,128)(2,1)S(1)}, u32[]{:S(2)}, u32[]{:S(2)}) collective-permute-start(bf16[2,2,32,256]{3,2,1,0:T(8,128)(2,1)S(1)} %collective-permute-done.2.refs_3_.refs_7_), channel_id=1, source_target_pairs={{0,1},{1,0},{2,3},{3,2},{4,5},{5,4},{6,7},{7,6},{8,9},{9,8},{10,11... | collective-permute-start | bytes 196616 | tf_op jit(solution)/shard_map/ppermute | solution.py:21
  13.7 4.0 %collective-permute-start.7 = (bf16[2,2,32,256]{3,2,1,0:T(8,128)(2,1)S(1)}, bf16[2,2,32,256]{3,2,1,0:T(8,128)(2,1)S(1)}, u32[]{:S(2)}, u32[]{:S(2)}) collective-permute-start(bf16[2,2,32,256]{3,2,1,0:T(8,128)(2,1)S(1)} %collective-permute-done.1.refs_1_.refs_6_.refs_2_), channel_id=1, source_target_pairs={{0,1},{1,0},{2,3},{3,2},{4,5},{5,4},{6,7},{7,6},{8,9},{9,8},{10,11... | collective-permute-start | bytes 196616 | tf_op jit(solution)/shard_map/ppermute | solution.py:21
  16.1 2.4 %collective-permute-start.9 = (bf16[2,2,32,256]{3,2,1,0:T(8,128)(2,1)S(1)}, bf16[2,2,32,256]{3,2,1,0:T(8,128)(2,1)S(1)}, u32[]{:S(2)}, u32[]{:S(2)}) collective-permute-start(bf16[2,2,32,256]{3,2,1,0:T(8,128)(2,1)S(1)} %collective-permute-done.3.refs_1_.refs_8_.refs_4_), channel_id=1, source_target_pairs={{0,1},{1,0},{2,3},{3,2},{4,5},{5,4},{6,7},{7,6},{8,9},{9,8},{10,11... | collective-permute-start | bytes 196616 | tf_op jit(solution)/shard_map/ppermute | solution.py:21
  20.2 2.9 %collective-permute-start.10 = (f32[4,2,32,256]{3,2,1,0:T(8,128)S(1)}, f32[4,2,32,256]{3,2,1,0:T(8,128)S(1)}, u32[]{:S(2)}, u32[]{:S(2)}) collective-permute-start(f32[4,2,32,256]{3,2,1,0:T(8,128)S(1)} %get-tuple-element.35), channel_id=1, source_target_pairs={{0,1},{1,0},{2,3},{3,2},{4,5},{5,4},{6,7},{7,6},{8,9},{9,8},{10,11... | collective-permute-start | bytes 786440 | tf_op jit(solution)/shard_map/ppermute | solution.py:21
  21.5 10.6 %collective-permute-start.15 = (s16[1,528,256]{2,1,0:T(8,128)(2,1)S(1)}, s16[1,528,256]{2,1,0:T(8,128)(2,1)S(1)}, u32[]{:S(2)}, u32[]{:S(2)}) collective-permute-start(s16[1,528,256]{2,1,0:T(8,128)(2,1)S(1)} %shard_map.79), channel_id=1, source_target_pairs={{0,16},{16,0},{1,17},{17,1},{2,18},{18,2},{3,19},{19,3},{4,20},{20... | collective-permute-start | bytes 811016 | tf_op jit(solution)/shard_map/ppermute | solution.py:21
  23.2 4.4 %collective-permute-start.11 = (s16[1,144,256]{2,1,0:T(8,128)(2,1)S(1)}, s16[1,144,256]{2,1,0:T(8,128)(2,1)S(1)}, u32[]{:S(2)}, u32[]{:S(2)}) collective-permute-start(s16[1,144,256]{2,1,0:T(8,128)(2,1)S(1)} %get-tuple-element.37), channel_id=1, source_target_pairs={{0,2},{1,3},{2,0},{3,1},{4,6},{5,7},{6,4},{7,5},{8,10},{9,11},{10,... | collective-permute-start | bytes 221192 | tf_op jit(solution)/shard_map/ppermute | solution.py:21
  27.7 5.3 %collective-permute-start.12 = (s16[1,48,256]{2,1,0:T(8,128)(2,1)S(1)}, s16[1,48,256]{2,1,0:T(8,128)(2,1)S(1)}, u32[]{:S(2)}, u32[]{:S(2)}) collective-permute-start(s16[1,48,256]{2,1,0:T(8,128)(2,1)S(1)} %get-tuple-element.39), channel_id=1, source_target_pairs={{0,8},{1,9},{2,10},{3,11},{4,12},{5,13},{6,14},{7,15},{8,0},{9,1},... | collective-permute-start | bytes 73736 | tf_op jit(solution)/shard_map/ppermute | solution.py:21
  30.5 3.8 %collective-permute-start.13 = (s16[1,48,256]{2,1,0:T(8,128)(2,1)S(1)}, s16[1,48,256]{2,1,0:T(8,128)(2,1)S(1)}, u32[]{:S(2)}, u32[]{:S(2)}) collective-permute-start(s16[1,48,256]{2,1,0:T(8,128)(2,1)S(1)} %get-tuple-element.40), channel_id=1, source_target_pairs={{0,4},{1,5},{2,6},{3,7},{4,0},{5,1},{6,2},{7,3},{8,12},{9,13},{10,... | collective-permute-start | bytes 73736 | tf_op jit(solution)/shard_map/ppermute | solution.py:21
  30.8 5.6 %collective-permute-start.14 = (s16[1,48,256]{2,1,0:T(8,128)(2,1)S(1)}, s16[1,48,256]{2,1,0:T(8,128)(2,1)S(1)}, u32[]{:S(2)}, u32[]{:S(2)}) collective-permute-start(s16[1,48,256]{2,1,0:T(8,128)(2,1)S(1)} %get-tuple-element.41), channel_id=1, source_target_pairs={{0,12},{1,13},{2,14},{3,15},{4,8},{5,9},{6,10},{7,11},{8,4},{9,5},... | collective-permute-start | bytes 73736 | tf_op jit(solution)/shard_map/ppermute | solution.py:21

commit v9 on v8

--- a/solution.py
+++ b/solution.py
@@ -115,7 +115,7 @@
             user_out[b, k] = r
 
 
-def prepare_kernel(*refs, n_users, cols, scale):
+def prepare_kernel(*refs, n_users, lanes, cols, scale):
     seen_ref = refs[0]
     users = refs[1 : 1 + n_users]
     fac_i, weight, part, u_all = refs[1 + n_users :]
@@ -137,7 +137,7 @@
             s = dot(v, fac, NT)
             part[t, items, :] = dot(v, tan, NT)
             at_col = cols[0] * cols[1] + ib * (sub // block)
-            seen = spread_seen(seen_ref, at_col, sub // block, block, t * tile % seen_ref.shape[1], tile)
+            seen = spread_seen(seen_ref, at_col, sub // block, block, lanes + t * tile % (seen_ref.shape[1] - lanes), tile)
             e = jnp.exp(jnp.abs(s) * -scale)
             p = 1.0 / (1.0 + e)
             weight[t, items, :] = e * p * p * seen
@@ -264,12 +264,13 @@
     )(*[pltpu.with_memory_space_constraint(x, pltpu.HBM) for x in (a, b)])
 
 
-GROUPS = 16
+GROUPS = 8
+STEP = 16
 
 
 def encode_rows(x, out_ref, k):
     rows = x.shape[0]
-    groups = min(GROUPS, rows // GROUPS)
+    groups = min(GROUPS, rows // STEP)
     step = rows // groups
     exps = []
     for g in range(groups):
@@ -307,7 +308,7 @@
 
 def decode_kernel(x_ref, q_ref, out_ref, buf, sems, *, at):
     n, rows, _ = x_ref.shape
-    groups = min(GROUPS, rows // GROUPS)
+    groups = min(GROUPS, rows // STEP)
     step = rows // groups
     parts = sems.shape[1]
     copies = []
@@ -337,37 +338,33 @@
 
 def decoded(q_ref, k):
     rows = q_ref.shape[1] - GROUPS
-    groups = min(GROUPS, rows // GROUPS)
+    groups = min(GROUPS, rows // STEP)
     return jnp.concatenate([decode_rows(q_ref, k, g, groups) for g in range(groups)], 0)
 
 
-def fold_kernel(mine, core_in, keep, coded):
-    n, n_a, us, width = mine.shape
-    rows = n_a * us
-    both = [(mine[i] + core_in[i]).reshape(rows, width) for i in range(n)]
-    for i in range(0, n, 2):
-        keep[i // 2] = both[i]
-    encode_rows(jnp.concatenate(both[1::2], 0), coded, 0)
+def fold_kernel(mine, core_in, coded):
+    n, n_a, us, width = core_in.shape
+    encode_rows((mine[:n] + core_in[...]).reshape(n * n_a * us, width), coded, 0)
 
 
 def fold(mine, core_in):
-    n, n_a, us, width = mine.shape
-    rows = n_a * us
+    n, n_a, us, width = core_in.shape
     return pl.pallas_call(
         fold_kernel,
         in_specs=[VM, VM],
-        out_specs=[VM] * 2,
-        out_shape=[pltpu.VMEM((n // 2, rows, width), f32), pltpu.VMEM((1, n // 2 * rows + GROUPS, width), jnp.int16)],
+        out_specs=VM,
+        out_shape=pltpu.VMEM((1, n * n_a * us + GROUPS, width), jnp.int16),
         compiler_params=PARAMS,
     )(in_vmem(mine), in_vmem(core_in))
 
 
-def spread_kernel(keep, q, own, *coded):
-    n, rows, _ = keep.shape
+def spread_kernel(mine, core_in, q, own, *coded):
+    n, n_a, us, width = core_in.shape
+    rows = n_a * us
     half = rows // 2
     came = decoded(q, 0)
     for i in range(n):
-        x = keep[i] + came[i * rows : (i + 1) * rows]
+        x = (mine[n + i] + core_in[i]).reshape(rows, width) + came[i * rows : (i + 1) * rows]
         for j in range(2):
             part = x[j * half : (j + 1) * half]
             if i == 0 and j == 0:
@@ -376,16 +373,16 @@
                 encode_rows(part, coded[2 * i + j - 1], 0)
 
 
-def spread(keep, q):
-    _, rows, width = keep.shape
-    half = rows // 2
+def spread(mine, core_in, q):
+    _, n_a, us, width = core_in.shape
+    half = n_a * us // 2
     return pl.pallas_call(
         spread_kernel,
-        in_specs=[VM] * 2,
+        in_specs=[VM] * 3,
         out_specs=[VM] * 4,
         out_shape=[pltpu.VMEM((half, width), f32)] + [pltpu.VMEM((1, half + GROUPS, width), jnp.int16)] * 3,
         compiler_params=PARAMS,
-    )(in_vmem(keep), in_vmem(q))
+    )(in_vmem(mine), in_vmem(core_in), in_vmem(q))
 
 
 def total_kernel(own, *refs):
@@ -428,7 +425,7 @@
         held_t = tans[0] if n == 0 else jnp.concatenate(tans, 0)
         facs.append(swap(held_f, "au", n_au, bit))
         tans.append(swap(held_t, "au", n_au, bit))
-    rows = [(b ^ r) // members for b in near for r in rel_a]
+    rows = [(b ^ r) // members for b in [*near, near[1], near[3], near[0], near[2]] for r in rel_a]
     facs[0], tans[0], seen = load(
         block_mask, facs[0], tans[0], rows_of=(members, rows), cols_of=(per, rel_items), us=us, scale=scale
     )
@@ -449,20 +446,24 @@
     sums = [first, second, third]
     at_mine, at_other = [(0, 0), (1, 0), (1, 2), (2, 0)], [(0, 1), (1, 1), (1, 3), (2, 1)]
     item_sums = [own_items]
+    turn = [1, 3, 0, 2]
+    mine, other = [mine[i] for i in turn], [other[i] for i in turn]
+    at_mine, at_other = [at_mine[i] for i in turn], [at_other[i] for i in turn]
     for g in range(1, len(facs)):
         first, second = {}, {}
         if facs[g].shape[0] == 1:
-            ready = prepare(seen, [*other, *mine], facs[g], cols=(g, per), scale=scale)
+            ready = prepare(seen, [*other, *mine], facs[g], lanes=4 * piece, cols=(g, per), scale=scale)
             first = {"ready": ready, "prepared": 0}
             second = {"ready": ready, "prepared": ready[0].shape[0] // 2}
-        out_other, item_sum = call(other, g, sums, at_other, None, **first)
-        out_mine, item_sum = call(mine, g, sums, at_mine, item_sum, **second)
+        out_other, item_sum = call(other, g, sums, at_other, None, lanes=4 * piece, **first)
+        out_mine, item_sum = call(mine, g, sums, at_mine, item_sum, lanes=4 * piece, **second)
         item_sums.append(item_sum)
         sums = [out_mine, out_other]
         at_mine, at_other = [(0, i) for i in range(4)], [(1, i) for i in range(4)]
 
-    keep, odd = fold(out_mine, swap(out_other, "ia", n_ia, core))
-    own, *coded = spread(keep, swap(odd, "ia", n_ia, near[1]))
+    come = [swap(out_other[2 * i : 2 * i + 2], "ia", n_ia, core) for i in range(2)]
+    odd = fold(out_mine, come[0])
+    own, *coded = spread(out_mine, come[1], swap(odd, "ia", n_ia, near[1]))
     far_bit = a_bits[-1]
     coded = [swap(q, "ia", n_ia, b) for q, b in zip(coded, [far_bit, near[2], far_bit ^ near[2]])]
     acc = total(own, coded)

time: 37.4 us -> 39 us (1.043)
  waiting for transfers between devices: 12.1 us -> 13.2 us
  starting transfers between devices: 17.1 us -> 17.6 us
    ppermute x16 -> x17, waiting for transfers between devices: 12.1 us -> 13.2 us  [swap(): return lax.ppermute(x, axis, [(i, i ^ bits) for i in range(size)])]
    ppermute x16 -> x17, starting transfers between devices: 17.1 us -> 17.6 us  [swap(): return lax.ppermute(x, axis, [(i, i ^ bits) for i in range(size)])]
  transfers between devices with their start and end apart: 16 -> 17, of which waited for: 7 -> 9; matrix products, arithmetic and copies ran while one was open for 0% -> 0% of each run, Pallas kernels for 14% -> 11%
where the time goes in v9:
time: 39 us; the launch traced here: 38.6 us
  starting transfers between devices  17.6 us (45%)
  waiting for transfers between devices  13.2 us (34%)
  Pallas kernels  7.01 us (18%)
  between operations  0.76 us (2%)
    ppermute x17, starting transfers between devices, swap(): return lax.ppermute(x, axis, [(i, i ^ bits) for i in range(size)])  17.6 us
    ppermute x17, waiting for transfers between devices, swap(): return lax.ppermute(x, axis, [(i, i ^ bits) for i in range(size)])  13.2 us
    pallas_call x5, Pallas kernels, region(): pl.pallas_call(functools.partial(region_kernel, n_users=len(users), sums_...  2.97 us
    pallas_call x1, Pallas kernels, load(): pl.pallas_call(functools.partial(load_kernel, **static), in_specs=[VM] +...  1.05 us
    pallas_call x1, Pallas kernels, add_decoded(): pl.pallas_call(functools.partial(decode_kernel, at=at), in_specs=[VM, VM]...  0.84 us
  transfers between devices with their start and end apart: 17, of which 9 were waited for; matrix products, arithmetic and copies ran while one was open for 0% of the time, Pallas kernels for 11%

profile of v9, /device:TPU:0, one launch (start us, length us, event | category | flops | bytes accessed | tf_op | source)
XLA Modules:
  0.0 38.6 jit_solution(1948485170026255969)
XLA Ops:
  0.6 0.8 %shard_map.69 = bf16[1,2,32,256]{3,2,1,0:T(8,128)(2,1)S(1)} custom-call(bf16[32,256]{1,0:T(8,128)(2,1)} %a.1, bf16[32,256]{1,0:T(8,128)(2,1)} %b.1), custom_call_target="tpu_custom_call" | custom-call | tf_op jit(solution)/shard_map/pallas_call | solution.py:257
  1.4 4.1 %collective-permute-start = (bf16[1,2,32,256]{3,2,1,0:T(8,128)(2,1)S(1)}, bf16[1,2,32,256]{3,2,1,0:T(8,128)(2,1)S(1)}, u32[]{:S(2)}, u32[]{:S(2)}) collective-permute-start(bf16[1,2,32,256]{3,2,1,0:T(8,128)(2,1)S(1)} %shard_map.69), channel_id=1, source_target_pairs={{0,8},{1,9},{2,10},{3,11},{4,12},{5,13},{6,14},{7,15},{8,0},{9,1},... | collective-permute-start | bytes 98312 | tf_op jit(solution)/shard_map/ppermute | solution.py:21
  5.5 1.5 %collective-permute-start.4 = (bf16[1,512,256]{2,1,0:T(8,128)(2,1)}, bf16[1,512,256]{2,1,0:T(8,128)(2,1)S(1)}, u32[]{:S(2)}, u32[]{:S(2)}) collective-permute-start(bf16[1,512,256]{2,1,0:T(8,128)(2,1)} %bitcast.4), channel_id=1, source_target_pairs={{0,16},{16,0},{1,17},{17,1},{2,18},{18,2},{3,19},{19,3},{4,20},{20... | collective-permute-start | bytes 786440 | tf_op jit(solution)/shard_map/ppermute | solution.py:21
  7.0 0.0 copy-start
  7.0 0.5 %collective-permute-start.5 = (bf16[1,512,256]{2,1,0:T(8,128)(2,1)}, bf16[1,512,256]{2,1,0:T(8,128)(2,1)S(1)}, u32[]{:S(2)}, u32[]{:S(2)}) collective-permute-start(bf16[1,512,256]{2,1,0:T(8,128)(2,1)} %bitcast.6), channel_id=1, source_target_pairs={{0,16},{16,0},{1,17},{17,1},{2,18},{18,2},{3,19},{19,3},{4,20},{20... | collective-permute-start | bytes 786440 | tf_op jit(solution)/shard_map/ppermute | solution.py:21
  7.5 0.2 collective-permute-done
  7.8 0.1 collective-permute-start.6
  7.9 1.6 %collective-permute-start.3 = (bf16[2,2,32,256]{3,2,1,0:T(8,128)(2,1)S(1)}, bf16[2,2,32,256]{3,2,1,0:T(8,128)(2,1)S(1)}, u32[]{:S(2)}, u32[]{:S(2)}) collective-permute-start(bf16[2,2,32,256]{3,2,1,0:T(8,128)(2,1)S(1)} %pad_maximum_fusion.refs_1_.refs_7_.refs_3_), channel_id=1, source_target_pairs={{0,4},{1,5},{2,6},{3,7},{4,0},{5,1},{6,2},{7,3},{8,12},{9,13},{10,... | collective-permute-start | bytes 196616 | tf_op jit(solution)/shard_map/ppermute | solution.py:21
  9.5 1.5 %collective-permute-start.1 = (bf16[2,2,32,256]{3,2,1,0:T(8,128)(2,1)S(1)}, bf16[2,2,32,256]{3,2,1,0:T(8,128)(2,1)S(1)}, u32[]{:S(2)}, u32[]{:S(2)}) collective-permute-start(bf16[2,2,32,256]{3,2,1,0:T(8,128)(2,1)S(1)} %pad_maximum_fusion.refs_1_.refs_7_.refs_3_), channel_id=1, source_target_pairs={{0,2},{1,3},{2,0},{3,1},{4,6},{5,7},{6,4},{7,5},{8,10},{9,11},{10,... | collective-permute-start | bytes 196616 | tf_op jit(solution)/shard_map/ppermute | solution.py:21
  11.0 0.0 collective-permute-done.6.refs_2_.refs_3_
  11.0 0.6 %collective-permute-start.2 = (bf16[2,2,32,256]{3,2,1,0:T(8,128)(2,1)S(1)}, bf16[2,2,32,256]{3,2,1,0:T(8,128)(2,1)S(1)}, u32[]{:S(2)}, u32[]{:S(2)}) collective-permute-start(bf16[2,2,32,256]{3,2,1,0:T(8,128)(2,1)S(1)} %pad_maximum_fusion.refs_1_.refs_7_.refs_3_), channel_id=1, source_target_pairs={{0,6},{1,7},{2,4},{3,5},{4,2},{5,3},{6,0},{7,1},{8,14},{9,15},{10,... | collective-permute-start | bytes 196616 | tf_op jit(solution)/shard_map/ppermute | solution.py:21
  11.6 0.8 %collective-permute-done.3.refs_3_.refs_8_.refs_4_ = bf16[2,2,32,256]{3,2,1,0:T(8,128)(2,1)S(1)} collective-permute-done((bf16[2,2,32,256]{3,2,1,0:T(8,128)(2,1)S(1)}, bf16[2,2,32,256]{3,2,1,0:T(8,128)(2,1)S(1)}, u32[]{:S(2)}, u32[]{:S(2)}) %collective-permute-start.3) | collective-permute-done | bytes 65568 | tf_op jit(solution)/shard_map/ppermute | solution.py:21
  12.4 0.0 collective-permute-start.8
  12.4 1.4 %collective-permute-done.1.refs_1_.refs_5_ = bf16[2,2,32,256]{3,2,1,0:T(8,128)(2,1)S(1)} collective-permute-done((bf16[2,2,32,256]{3,2,1,0:T(8,128)(2,1)S(1)}, bf16[2,2,32,256]{3,2,1,0:T(8,128)(2,1)S(1)}, u32[]{:S(2)}, u32[]{:S(2)}) %collective-permute-start.1) | collective-permute-done | bytes 65568 | tf_op jit(solution)/shard_map/ppermute | solution.py:21
  13.7 0.0 collective-permute-start.7
  13.7 2.4 %collective-permute-done.2.refs_1_.refs_6_.refs_2_ = bf16[2,2,32,256]{3,2,1,0:T(8,128)(2,1)S(1)} collective-permute-done((bf16[2,2,32,256]{3,2,1,0:T(8,128)(2,1)S(1)}, bf16[2,2,32,256]{3,2,1,0:T(8,128)(2,1)S(1)}, u32[]{:S(2)}, u32[]{:S(2)}) %collective-permute-start.2) | collective-permute-done | bytes 65568 | tf_op jit(solution)/shard_map/ppermute | solution.py:21
  16.1 0.0 collective-permute-start.9
  16.1 0.0 copy-done
  16.1 1.0 %shard_map.68 = (bf16[1,512,256]{2,1,0:T(8,128)(2,1)S(1)}, bf16[1,512,256]{2,1,0:T(8,128)(2,1)S(1)}, f32[8,512]{1,0:T(8,128)S(1)}) custom-call(s32[4,8]{1,0:T(4,128)S(1)} %copy-done, bf16[1,512,256]{2,1,0:T(8,128)(2,1)} %bitcast.5, bf16[1,512,256]{2,1,0:T(8,128)(2,1)} %bitcast.7), custom_call_target="tpu_custom_call" | custom-call | tf_op jit(solution)/shard_map/pallas_call | solution.py:235
  17.2 0.6 %shard_map.70 = (f32[2,2,32,256]{3,2,1,0:T(8,128)S(1)}, f32[1,512,256]{2,1,0:T(8,128)S(1)}) custom-call(f32[8,512]{1,0:T(8,128)S(1)} %get-tuple-element.21.refs_0_, bf16[2,2,32,256]{3,2,1,0:T(8,128)(2,1)S(1)} %pad_maximum_fusion.refs_1_.refs_7_.refs_3_, bf16[2,2,32,256]{3,2,1,0:T(8,128)(2,1)S(1)} %collective-permute-done.6.refs_2_.refs_3_, ...), custom_call_target="tpu_custom_call" | custom-call | tf_op jit(solution)/shard_map/pallas_call | solution.py:164
  17.8 0.0 collective-permute-done.8.refs_4_
  17.8 0.0 collective-permute-done.7.refs_2_.refs_1_
  17.8 0.7 %shard_map.71 = (f32[4,2,32,256]{3,2,1,0:T(8,128)S(1)}, f32[1,512,256]{2,1,0:T(8,128)S(1)}) custom-call(f32[8,512]{1,0:T(8,128)S(1)} %get-tuple-element.21.refs_0_, bf16[2,2,32,256]{3,2,1,0:T(8,128)(2,1)S(1)} %collective-permute-done.1.refs_1_.refs_5_, ...), custom_call_target="tpu_custom_call", output_to_operand_aliasing={{1}: (7, {})} | custom-call | tf_op jit(solution)/shard_map/pallas_call | solution.py:164
  18.5 0.0 collective-permute-done.9.refs_2_
  18.5 0.6 %shard_map.72 = (f32[2,2,32,256]{3,2,1,0:T(8,128)S(1)}, f32[1,512,256]{2,1,0:T(8,128)S(1)}) custom-call(f32[8,512]{1,0:T(8,128)S(1)} %get-tuple-element.21.refs_0_, bf16[2,2,32,256]{3,2,1,0:T(8,128)(2,1)S(1)} %collective-permute-done.2.refs_1_.refs_6_.refs_2_, ...), custom_call_target="tpu_custom_call", output_to_operand_aliasing={{1}: (5, {})} | custom-call | tf_op jit(solution)/shard_map/pallas_call | solution.py:164
  19.1 0.0 collective-permute-done.4.refs_9_.refs_5_
  19.1 0.5 %shard_map.73 = (f32[2,512,256]{2,1,0:T(8,128)S(1)}, f32[2,512,256]{2,1,0:T(8,128)S(1)}) custom-call(f32[8,512]{1,0:T(8,128)S(1)} %get-tuple-element.21.refs_0_, bf16[2,2,32,256]{3,2,1,0:T(8,128)(2,1)S(1)} %collective-permute-done.7.refs_2_.refs_1_, bf16[2,2,32,256]{3,2,1,0:T(8,128)(2,1)S(1)} %collective-permute-done.9.refs_2_, ...), custom_call_target="tpu_custom_call" | custom-call | tf_op jit(solution)/shard_map/pallas_call | solution.py:194
  19.6 0.0 collective-permute-done.5.refs_6_
  19.6 0.6 %shard_map.74 = (f32[4,2,32,256]{3,2,1,0:T(8,128)S(1)}, f32[1,512,256]{2,1,0:T(8,128)S(1)}) custom-call(f32[8,512]{1,0:T(8,128)S(1)} %get-tuple-element.21.refs_0_, bf16[2,2,32,256]{3,2,1,0:T(8,128)(2,1)S(1)} %collective-permute-done.7.refs_2_.refs_1_, bf16[2,2,32,256]{3,2,1,0:T(8,128)(2,1)S(1)} %collective-permute-done.9.refs_2_, ...), custom_call_target="tpu_custom_call" | custom-call | tf_op jit(solution)/shard_map/pallas_call | solution.py:164
  20.2 0.6 %shard_map.75 = (f32[4,2,32,256]{3,2,1,0:T(8,128)S(1)}, f32[1,512,256]{2,1,0:T(8,128)S(1)}) custom-call(f32[8,512]{1,0:T(8,128)S(1)} %get-tuple-element.21.refs_0_, bf16[2,2,32,256]{3,2,1,0:T(8,128)(2,1)S(1)} %collective-permute-done.1.refs_1_.refs_5_, ...), custom_call_target="tpu_custom_call", output_to_operand_aliasing={{1}: (10, {})} | custom-call | tf_op jit(solution)/shard_map/pallas_call | solution.py:164
  20.8 0.1 shard_map.79
  20.9 1.6 %collective-permute-start.16 = (s16[1,520,256]{2,1,0:T(8,128)(2,1)S(1)}, s16[1,520,256]{2,1,0:T(8,128)(2,1)S(1)}, u32[]{:S(2)}, u32[]{:S(2)}) collective-permute-start(s16[1,520,256]{2,1,0:T(8,128)(2,1)S(1)} %shard_map.79), channel_id=1, source_target_pairs={{0,16},{16,0},{1,17},{17,1},{2,18},{18,2},{3,19},{19,3},{4,20},{20... | collective-permute-start | bytes 798728 | tf_op jit(solution)/shard_map/ppermute | solution.py:21
  22.5 0.3 collective-permute-start.11
  22.8 0.3 collective-permute-start.10
  23.1 0.8 %collective-permute-done.11.core_in = f32[2,2,32,256]{3,2,1,0:T(8,128)S(1)} collective-permute-done((f32[2,2,32,256]{3,2,1,0:T(8,128)S(1)}, f32[2,2,32,256]{3,2,1,0:T(8,128)S(1)}, u32[]{:S(2)}, u32[]{:S(2)}) %collective-permute-start.11) | collective-permute-done | bytes 131104 | tf_op jit(solution)/shard_map/ppermute | solution.py:21
  23.9 0.1 shard_map.76
  24.0 1.0 %collective-permute-start.12 = (s16[1,136,256]{2,1,0:T(8,128)(2,1)S(1)}, s16[1,136,256]{2,1,0:T(8,128)(2,1)S(1)}, u32[]{:S(2)}, u32[]{:S(2)}) collective-permute-start(s16[1,136,256]{2,1,0:T(8,128)(2,1)S(1)} %shard_map.76), channel_id=1, source_target_pairs={{0,2},{1,3},{2,0},{3,1},{4,6},{5,7},{6,4},{7,5},{8,10},{9,11},{10,... | collective-permute-start | bytes 208904 | tf_op jit(solution)/shard_map/ppermute | solution.py:21
  25.0 0.0 collective-permute-done.10.core_in
  25.0 3.3 %collective-permute-done.12.q = s16[1,136,256]{2,1,0:T(8,128)(2,1)S(1)} collective-permute-done((s16[1,136,256]{2,1,0:T(8,128)(2,1)S(1)}, s16[1,136,256]{2,1,0:T(8,128)(2,1)S(1)}, u32[]{:S(2)}, u32[]{:S(2)}) %collective-permute-start.12) | collective-permute-done | bytes 69664 | tf_op jit(solution)/shard_map/ppermute | solution.py:21
  28.4 0.1 shard_map.77
  28.4 2.9 %collective-permute-start.13 = (s16[1,40,256]{2,1,0:T(8,128)(2,1)S(1)}, s16[1,40,256]{2,1,0:T(8,128)(2,1)S(1)}, u32[]{:S(2)}, u32[]{:S(2)}) collective-permute-start(s16[1,40,256]{2,1,0:T(8,128)(2,1)S(1)} %get-tuple-element.35), channel_id=1, source_target_pairs={{0,8},{1,9},{2,10},{3,11},{4,12},{5,13},{6,14},{7,15},{8,0},{9,1},... | collective-permute-start | bytes 61448 | tf_op jit(solution)/shard_map/ppermute | solution.py:21
  31.3 0.2 collective-permute-start.14
  31.6 1.3 %collective-permute-start.15 = (s16[1,40,256]{2,1,0:T(8,128)(2,1)S(1)}, s16[1,40,256]{2,1,0:T(8,128)(2,1)S(1)}, u32[]{:S(2)}, u32[]{:S(2)}) collective-permute-start(s16[1,40,256]{2,1,0:T(8,128)(2,1)S(1)} %get-tuple-element.37), channel_id=1, source_target_pairs={{0,12},{1,13},{2,14},{3,15},{4,8},{5,9},{6,10},{7,11},{8,4},{9,5},... | collective-permute-start | bytes 61448 | tf_op jit(solution)/shard_map/ppermute | solution.py:21
  32.9 0.3 collective-permute-done.13.refs_0_
  33.2 2.1 %collective-permute-done.14.refs_1_ = s16[1,40,256]{2,1,0:T(8,128)(2,1)S(1)} collective-permute-done((s16[1,40,256]{2,1,0:T(8,128)(2,1)S(1)}, s16[1,40,256]{2,1,0:T(8,128)(2,1)S(1)}, u32[]{:S(2)}, u32[]{:S(2)}) %collective-permute-start.14) | collective-permute-done | bytes 20512 | tf_op jit(solution)/shard_map/ppermute | solution.py:21
  35.3 1.9 %collective-permute-done.15.refs_2_ = s16[1,40,256]{2,1,0:T(8,128)(2,1)S(1)} collective-permute-done((s16[1,40,256]{2,1,0:T(8,128)(2,1)S(1)}, s16[1,40,256]{2,1,0:T(8,128)(2,1)S(1)}, u32[]{:S(2)}, u32[]{:S(2)}) %collective-permute-start.15) | collective-permute-done | bytes 20512 | tf_op jit(solution)/shard_map/ppermute | solution.py:21
  37.1 0.6 %shard_map.78 = f32[32,256]{1,0:T(8,128)} custom-call(f32[32,256]{1,0:T(8,128)S(1)} %get-tuple-element.34.own, s16[1,40,256]{2,1,0:T(8,128)(2,1)S(1)} %collective-permute-done.13.refs_0_, s16[1,40,256]{2,1,0:T(8,128)(2,1)S(1)} %collective-permute-done.14.refs_1_, s16[1,40,256]{2,1,0:T(8,128)(2,1)S(1)} %collective-permute-done.15.refs_2_), custom_call_target="tpu_custom_call" | custom-call | tf_op jit(solution)/shard_map/pallas_call | solution.py:396
  37.8 0.0 collective-permute-done.16.q_ref
  37.8 0.8 %shard_map.80 = f32[1,512,256]{2,1,0:T(8,128)} custom-call(f32[1,512,256]{2,1,0:T(8,128)S(1)} %get-tuple-element.38.x_ref, s16[1,520,256]{2,1,0:T(8,128)(2,1)S(1)} %collective-permute-done.16.q_ref), custom_call_target="tpu_custom_call" | custom-call | tf_op jit(solution)/shard_map/pallas_call | solution.py:329
  (2 shorter events, 0.0 us)
Async XLA Ops:
  1.4 6.4 %collective-permute-start = (bf16[1,2,32,256]{3,2,1,0:T(8,128)(2,1)S(1)}, bf16[1,2,32,256]{3,2,1,0:T(8,128)(2,1)S(1)}, u32[]{:S(2)}, u32[]{:S(2)}) collective-permute-start(bf16[1,2,32,256]{3,2,1,0:T(8,128)(2,1)S(1)} %shard_map.69), channel_id=1, source_target_pairs={{0,8},{1,9},{2,10},{3,11},{4,12},{5,13},{6,14},{7,15},{8,0},{9,1},... | collective-permute-start | bytes 98312 | tf_op jit(solution)/shard_map/ppermute | solution.py:21
  5.5 13.6 %collective-permute-start.4 = (bf16[1,512,256]{2,1,0:T(8,128)(2,1)}, bf16[1,512,256]{2,1,0:T(8,128)(2,1)S(1)}, u32[]{:S(2)}, u32[]{:S(2)}) collective-permute-start(bf16[1,512,256]{2,1,0:T(8,128)(2,1)} %bitcast.4), channel_id=1, source_target_pairs={{0,16},{16,0},{1,17},{17,1},{2,18},{18,2},{3,19},{19,3},{4,20},{20... | collective-permute-start | bytes 786440 | tf_op jit(solution)/shard_map/ppermute | solution.py:21
  7.0 9.1 %copy-start = (s32[4,8]{1,0:T(4,128)S(1)}, s32[4,8]{1,0:T(4,128)}, u32[]{:S(2)}) copy-start(s32[4,8]{1,0:T(4,128)} %mask.1) | copy-start | bytes 388
  7.0 12.6 %collective-permute-start.5 = (bf16[1,512,256]{2,1,0:T(8,128)(2,1)}, bf16[1,512,256]{2,1,0:T(8,128)(2,1)S(1)}, u32[]{:S(2)}, u32[]{:S(2)}) collective-permute-start(bf16[1,512,256]{2,1,0:T(8,128)(2,1)} %bitcast.6), channel_id=1, source_target_pairs={{0,16},{16,0},{1,17},{17,1},{2,18},{18,2},{3,19},{19,3},{4,20},{20... | collective-permute-start | bytes 786440 | tf_op jit(solution)/shard_map/ppermute | solution.py:21
  7.8 3.2 %collective-permute-start.6 = (bf16[2,2,32,256]{3,2,1,0:T(8,128)(2,1)S(1)}, bf16[2,2,32,256]{3,2,1,0:T(8,128)(2,1)S(1)}, u32[]{:S(2)}, u32[]{:S(2)}) collective-permute-start(bf16[2,2,32,256]{3,2,1,0:T(8,128)(2,1)S(1)} %pad_maximum_fusion.refs_1_.refs_7_.refs_3_), channel_id=1, source_target_pairs={{0,1},{1,0},{2,3},{3,2},{4,5},{5,4},{6,7},{7,6},{8,9},{9,8},{10,11... | collective-permute-start | bytes 196616 | tf_op jit(solution)/shard_map/ppermute | solution.py:21
  7.9 4.5 %collective-permute-start.3 = (bf16[2,2,32,256]{3,2,1,0:T(8,128)(2,1)S(1)}, bf16[2,2,32,256]{3,2,1,0:T(8,128)(2,1)S(1)}, u32[]{:S(2)}, u32[]{:S(2)}) collective-permute-start(bf16[2,2,32,256]{3,2,1,0:T(8,128)(2,1)S(1)} %pad_maximum_fusion.refs_1_.refs_7_.refs_3_), channel_id=1, source_target_pairs={{0,4},{1,5},{2,6},{3,7},{4,0},{5,1},{6,2},{7,3},{8,12},{9,13},{10,... | collective-permute-start | bytes 196616 | tf_op jit(solution)/shard_map/ppermute | solution.py:21
  9.5 4.3 %collective-permute-start.1 = (bf16[2,2,32,256]{3,2,1,0:T(8,128)(2,1)S(1)}, bf16[2,2,32,256]{3,2,1,0:T(8,128)(2,1)S(1)}, u32[]{:S(2)}, u32[]{:S(2)}) collective-permute-start(bf16[2,2,32,256]{3,2,1,0:T(8,128)(2,1)S(1)} %pad_maximum_fusion.refs_1_.refs_7_.refs_3_), channel_id=1, source_target_pairs={{0,2},{1,3},{2,0},{3,1},{4,6},{5,7},{6,4},{7,5},{8,10},{9,11},{10,... | collective-permute-start | bytes 196616 | tf_op jit(solution)/shard_map/ppermute | solution.py:21
  11.0 5.2 %collective-permute-start.2 = (bf16[2,2,32,256]{3,2,1,0:T(8,128)(2,1)S(1)}, bf16[2,2,32,256]{3,2,1,0:T(8,128)(2,1)S(1)}, u32[]{:S(2)}, u32[]{:S(2)}) collective-permute-start(bf16[2,2,32,256]{3,2,1,0:T(8,128)(2,1)S(1)} %pad_maximum_fusion.refs_1_.refs_7_.refs_3_), channel_id=1, source_target_pairs={{0,6},{1,7},{2,4},{3,5},{4,2},{5,3},{6,0},{7,1},{8,14},{9,15},{10,... | collective-permute-start | bytes 196616 | tf_op jit(solution)/shard_map/ppermute | solution.py:21
  12.4 5.4 %collective-permute-start.8 = (bf16[2,2,32,256]{3,2,1,0:T(8,128)(2,1)S(1)}, bf16[2,2,32,256]{3,2,1,0:T(8,128)(2,1)S(1)}, u32[]{:S(2)}, u32[]{:S(2)}) collective-permute-start(bf16[2,2,32,256]{3,2,1,0:T(8,128)(2,1)S(1)} %collective-permute-done.3.refs_3_.refs_8_.refs_4_), channel_id=1, source_target_pairs={{0,1},{1,0},{2,3},{3,2},{4,5},{5,4},{6,7},{7,6},{8,9},{9,8},{10,11... | collective-permute-start | bytes 196616 | tf_op jit(solution)/shard_map/ppermute | solution.py:21
  13.7 4.0 %collective-permute-start.7 = (bf16[2,2,32,256]{3,2,1,0:T(8,128)(2,1)S(1)}, bf16[2,2,32,256]{3,2,1,0:T(8,128)(2,1)S(1)}, u32[]{:S(2)}, u32[]{:S(2)}) collective-permute-start(bf16[2,2,32,256]{3,2,1,0:T(8,128)(2,1)S(1)} %collective-permute-done.1.refs_1_.refs_5_), channel_id=1, source_target_pairs={{0,1},{1,0},{2,3},{3,2},{4,5},{5,4},{6,7},{7,6},{8,9},{9,8},{10,11... | collective-permute-start | bytes 196616 | tf_op jit(solution)/shard_map/ppermute | solution.py:21
  16.1 2.4 %collective-permute-start.9 = (bf16[2,2,32,256]{3,2,1,0:T(8,128)(2,1)S(1)}, bf16[2,2,32,256]{3,2,1,0:T(8,128)(2,1)S(1)}, u32[]{:S(2)}, u32[]{:S(2)}) collective-permute-start(bf16[2,2,32,256]{3,2,1,0:T(8,128)(2,1)S(1)} %collective-permute-done.2.refs_1_.refs_6_.refs_2_), channel_id=1, source_target_pairs={{0,1},{1,0},{2,3},{3,2},{4,5},{5,4},{6,7},{7,6},{8,9},{9,8},{10,11... | collective-permute-start | bytes 196616 | tf_op jit(solution)/shard_map/ppermute | solution.py:21
  20.9 16.9 %collective-permute-start.16 = (s16[1,520,256]{2,1,0:T(8,128)(2,1)S(1)}, s16[1,520,256]{2,1,0:T(8,128)(2,1)S(1)}, u32[]{:S(2)}, u32[]{:S(2)}) collective-permute-start(s16[1,520,256]{2,1,0:T(8,128)(2,1)S(1)} %shard_map.79), channel_id=1, source_target_pairs={{0,16},{16,0},{1,17},{17,1},{2,18},{18,2},{3,19},{19,3},{4,20},{20... | collective-permute-start | bytes 798728 | tf_op jit(solution)/shard_map/ppermute | solution.py:21
  22.5 1.4 %collective-permute-start.11 = (f32[2,2,32,256]{3,2,1,0:T(8,128)S(1)}, f32[2,2,32,256]{3,2,1,0:T(8,128)S(1)}, u32[]{:S(2)}, u32[]{:S(2)}) collective-permute-start(f32[2,2,32,256]{3,2,1,0:T(8,128)S(1)} %get-tuple-element.40), channel_id=1, source_target_pairs={{0,1},{1,0},{2,3},{3,2},{4,5},{5,4},{6,7},{7,6},{8,9},{9,8},{10,11... | collective-permute-start | bytes 393224 | tf_op jit(solution)/shard_map/ppermute | solution.py:21
  22.8 2.2 %collective-permute-start.10 = (f32[2,2,32,256]{3,2,1,0:T(8,128)S(1)}, f32[2,2,32,256]{3,2,1,0:T(8,128)S(1)}, u32[]{:S(2)}, u32[]{:S(2)}) collective-permute-start(f32[2,2,32,256]{3,2,1,0:T(8,128)S(1)} %get-tuple-element.41), channel_id=1, source_target_pairs={{0,1},{1,0},{2,3},{3,2},{4,5},{5,4},{6,7},{7,6},{8,9},{9,8},{10,11... | collective-permute-start | bytes 393224 | tf_op jit(solution)/shard_map/ppermute | solution.py:21
  24.0 4.4 %collective-permute-start.12 = (s16[1,136,256]{2,1,0:T(8,128)(2,1)S(1)}, s16[1,136,256]{2,1,0:T(8,128)(2,1)S(1)}, u32[]{:S(2)}, u32[]{:S(2)}) collective-permute-start(s16[1,136,256]{2,1,0:T(8,128)(2,1)S(1)} %shard_map.76), channel_id=1, source_target_pairs={{0,2},{1,3},{2,0},{3,1},{4,6},{5,7},{6,4},{7,5},{8,10},{9,11},{10,... | collective-permute-start | bytes 208904 | tf_op jit(solution)/shard_map/ppermute | solution.py:21
  28.4 4.8 %collective-permute-start.13 = (s16[1,40,256]{2,1,0:T(8,128)(2,1)S(1)}, s16[1,40,256]{2,1,0:T(8,128)(2,1)S(1)}, u32[]{:S(2)}, u32[]{:S(2)}) collective-permute-start(s16[1,40,256]{2,1,0:T(8,128)(2,1)S(1)} %get-tuple-element.35), channel_id=1, source_target_pairs={{0,8},{1,9},{2,10},{3,11},{4,12},{5,13},{6,14},{7,15},{8,0},{9,1},... | collective-permute-start | bytes 61448 | tf_op jit(solution)/shard_map/ppermute | solution.py:21
  31.3 3.9 %collective-permute-start.14 = (s16[1,40,256]{2,1,0:T(8,128)(2,1)S(1)}, s16[1,40,256]{2,1,0:T(8,128)(2,1)S(1)}, u32[]{:S(2)}, u32[]{:S(2)}) collective-permute-start(s16[1,40,256]{2,1,0:T(8,128)(2,1)S(1)} %get-tuple-element.36), channel_id=1, source_target_pairs={{0,4},{1,5},{2,6},{3,7},{4,0},{5,1},{6,2},{7,3},{8,12},{9,13},{10,... | collective-permute-start | bytes 61448 | tf_op jit(solution)/shard_map/ppermute | solution.py:21
  31.6 5.6 %collective-permute-start.15 = (s16[1,40,256]{2,1,0:T(8,128)(2,1)S(1)}, s16[1,40,256]{2,1,0:T(8,128)(2,1)S(1)}, u32[]{:S(2)}, u32[]{:S(2)}) collective-permute-start(s16[1,40,256]{2,1,0:T(8,128)(2,1)S(1)} %get-tuple-element.37), channel_id=1, source_target_pairs={{0,12},{1,13},{2,14},{3,15},{4,8},{5,9},{6,10},{7,11},{8,4},{9,5},... | collective-permute-start | bytes 61448 | tf_op jit(solution)/shard_map/ppermute | solution.py:21
